TPU v7x, 32 devices: a whole 2x2x4 slice. The times are simulated.
32 devices in a mesh: dp: 4 (over x, core), ctx: 8 (over z, y).
Axes of the slice: x: 2, y: 2, z: 4, core: 2. Of those that a mesh axis runs over, the one named last changes fastest.
Arguments:
- inputs: bfloat16 [8, 512, 2048], P('dp', 'ctx'), may hold values from -6 to 6
- cotangent: bfloat16 [8, 512, 2048], P('dp', 'ctx'), may hold values from -6 to 6
- lengths: int32 [8], P('dp'), may hold values from 128 to 512, as said below
- query_weight: bfloat16 [2048, 2048], P(('dp', 'ctx')), may hold values from -0.125 to 0.125
- key_weight: bfloat16 [2048, 2048], P(('dp', 'ctx')), may hold values from -0.125 to 0.125
- value_weight: bfloat16 [2048, 2048], P(('dp', 'ctx')), may hold values from -0.125 to 0.125
- mix_weight: bfloat16 [2048, 2048], P(('dp', 'ctx')), may hold values from -0.75 to 0.75
- gate_weight: bfloat16 [2048, 8192], P(('dp', 'ctx')), may hold values from -0.125 to 0.125
- up_weight: bfloat16 [2048, 8192], P(('dp', 'ctx')), may hold values from -0.125 to 0.125
- down_weight: bfloat16 [2048, 8192], P(('dp', 'ctx')), may hold values from -0.0625 to 0.0625
- attn_gain: bfloat16 [2048], P(('dp', 'ctx')), may hold values from 0.5 to 1.5
- ffn_gain: bfloat16 [2048], P(('dp', 'ctx')), may hold values from 0.5 to 1.5
Outputs:
- activations: bfloat16 [8, 512, 2048], P('dp', 'ctx')
- input_grad: bfloat16 [8, 512, 2048], P('dp', 'ctx')
- query_grad: float32 [2048, 2048], P(('dp', 'ctx'))
- key_grad: float32 [2048, 2048], P(('dp', 'ctx'))
- value_grad: float32 [2048, 2048], P(('dp', 'ctx'))
- mix_grad: float32 [2048, 2048], P(('dp', 'ctx'))
- gate_grad: float32 [2048, 8192], P(('dp', 'ctx'))
- up_grad: float32 [2048, 8192], P(('dp', 'ctx'))
- down_grad: float32 [2048, 8192], P(('dp', 'ctx'))
- attn_gain_grad: float32 [2048], P(('dp', 'ctx'))
- ffn_gain_grad: float32 [2048], P(('dp', 'ctx'))
Inputs may be any that keep to these rules, and one draw needn't show every extreme that they name: `lengths`: each sequence has 128 to 512 valid slots at its start; the first sequence is full.
All inputs are finite; a program needn't handle non-finite values.
Results may differ from a plain program's by a relative error of at most 0.03.
Values may be sent and summed in bfloat16 or wider, within the bound.
No kernel may reach another device: no remote copies, remote signals or barrier semaphores. Data moves between devices by JAX's collectives and lax.ppermute only.
A program may use at most 576 MiB of HBM per device.

v0:
```python
import jax
import jax.numpy as jnp
from jax import lax
from jax.sharding import PartitionSpec as P

HEADS = 32
MB = 2


EPSILON = 1e-05
THETA = 130000.0
NEGATIVE = -1e30
SUB_BLOCK = 512


def rotation(positions, half):
    freqs = THETA ** (-(jnp.arange(half, dtype=jnp.float32) * 2.0) / (2.0 * half))
    angles = positions.astype(jnp.float32)[:, None] * freqs[None, :]
    return (jnp.cos(angles), jnp.sin(angles))


def rotate(tensor, cosine, sine):
    half = tensor.shape[-1] // 2
    first = tensor[..., :half]
    second = tensor[..., half:]
    cosine = cosine[:, None, :]
    sine = sine[:, None, :]
    return jnp.concatenate(
        [first * cosine - second * sine, second * cosine + first * sine], axis=-1
    )


def unrotate(tensor, cosine, sine):
    half = tensor.shape[-1] // 2
    first = tensor[..., :half]
    second = tensor[..., half:]
    cosine = cosine[:, None, :]
    sine = sine[:, None, :]
    return jnp.concatenate(
        [first * cosine + second * sine, second * cosine - first * sine], axis=-1
    )


def normalize(values):
    factor = lax.rsqrt(jnp.mean(values * values, axis=-1, keepdims=True) + EPSILON)
    return (values * factor, factor)


def contract_last(left, right):
    return lax.dot_general(
        left, right, (((1,), (1,)), ((), ())), preferred_element_type=jnp.float32
    )


def contract_first(left, right):
    return lax.dot_general(
        left, right, (((0,), (0,)), ((), ())), preferred_element_type=jnp.float32
    )


def norm_backward(grad_normed, normed, factor, gain_full):
    scaled = grad_normed * gain_full[None, :]
    return factor * (scaled - normed * jnp.mean(normed * scaled, axis=-1, keepdims=True))


def allowed_mask(query_pos, key_pos, block_len):
    causal = key_pos[None, :] <= query_pos[:, None]
    inside = key_pos[None, None, None, :] < block_len[:, None, None, None]
    return causal[None, None] & inside


def run_blocks(step_fn, carry, pieces):
    total = pieces[0].shape[1]
    block = SUB_BLOCK
    number = total // block
    split = tuple(
        (
            jnp.swapaxes(piece.reshape((piece.shape[0], number, block) + piece.shape[2:]), 0, 1)
            for piece in pieces
        )
    )

    def one_block(state, args):
        sub_pieces, index = args
        return (step_fn(state, sub_pieces, index * block), None)

    carry, unused = lax.scan(one_block, carry, (split, jnp.arange(number, dtype=jnp.int32)))
    return carry


def body(
    inputs,
    cotangent,
    lengths,
    query_weight,
    key_weight,
    value_weight,
    mix_weight,
    gate_weight,
    up_weight,
    down_weight,
    attn_gain,
    ffn_gain,
):
    groups, slots, width = inputs.shape
    head_size = width // HEADS
    per_batch = groups // MB
    rows = per_batch * slots
    scale = head_size ** (-0.5)
    first_slot = lax.axis_index("ctx") * slots
    last_slot = first_slot + slots - 1
    positions = first_slot + jnp.arange(slots, dtype=jnp.int32)
    cosine, sine = rotation(positions, head_size // 2)
    attn_set = (
        lax.all_gather(query_weight, ("dp", "ctx"), axis=0, tiled=True),
        lax.all_gather(key_weight, ("dp", "ctx"), axis=0, tiled=True),
        lax.all_gather(value_weight, ("dp", "ctx"), axis=0, tiled=True),
        lax.all_gather(mix_weight, ("dp", "ctx"), axis=0, tiled=True),
        lax.all_gather(attn_gain, ("dp", "ctx"), axis=0, tiled=True),
    )
    ffn_set = (
        lax.all_gather(gate_weight, ("dp", "ctx"), axis=0, tiled=True),
        lax.all_gather(up_weight, ("dp", "ctx"), axis=0, tiled=True),
        lax.all_gather(down_weight, ("dp", "ctx"), axis=0, tiled=True),
        lax.all_gather(ffn_gain, ("dp", "ctx"), axis=0, tiled=True),
    )
    query_full, key_full, value_full, mix_full, attn_gain_full = attn_set
    gate_full, up_full, down_full, ffn_gain_full = ffn_set
    attn_full = attn_gain_full.astype(jnp.float32)
    ffn_full = ffn_gain_full.astype(jnp.float32)
    outputs_list = []
    saved = []
    for part in range(MB):
        block_in = (
            inputs[part * per_batch : (part + 1) * per_batch]
            .reshape(rows, width)
            .astype(jnp.float32)
        )
        block_len = lengths[part * per_batch : (part + 1) * per_batch]
        longest = jnp.max(block_len)
        valid = (positions[None, :] < block_len[:, None]).astype(jnp.float32).reshape(rows, 1)
        normed_one, factor_one = normalize(block_in)
        xn_one = (normed_one * attn_full[None, :]).astype(jnp.bfloat16)
        queries = jnp.dot(xn_one, query_full, preferred_element_type=jnp.float32)
        keys = jnp.dot(xn_one, key_full, preferred_element_type=jnp.float32)
        values = jnp.dot(xn_one, value_full, preferred_element_type=jnp.float32)
        query_rot = rotate(
            queries.reshape(per_batch, slots, HEADS, head_size), cosine, sine
        ).astype(jnp.bfloat16)
        key_rot = rotate(keys.reshape(per_batch, slots, HEADS, head_size), cosine, sine).astype(
            jnp.bfloat16
        )
        value_low = values.astype(jnp.bfloat16).reshape(per_batch, slots, HEADS, head_size)
        key_flat = key_rot.reshape(per_batch, slots, width)
        value_flat = value_low.reshape(per_batch, slots, width)

        def attend_piece(carry, pieces, start):
            key_piece, value_piece = pieces
            count = key_piece.shape[1]

            def attend_compute(state):
                run_max, run_sum, run_out = state
                key_heads = key_piece.reshape(per_batch, count, HEADS, head_size)
                value_heads = value_piece.reshape(per_batch, count, HEADS, head_size)
                key_pos = start + jnp.arange(count, dtype=jnp.int32)
                allowed = allowed_mask(positions, key_pos, block_len)
                scores = (
                    jnp.einsum(
                        "bqhd,bkhd->bhqk", query_rot, key_heads, preferred_element_type=jnp.float32
                    )
                    * scale
                )
                masked = jnp.where(allowed, scores, NEGATIVE)
                new_max = jnp.maximum(run_max, jnp.max(masked, axis=-1))
                weights = jnp.where(allowed, jnp.exp(masked - new_max[..., None]), 0.0)
                factor = jnp.exp(run_max - new_max)
                new_sum = run_sum * factor + jnp.sum(weights, axis=-1)
                new_out = run_out * factor[..., None] + jnp.einsum(
                    "bhqk,bkhd->bhqd",
                    weights.astype(jnp.bfloat16),
                    value_heads,
                    preferred_element_type=jnp.float32,
                )
                return (new_max, new_sum, new_out)

            needed = (start <= last_slot) & (start < longest)
            return lax.cond(needed, attend_compute, lambda state: state, carry)

        start_state = (
            jnp.full((per_batch, HEADS, slots), NEGATIVE, jnp.float32),
            jnp.zeros((per_batch, HEADS, slots), jnp.float32),
            jnp.zeros((per_batch, HEADS, slots, head_size), jnp.float32),
        )
        keys_all, values_all = (
            lax.all_gather(key_flat, "ctx", axis=1, tiled=True),
            lax.all_gather(value_flat, "ctx", axis=1, tiled=True),
        )
        run_max, run_sum, run_out = run_blocks(attend_piece, start_state, (keys_all, values_all))
        attended = jnp.transpose(run_out / run_sum[..., None], (0, 2, 1, 3))
        log_total = run_max + jnp.log(run_sum)
        mixed_in = attended.reshape(rows, width).astype(jnp.bfloat16)
        residual = block_in + jnp.dot(mixed_in, mix_full, preferred_element_type=jnp.float32)
        normed_two, factor_two = normalize(residual)
        xn_two = (normed_two * ffn_full[None, :]).astype(jnp.bfloat16)
        gate = jnp.dot(xn_two, gate_full, preferred_element_type=jnp.float32)
        up = jnp.dot(xn_two, up_full, preferred_element_type=jnp.float32)
        sigma = jax.nn.sigmoid(gate)
        silu_gate = gate * sigma
        hidden = (silu_gate * up).astype(jnp.bfloat16)
        branch = contract_last(hidden, down_full)
        outputs_list.append(
            (valid * (residual + branch)).astype(jnp.bfloat16).reshape(per_batch, slots, width)
        )
        saved.append(
            {
                "block_len": block_len,
                "longest": longest,
                "valid": valid,
                "normed_one": normed_one,
                "factor_one": factor_one,
                "xn_one": xn_one,
                "query_rot": query_rot,
                "key_rot": key_rot,
                "value_low": value_low,
                "key_flat": key_flat,
                "value_flat": value_flat,
                "attended": attended,
                "log_total": log_total,
                "mixed_in": mixed_in,
                "normed_two": normed_two,
                "factor_two": factor_two,
                "xn_two": xn_two,
                "gate": gate,
                "up": up,
                "sigma": sigma,
                "silu_gate": silu_gate,
                "hidden": hidden,
            }
        )
    ffn_back_set = (
        lax.all_gather(gate_weight, ("dp", "ctx"), axis=0, tiled=True),
        lax.all_gather(up_weight, ("dp", "ctx"), axis=0, tiled=True),
        lax.all_gather(down_weight, ("dp", "ctx"), axis=0, tiled=True),
        lax.all_gather(ffn_gain, ("dp", "ctx"), axis=0, tiled=True),
    )
    attn_back_set = (
        lax.all_gather(query_weight, ("dp", "ctx"), axis=0, tiled=True),
        lax.all_gather(key_weight, ("dp", "ctx"), axis=0, tiled=True),
        lax.all_gather(value_weight, ("dp", "ctx"), axis=0, tiled=True),
        lax.all_gather(mix_weight, ("dp", "ctx"), axis=0, tiled=True),
        lax.all_gather(attn_gain, ("dp", "ctx"), axis=0, tiled=True),
    )
    gate_back, up_back, down_back, ffn_gain_back = ffn_back_set
    query_back, key_back, value_back, mix_back, attn_gain_back = attn_back_set
    attn_full_back = attn_gain_back.astype(jnp.float32)
    ffn_full_back = ffn_gain_back.astype(jnp.float32)
    grads_list = []
    records = []
    attn_gain_term = jnp.zeros((width,), jnp.float32)
    ffn_gain_term = jnp.zeros((width,), jnp.float32)
    for part in range(MB):
        item = saved[part]
        block_len = item["block_len"]
        longest = item["longest"]
        query_rot = item["query_rot"]
        key_rot = item["key_rot"]
        value_low = item["value_low"]
        block_cot = (
            cotangent[part * per_batch : (part + 1) * per_batch]
            .reshape(rows, width)
            .astype(jnp.float32)
        )
        grad_out = block_cot * item["valid"]
        grad_low = grad_out.astype(jnp.bfloat16)
        grad_hidden = jnp.dot(grad_low, down_back, preferred_element_type=jnp.float32)
        sigma = item["sigma"]
        gate = item["gate"]
        gate_low = (grad_hidden * item["up"] * sigma * (1.0 + gate * (1.0 - sigma))).astype(
            jnp.bfloat16
        )
        up_low = (grad_hidden * item["silu_gate"]).astype(jnp.bfloat16)
        grad_two = contract_last(gate_low, gate_back) + contract_last(up_low, up_back)
        normed_two = item["normed_two"]
        ffn_gain_term = ffn_gain_term + jnp.sum(grad_two * normed_two, axis=0)
        dres = grad_out + norm_backward(grad_two, normed_two, item["factor_two"], ffn_full_back)
        dres_low = dres.astype(jnp.bfloat16)
        grad_mixed = contract_last(dres_low, mix_back)
        grad_heads = grad_mixed.astype(jnp.bfloat16).reshape(per_batch, slots, HEADS, head_size)
        delta = jnp.sum(grad_heads.astype(jnp.float32) * item["attended"], axis=-1)
        delta_local = jnp.transpose(delta, (0, 2, 1))
        log_total = item["log_total"]

        def query_piece_grads(carry, pieces, start):
            key_piece, value_piece = pieces
            count = key_piece.shape[1]

            def query_compute(total):
                key_heads = key_piece.reshape(per_batch, count, HEADS, head_size)
                value_heads = value_piece.reshape(per_batch, count, HEADS, head_size)
                key_pos = start + jnp.arange(count, dtype=jnp.int32)
                allowed = allowed_mask(positions, key_pos, block_len)
                scores = (
                    jnp.einsum(
                        "bqhd,bkhd->bhqk", query_rot, key_heads, preferred_element_type=jnp.float32
                    )
                    * scale
                )
                prob = jnp.where(
                    allowed,
                    jnp.exp(jnp.where(allowed, scores, NEGATIVE) - log_total[..., None]),
                    0.0,
                )
                grad_prob = jnp.einsum(
                    "bqhd,bkhd->bhqk", grad_heads, value_heads, preferred_element_type=jnp.float32
                )
                grad_score = (prob * (grad_prob - delta_local[..., None]) * scale).astype(
                    jnp.bfloat16
                )
                return total + jnp.einsum(
                    "bhqk,bkhd->bqhd", grad_score, key_heads, preferred_element_type=jnp.float32
                )

            needed = (start <= last_slot) & (start < longest)
            return lax.cond(needed, query_compute, lambda total: total, carry)

        head_empty = jnp.zeros((per_batch, slots, HEADS, head_size), jnp.float32)
        keys_again, values_again = (
            lax.all_gather(item["key_flat"], "ctx", axis=1, tiled=True),
            lax.all_gather(item["value_flat"], "ctx", axis=1, tiled=True),
        )
        grad_query_rot = run_blocks(query_piece_grads, head_empty, (keys_again, values_again))
        query_flat = query_rot.reshape(per_batch, slots, width)
        grad_flat = grad_heads.reshape(per_batch, slots, width)
        log_sent = jnp.transpose(log_total, (0, 2, 1))

        def key_value_piece(carry, pieces, start):
            query_piece, grad_piece, log_piece, delta_piece = pieces
            count = query_piece.shape[1]

            def key_compute(state):
                key_total, value_total = state
                query_heads = query_piece.reshape(per_batch, count, HEADS, head_size)
                grad_piece_heads = grad_piece.reshape(per_batch, count, HEADS, head_size)
                query_pos = start + jnp.arange(count, dtype=jnp.int32)
                allowed = jnp.swapaxes(allowed_mask(query_pos, positions, block_len), -1, -2)
                scores = (
                    jnp.einsum(
                        "bkhd,bqhd->bhkq", key_rot, query_heads, preferred_element_type=jnp.float32
                    )
                    * scale
                )
                log_heads = jnp.transpose(log_piece, (0, 2, 1))
                delta_heads = jnp.transpose(delta_piece, (0, 2, 1))
                prob = jnp.where(
                    allowed,
                    jnp.exp(jnp.where(allowed, scores, NEGATIVE) - log_heads[:, :, None, :]),
                    0.0,
                )
                value_total = value_total + jnp.einsum(
                    "bhkq,bqhd->bkhd",
                    prob.astype(jnp.bfloat16),
                    grad_piece_heads,
                    preferred_element_type=jnp.float32,
                )
                grad_prob = jnp.einsum(
                    "bkhd,bqhd->bhkq",
                    value_low,
                    grad_piece_heads,
                    preferred_element_type=jnp.float32,
                )
                grad_score = (prob * (grad_prob - delta_heads[:, :, None, :]) * scale).astype(
                    jnp.bfloat16
                )
                key_total = key_total + jnp.einsum(
                    "bhkq,bqhd->bkhd", grad_score, query_heads, preferred_element_type=jnp.float32
                )
                return (key_total, value_total)

            needed = (start + count - 1 >= first_slot) & (first_slot < longest)
            return lax.cond(needed, key_compute, lambda state: state, carry)

        gathered = (
            lax.all_gather(query_flat, "ctx", axis=1, tiled=True),
            lax.all_gather(grad_flat, "ctx", axis=1, tiled=True),
            lax.all_gather(log_sent.astype(jnp.bfloat16), "ctx", axis=1, tiled=True).astype(
                log_sent.dtype
            ),
            lax.all_gather(delta.astype(jnp.bfloat16), "ctx", axis=1, tiled=True).astype(
                delta.dtype
            ),
        )
        grad_key_rot, grad_value = run_blocks(
            key_value_piece, (head_empty, head_empty), tuple(gathered)
        )
        query_low = unrotate(grad_query_rot, cosine, sine).astype(jnp.bfloat16).reshape(rows, width)
        key_low = unrotate(grad_key_rot, cosine, sine).astype(jnp.bfloat16).reshape(rows, width)
        value_grad_low = grad_value.astype(jnp.bfloat16).reshape(rows, width)
        grad_one = (
            contract_last(query_low, query_back)
            + contract_last(key_low, key_back)
            + contract_last(value_grad_low, value_back)
        )
        normed_one = item["normed_one"]
        attn_gain_term = attn_gain_term + jnp.sum(grad_one * normed_one, axis=0)
        input_part = dres + norm_backward(grad_one, normed_one, item["factor_one"], attn_full_back)
        grads_list.append(input_part.astype(jnp.bfloat16).reshape(per_batch, slots, width))
        records.append(
            {
                "xn_one": item["xn_one"],
                "query_low": query_low,
                "key_low": key_low,
                "value_low": value_grad_low,
                "mixed_in": item["mixed_in"],
                "dres_low": dres_low,
                "xn_two": item["xn_two"],
                "gate_low": gate_low,
                "up_low": up_low,
                "grad_low": grad_low,
                "hidden": item["hidden"],
            }
        )

    def joined(name):
        return jnp.concatenate([record[name] for record in records], axis=0)

    xn_one_all = joined("xn_one")
    attn_terms = (
        contract_first(xn_one_all, joined("query_low")),
        contract_first(xn_one_all, joined("key_low")),
        contract_first(xn_one_all, joined("value_low")),
        contract_first(joined("mixed_in"), joined("dres_low")),
        attn_gain_term,
        ffn_gain_term,
    )
    attn_parts = (
        lax.psum_scatter(attn_terms[0], ("dp", "ctx"), scatter_dimension=0, tiled=True),
        lax.psum_scatter(attn_terms[1], ("dp", "ctx"), scatter_dimension=0, tiled=True),
        lax.psum_scatter(attn_terms[2], ("dp", "ctx"), scatter_dimension=0, tiled=True),
        lax.psum_scatter(attn_terms[3], ("dp", "ctx"), scatter_dimension=0, tiled=True),
        lax.psum_scatter(attn_terms[4], ("dp", "ctx"), scatter_dimension=0, tiled=True),
        lax.psum_scatter(attn_terms[5], ("dp", "ctx"), scatter_dimension=0, tiled=True),
    )
    xn_two_all = joined("xn_two")
    gate_low_all = joined("gate_low")
    up_low_all = joined("up_low")
    grad_low_all = joined("grad_low")
    hidden_all = joined("hidden")
    hidden_width = gate_weight.shape[1]
    all_rows = xn_two_all.shape[0]
    stacked_left = jnp.concatenate([xn_two_all, grad_low_all], axis=0)
    upper_right = jnp.concatenate(
        [gate_low_all, up_low_all, jnp.zeros((all_rows, hidden_width), jnp.bfloat16)], axis=1
    )
    lower_right = jnp.concatenate(
        [jnp.zeros((all_rows, 2 * hidden_width), jnp.bfloat16), hidden_all], axis=1
    )
    stacked_right = jnp.concatenate([upper_right, lower_right], axis=0)
    ffn_parts = lax.psum_scatter(
        contract_first(stacked_left, stacked_right), ("dp", "ctx"), scatter_dimension=0, tiled=True
    )
    gate_grad = ffn_parts[:, :hidden_width]
    up_grad = ffn_parts[:, hidden_width : 2 * hidden_width]
    down_grad = ffn_parts[:, 2 * hidden_width :]
    activations = jnp.concatenate(outputs_list, axis=0)
    input_grad = jnp.concatenate(grads_list, axis=0)
    return (
        activations,
        input_grad,
        attn_parts[0],
        attn_parts[1],
        attn_parts[2],
        attn_parts[3],
        gate_grad,
        up_grad,
        down_grad,
        attn_parts[4],
        attn_parts[5],
    )


def solution(mesh):
    in_specs = (
        P("dp", "ctx", None),
        P("dp", "ctx", None),
        P("dp"),
        P(("dp", "ctx"), None),
        P(("dp", "ctx"), None),
        P(("dp", "ctx"), None),
        P(("dp", "ctx"), None),
        P(("dp", "ctx"), None),
        P(("dp", "ctx"), None),
        P(("dp", "ctx"), None),
        P(("dp", "ctx")),
        P(("dp", "ctx")),
    )
    out_specs = (
        P("dp", "ctx", None),
        P("dp", "ctx", None),
        P(("dp", "ctx"), None),
        P(("dp", "ctx"), None),
        P(("dp", "ctx"), None),
        P(("dp", "ctx"), None),
        P(("dp", "ctx"), None),
        P(("dp", "ctx"), None),
        P(("dp", "ctx"), None),
        P(("dp", "ctx")),
        P(("dp", "ctx")),
    )
    return jax.shard_map(body, mesh=mesh, in_specs=in_specs, out_specs=out_specs, check_vma=False)
```

profile of v0, /device:TPU:0, one launch (start us, length us, event | category | flops | bytes accessed | tf_op | source)
XLA Modules:
  0.0 4453.8 jit_solution(5979839053192137578)
XLA Ops:
  11.2 43.4 all-reduce.6
  57.1 33.9 all-gather.26.cloned.1.call-done
  97.0 72.6 %all-gather.22.cloned.1.call-done = bf16[2048,2048]{1,0:T(8,128)(2,1)} async-done(((bf16[64,2048]{1,0:T(8,128)(2,1)}), bf16[2048,2048]{1,0:T(8,128)(2,1)}) %all-gather.22.cloned.1.call-update) | async-done | bytes 8388624 | tf_op jit(solution)/shard_map/all_gather | solution.py:116
  169.6 12.2 copy.134
  181.8 66.6 %all-gather.20.cloned.1.call-done = bf16[2048,2048]{1,0:T(8,128)(2,1)} async-done(((bf16[64,2048]{1,0:T(8,128)(2,1)}), bf16[2048,2048]{1,0:T(8,128)(2,1)}) %all-gather.20.cloned.1.call-update) | async-done | bytes 8388624 | tf_op jit(solution)/shard_map/all_gather | solution.py:115
  248.4 12.3 copy.133
  298.1 50.2 %all-gather.24.cloned.1.call-done = bf16[1,512,2048]{2,1,0:T(8,128)(2,1)} async-done(((bf16[1,64,2048]{2,1,0:T(8,128)(2,1)}), bf16[1,512,2048]{2,1,0:T(8,128)(2,1)}) %all-gather.24.cloned.1.call-update) | async-done | bytes 2097168 | tf_op jit(solution)/shard_map/all_gather | solution.py:195
  348.3 14.9 conditional.6
  366.5 31.5 all-gather.44.cloned.1.call-done
  398.0 50.4 %all-gather.36.cloned.1.call-done = bf16[1,512,2048]{2,1,0:T(8,128)(2,1)} async-done(((bf16[1,64,2048]{2,1,0:T(8,128)(2,1)}), bf16[1,512,2048]{2,1,0:T(8,128)(2,1)}) %all-gather.36.cloned.1.call-update) | async-done | bytes 2097168 | tf_op jit(solution)/shard_map/all_gather | solution.py:195
  448.3 15.2 conditional.7
  464.7 62.2 %all-gather.28.cloned.1.call-done = bf16[2048,2048]{1,0:T(8,128)(2,1)} async-done(((bf16[64,2048]{1,0:T(8,128)(2,1)}), bf16[2048,2048]{1,0:T(8,128)(2,1)}) %all-gather.28.cloned.1.call-update) | async-done | bytes 8388624 | tf_op jit(solution)/shard_map/all_gather | solution.py:118
  534.6 188.2 %all-gather.32.cloned.1.call-done = bf16[2048,8192]{1,0:T(8,128)(2,1)} async-done(((bf16[64,8192]{1,0:T(8,128)(2,1)}), bf16[2048,8192]{1,0:T(8,128)(2,1)}) %all-gather.32.cloned.1.call-update) | async-done | bytes 33554448 | tf_op jit(solution)/shard_map/all_gather | solution.py:123
  722.8 15.8 fusion.236
  738.6 179.4 %all-gather.30.cloned.1.call-done = bf16[2048,8192]{1,0:T(8,128)(2,1)} async-done(((bf16[64,8192]{1,0:T(8,128)(2,1)}), bf16[2048,8192]{1,0:T(8,128)(2,1)}) %all-gather.30.cloned.1.call-update) | async-done | bytes 33554448 | tf_op jit(solution)/shard_map/all_gather | solution.py:122
  918.0 15.6 fusion.235
  933.7 179.8 %all-gather.34.cloned.1.call-done = bf16[2048,8192]{1,0:T(8,128)(2,1)} async-done(((bf16[64,8192]{1,0:T(8,128)(2,1)}), bf16[2048,8192]{1,0:T(8,128)(2,1)}) %all-gather.34.cloned.1.call-update) | async-done | bytes 33554448 | tf_op jit(solution)/shard_map/all_gather | solution.py:124
  1113.4 19.6 multiply_convert_fusion.6
  1133.0 16.2 fusion.239
  1149.2 16.5 multiply_reduce_fusion.1
  1165.7 14.9 fusion.238
  1180.6 14.9 fusion.237
  1195.5 19.4 multiply_convert_fusion.4
  1214.9 15.8 fusion.241
  1230.7 16.3 multiply_reduce_fusion
  1272.6 70.4 %fusion.124 = f32[2048,24576]{1,0:T(8,128)} fusion(bf16[128,24576]{1,0:T(8,128)(2,1)} %fusion.136, bf16[128,8192]{1,0:T(8,128)(2,1)} %broadcast_in_dim.162, bf16[64,8192]{1,0:T(8,128)(2,1)S(1)} %get-tuple-element.949, bf16[64,8192]{1,0:T(8,128)(2,1)S(1)} %copy-done.11, bf16[64,8192]{1,0:T(8,128)(2,1)} %copy-done.14, bf16[64,8192]{1,0:T(8,128)(2,1)S(1)} %copy-done.13, ...), kind=kOutput, calls=%fused_computation.131 | convolution fusion | flops 25849495552 | bytes 214958080 | tf_op jit(solution)/shard_map/dot_general | solution.py:56
  1344.2 8.2 fusion.198
  1354.0 31.4 all_gather.94
  1386.3 31.3 all_gather.90
  1421.4 29.4 conditional.10
  1436.1 7.5 fusion.111
  1450.8 30.7 all_gather.96
  1484.4 24.5 conditional.8
  1497.5 7.6 fusion.100
  1508.9 30.7 all_gather.92
  1540.6 31.3 conditional.11
  1574.7 29.4 conditional.9
  1610.4 11.9 fusion.190
  1625.6 11.7 fusion.186
  1640.7 11.8 fusion.194
  1654.3 18.7 fusion.142
  1673.1 16.9 fusion.141
  1718.4 41.1 all-reduce.5
  1761.9 1244.3 %reduce-scatter.14.cloned.1.call-done = f32[64,24576]{1,0:T(8,128)} async-done(((f32[2048,24576]{1,0:T(8,128)}), f32[64,24576]{1,0:T(8,128)}) %reduce-scatter.14.cloned.1.call-update) | async-done | bytes 6291472 | tf_op jit(solution)/shard_map/reduce_scatter | solution.py:458
  3011.9 354.4 %reduce-scatter.12.cloned.1.call-done = f32[64,2048]{1,0:T(8,128)} async-done(((f32[2048,2048]{1,0:T(8,128)}), f32[64,2048]{1,0:T(8,128)}) %reduce-scatter.12.cloned.1.call-update) | async-done | bytes 524304 | tf_op jit(solution)/shard_map/reduce_scatter | solution.py:439
  3366.3 360.1 %reduce-scatter.8.cloned.1.call-done = f32[64,2048]{1,0:T(8,128)} async-done(((f32[2048,2048]{1,0:T(8,128)}), f32[64,2048]{1,0:T(8,128)}) %reduce-scatter.8.cloned.1.call-update) | async-done | bytes 524304 | tf_op jit(solution)/shard_map/reduce_scatter | solution.py:437
  3726.4 360.2 %reduce-scatter.6.cloned.1.call-done = f32[64,2048]{1,0:T(8,128)} async-done(((f32[2048,2048]{1,0:T(8,128)}), f32[64,2048]{1,0:T(8,128)}) %reduce-scatter.6.cloned.1.call-update) | async-done | bytes 524304 | tf_op jit(solution)/shard_map/reduce_scatter | solution.py:436
  4086.6 360.1 %reduce-scatter.10.cloned.1.call-done = f32[64,2048]{1,0:T(8,128)} async-done(((f32[2048,2048]{1,0:T(8,128)}), f32[64,2048]{1,0:T(8,128)}) %reduce-scatter.10.cloned.1.call-update) | async-done | bytes 524304 | tf_op jit(solution)/shard_map/reduce_scatter | solution.py:438
  (388 shorter events, 277.2 us)
Async XLA Ops:
  7.2 83.7 %all-gather.26.cloned.1.call-start = ((), (), s32[]{:S(2)}) async-start(), calls=%async_computation.8 | async-start | bytes 8650752 | tf_op jit(solution)/shard_map/all_gather | solution.py:117
  7.9 161.7 %all-gather.22.cloned.1.call-start = ((), (), s32[]{:S(2)}) async-start(), calls=%async_computation.6 | async-start | bytes 8650752 | tf_op jit(solution)/shard_map/all_gather | solution.py:116
  8.7 239.7 %all-gather.20.cloned.1.call-start = ((), (), s32[]{:S(2)}) async-start(), calls=%async_computation.5 | async-start | bytes 8650752 | tf_op jit(solution)/shard_map/all_gather | solution.py:115
  9.4 288.7 %all-gather.42.cloned.1.call-start = ((), (), s32[]{:S(2)}) async-start(), calls=%async_computation.21 | async-start | bytes 2359296 | tf_op jit(solution)/shard_map/all_gather | solution.py:196
  54.5 217.2 %copy-start.57 = (f32[2048]{0:T(1024)}, f32[2048]{0:T(1024)S(1)}, u32[]{:S(2)}) copy-start(f32[2048]{0:T(1024)S(1)} %convert_element_type.426) | copy-start | bytes 24580
  55.8 213.4 %copy-start.72 = (f32[64]{0:T(128)}, f32[64]{0:T(128)S(1)}, u32[]{:S(2)}) copy-start(f32[64]{0:T(128)S(1)} %get-tuple-element.1002) | copy-start | bytes 772
  55.8 215.9 %copy-start.74 = (f32[64]{0:T(128)}, f32[64]{0:T(128)S(1)}, u32[]{:S(2)}) copy-start(f32[64]{0:T(128)S(1)} %get-tuple-element.1003) | copy-start | bytes 772
  57.0 219.6 %copy-start.21 = (bf16[64,2048]{1,0:T(8,128)(2,1)}, bf16[64,2048]{1,0:T(8,128)(2,1)S(1)}, u32[]{:S(2)}) copy-start(bf16[64,2048]{1,0:T(8,128)(2,1)S(1)} %get-tuple-element.973) | copy-start | bytes 786436
  96.6 251.7 %all-gather.24.cloned.1.call-start = ((), (), s32[]{:S(2)}) async-start(), calls=%async_computation.7 | async-start | bytes 2359296 | tf_op jit(solution)/shard_map/all_gather | solution.py:195
  97.0 177.2 %copy-start.63 = (f32[64,32]{0,1:T(8,128)}, f32[64,32]{0,1:T(8,128)S(1)}, u32[]{:S(2)}) copy-start(f32[64,32]{0,1:T(8,128)S(1)} %get-tuple-element.989) | copy-start | bytes 24580
  97.0 177.2 %copy-start.65 = (f32[64,32]{0,1:T(8,128)}, f32[64,32]{0,1:T(8,128)S(1)}, u32[]{:S(2)}) copy-start(f32[64,32]{0,1:T(8,128)S(1)} %get-tuple-element.990) | copy-start | bytes 24580
  276.6 121.3 %all-gather.44.cloned.1.call-start = ((), (), s32[]{:S(2)}) async-start(), calls=%async_computation.22 | async-start | bytes 2359296 | tf_op jit(solution)/shard_map/all_gather | solution.py:196
  282.4 165.9 %all-gather.36.cloned.1.call-start = ((), (), s32[]{:S(2)}) async-start(), calls=%async_computation.13 | async-start | bytes 2359296 | tf_op jit(solution)/shard_map/all_gather | solution.py:195
  283.7 243.3 %all-gather.28.cloned.1.call-start = ((), (), s32[]{:S(2)}) async-start(), calls=%async_computation.9 | async-start | bytes 8650752 | tf_op jit(solution)/shard_map/all_gather | solution.py:118
  284.5 438.3 %all-gather.32.cloned.1.call-start = ((), (), s32[]{:S(2)}) async-start(), calls=%async_computation.11 | async-start | bytes 34603008 | tf_op jit(solution)/shard_map/all_gather | solution.py:123
  285.2 632.8 %all-gather.30.cloned.1.call-start = ((), (), s32[]{:S(2)}) async-start(), calls=%async_computation.10 | async-start | bytes 34603008 | tf_op jit(solution)/shard_map/all_gather | solution.py:122
  285.8 827.6 %all-gather.34.cloned.1.call-start = ((), (), s32[]{:S(2)}) async-start(), calls=%async_computation.12 | async-start | bytes 34603008 | tf_op jit(solution)/shard_map/all_gather | solution.py:124
  286.5 1254.1 %all-gather.40.cloned.1.call-start = ((), (), s32[]{:S(2)}) async-start(), calls=%async_computation.15 | async-start | bytes 2359296 | tf_op jit(solution)/shard_map/all_gather | solution.py:383
  288.7 159.7 %copy-start.76 = (s32[64]{0:T(128)}, s32[64]{0:T(128)S(1)}, u32[]{:S(2)}) copy-start(s32[64]{0:T(128)S(1)} %iota_add_fusion) | copy-start | bytes 772
  290.0 957.0 %copy-start.78 = (f32[64]{0:T(128)}, f32[64]{0:T(128)S(1)}, u32[]{:S(2)}) copy-start(f32[64]{0:T(128)S(1)} %get-tuple-element.1000) | copy-start | bytes 772
  290.0 957.0 %copy-start.80 = (f32[64]{0:T(128)}, f32[64]{0:T(128)S(1)}, u32[]{:S(2)}) copy-start(f32[64]{0:T(128)S(1)} %get-tuple-element.1001) | copy-start | bytes 772
  292.1 156.2 %copy-start.25 = (bf16[1,64,32,64]{1,3,2,0:T(8,128)(2,1)}, bf16[1,64,32,64]{1,3,2,0:T(8,128)(2,1)S(1)}, u32[]{:S(2)}) copy-start(bf16[1,64,32,64]{1,3,2,0:T(8,128)(2,1)S(1)} %maximum_convert_fusion.2) | copy-start | bytes 786436
  293.0 1247.6 %all-gather.48.cloned.1.call-start = ((), (), s32[]{:S(2)}) async-start(), calls=%async_computation.24 | async-start | bytes 2359296 | tf_op jit(solution)/shard_map/all_gather | solution.py:384
  363.2 85.1 %copy-start.67 = (f32[1,32,64]{2,1,0:T(8,128)}, f32[1,32,64]{2,1,0:T(8,128)S(1)}, u32[]{:S(2)}) copy-start(f32[1,32,64]{2,1,0:T(8,128)S(1)} %get-tuple-element.610) | copy-start | bytes 24580
  363.2 85.1 %copy-start.17 = (f32[1,32,64,64]{3,2,1,0:T(8,128)}, f32[1,32,64,64]{3,2,1,0:T(8,128)S(1)}, u32[]{:S(2)}) copy-start(f32[1,32,64,64]{3,2,1,0:T(8,128)S(1)} %get-tuple-element.609) | copy-start | bytes 1572868
  366.4 165.8 %copy-start.32 = (bf16[64,2048]{1,0:T(8,128)(2,1)}, bf16[64,2048]{1,0:T(8,128)(2,1)S(1)}, u32[]{:S(2)}) copy-start(bf16[64,2048]{1,0:T(8,128)(2,1)S(1)} %convert_element_type.435) | copy-start | bytes 786436
  463.6 68.7 %copy-start.4 = (f32[1,32,64,64]{3,2,1,0:T(8,128)}, f32[1,32,64,64]{3,2,1,0:T(8,128)S(1)}, u32[]{:S(2)}) copy-start(f32[1,32,64,64]{3,2,1,0:T(8,128)S(1)} %get-tuple-element.611) | copy-start | bytes 1572868
  463.6 68.7 %copy-start.55 = (f32[1,32,64]{2,1,0:T(8,128)}, f32[1,32,64]{2,1,0:T(8,128)S(1)}, u32[]{:S(2)}) copy-start(f32[1,32,64]{2,1,0:T(8,128)S(1)} %get-tuple-element.612) | copy-start | bytes 24580
  463.6 68.7 %copy-start.61 = (f32[1,32,64]{1,0,2:T(1,128)}, f32[1,32,64]{1,0,2:T(1,128)S(1)}, u32[]{:S(2)}) copy-start(f32[1,32,64]{1,0,2:T(1,128)S(1)} %get-tuple-element.836) | copy-start | bytes 24580
  464.7 67.5 %copy-start.34 = (bf16[64,2048]{1,0:T(8,128)(2,1)}, bf16[64,2048]{1,0:T(8,128)(2,1)S(1)}, u32[]{:S(2)}) copy-start(bf16[64,2048]{1,0:T(8,128)(2,1)S(1)} %convert_element_type.452) | copy-start | bytes 786436
  532.3 714.8 %copy-start.6 = (f32[64,2048]{1,0:T(8,128)}, f32[64,2048]{1,0:T(8,128)S(1)}, u32[]{:S(2)}) copy-start(f32[64,2048]{1,0:T(8,128)S(1)} %get-tuple-element.996) | copy-start | bytes 1572868
  534.5 712.5 %copy-start.8 = (f32[64,2048]{1,0:T(8,128)}, f32[64,2048]{1,0:T(8,128)S(1)}, u32[]{:S(2)}) copy-start(f32[64,2048]{1,0:T(8,128)S(1)} %get-tuple-element.994) | copy-start | bytes 1572868
  534.6 383.4 %copy-start.27 = (bf16[64,2048]{1,0:T(8,128)(2,1)}, bf16[64,2048]{1,0:T(8,128)(2,1)S(1)}, u32[]{:S(2)}) copy-start(bf16[64,2048]{1,0:T(8,128)(2,1)S(1)} %multiply_convert_fusion.11) | copy-start | bytes 786436
  738.6 374.8 %copy-start.45 = (bf16[64,2048]{1,0:T(8,128)(2,1)S(1)}, bf16[64,2048]{1,0:T(8,128)(2,1)}, u32[]{:S(2)}) copy-start(bf16[64,2048]{1,0:T(8,128)(2,1)} %get-tuple-element.974) | copy-start | bytes 786436
  1255.4 319.3 %all-gather.38.cloned.1.call-start = ((), (), s32[]{:S(2)}) async-start(), calls=%async_computation.14 | async-start | bytes 2359296 | tf_op jit(solution)/shard_map/all_gather | solution.py:383
  1257.4 317.3 %all-gather.46.cloned.1.call-start = ((), (), s32[]{:S(2)}) async-start(), calls=%async_computation.23 | async-start | bytes 2359296 | tf_op jit(solution)/shard_map/all_gather | solution.py:384
  1264.2 1742.0 %reduce-scatter.14.cloned.1.call-start = ((), (), s32[]{:S(2)}) async-start(), calls=%async_computation.20 | async-start | bytes 207618048 | tf_op jit(solution)/shard_map/reduce_scatter | solution.py:458
  1343.0 2023.2 %reduce-scatter.12.cloned.1.call-start = ((), (), s32[]{:S(2)}) async-start(), calls=%async_computation.19 | async-start | bytes 17301504 | tf_op jit(solution)/shard_map/reduce_scatter | solution.py:439
  1352.4 66.3 %copy-start.44 = (bf16[64,2048]{1,0:T(8,128)(2,1)S(1)}, bf16[64,2048]{1,0:T(8,128)(2,1)}, u32[]{:S(2)}) copy-start(bf16[64,2048]{1,0:T(8,128)(2,1)} %convolution_convert_fusion) | copy-start | bytes 786436
  1352.4 66.8 %copy-start.43 = (bf16[64,2048]{1,0:T(8,128)(2,1)S(1)}, bf16[64,2048]{1,0:T(8,128)(2,1)}, u32[]{:S(2)}) copy-start(bf16[64,2048]{1,0:T(8,128)(2,1)} %convolution_convert_fusion.1) | copy-start | bytes 786436
  1352.4 68.1 %copy-start.5 = (f32[1,32,64,64]{3,2,1,0:T(8,128)S(1)}, f32[1,32,64,64]{3,2,1,0:T(8,128)}, u32[]{:S(2)}) copy-start(f32[1,32,64,64]{3,2,1,0:T(8,128)} %copy-done.4) | copy-start | bytes 1572868
  1352.4 68.1 %copy-start.56 = (f32[1,32,64]{2,1,0:T(8,128)S(1)}, f32[1,32,64]{2,1,0:T(8,128)}, u32[]{:S(2)}) copy-start(f32[1,32,64]{2,1,0:T(8,128)} %copy-done.55) | copy-start | bytes 24580
  1352.4 69.0 %copy-start.26 = (bf16[1,64,32,64]{1,3,2,0:T(8,128)(2,1)S(1)}, bf16[1,64,32,64]{1,3,2,0:T(8,128)(2,1)}, u32[]{:S(2)}) copy-start(bf16[1,64,32,64]{1,3,2,0:T(8,128)(2,1)} %copy-done.25) | copy-start | bytes 786436
  1352.4 69.0 %copy-start.77 = (s32[64]{0:T(128)S(1)}, s32[64]{0:T(128)}, u32[]{:S(2)}) copy-start(s32[64]{0:T(128)} %copy-done.76) | copy-start | bytes 772
  1352.4 2374.0 %reduce-scatter.8.cloned.1.call-start = ((), (), s32[]{:S(2)}) async-start(), calls=%async_computation.17 | async-start | bytes 17301504 | tf_op jit(solution)/shard_map/reduce_scatter | solution.py:437
  1421.4 61.2 %copy-start.18 = (f32[1,32,64,64]{3,2,1,0:T(8,128)S(1)}, f32[1,32,64,64]{3,2,1,0:T(8,128)}, u32[]{:S(2)}) copy-start(f32[1,32,64,64]{3,2,1,0:T(8,128)} %copy-done.17) | copy-start | bytes 1572868
  1622.3 2464.3 %reduce-scatter.6.cloned.1.call-start = ((), (), s32[]{:S(2)}) async-start(), calls=%async_computation.16 | async-start | bytes 17301504 | tf_op jit(solution)/shard_map/reduce_scatter | solution.py:436
  1637.3 2809.4 %reduce-scatter.10.cloned.1.call-start = ((), (), s32[]{:S(2)}) async-start(), calls=%async_computation.18 | async-start | bytes 17301504 | tf_op jit(solution)/shard_map/reduce_scatter | solution.py:438
  (61 other events, 713.5 us)
Sparse Core Ops, SparseCore 0:
  11.0 79.8 all-gather.25
  93.9 75.6 all-gather.21
  172.6 75.6 all-gather.19
  250.3 47.7 all-gather.41
  300.6 47.6 all-gather.23
  350.3 47.6 all-gather.43
  400.7 47.6 all-gather.35
  451.3 75.6 all-gather.27
  530.0 192.7 all-gather.31
  725.6 192.3 all-gather.29
  921.0 192.3 all-gather.33
  1115.4 47.2 all-gather.39
  1255.5 47.5 all-gather.47
  1305.0 47.6 all-gather.37
  1354.7 50.3 all-gather.45
  1411.4 1594.7 reduce-scatter.13
  3008.9 357.3 reduce-scatter.11
  3369.0 357.3 reduce-scatter.7
  3729.2 357.3 reduce-scatter.5
  4089.3 357.3 reduce-scatter.9
where the time goes:
time: 4460 us; the launch traced here: 4450 us
  waiting for transfers between devices  3600 us (81%)
  matrix products  457 us (10%)
  blocking collectives  209 us (5%)
  local copies, waits for them, and re-layouts  122 us (3%)
    reduce_scatter x1, waiting for transfers between devices, body(): lax.psum_scatter(contract_first(stacked_left, stacked_right), ('dp', 'ctx...  1240 us
    reduce_scatter x1, waiting for transfers between devices, body(): lax.psum_scatter(attn_terms[0], ('dp', 'ctx'), scatter_dimension=0, tiled...  360 us
    reduce_scatter x1, waiting for transfers between devices, body(): lax.psum_scatter(attn_terms[1], ('dp', 'ctx'), scatter_dimension=0, tiled...  360 us
    reduce_scatter x1, waiting for transfers between devices, body(): lax.psum_scatter(attn_terms[2], ('dp', 'ctx'), scatter_dimension=0, tiled...  360 us
    reduce_scatter x1, waiting for transfers between devices, body(): lax.psum_scatter(attn_terms[3], ('dp', 'ctx'), scatter_dimension=0, tiled...  354 us
    all_gather x1, waiting for transfers between devices, body(): lax.all_gather(up_weight, ('dp', 'ctx'), axis=0, tiled=True)  188 us
    all_gather x1, waiting for transfers between devices, body(): lax.all_gather(down_weight, ('dp', 'ctx'), axis=0, tiled=True)  180 us
    all_gather x1, waiting for transfers between devices, body(): lax.all_gather(gate_weight, ('dp', 'ctx'), axis=0, tiled=True)  179 us
  transfers between devices with their start and end apart: 20, of which 16 were waited for; matrix products, arithmetic and copies ran while one was open for 14% of the time, Pallas kernels for 0%

commit v1 on v0

v1 whole, which is shorter than its diff:
```python
import functools

import jax
import jax.numpy as jnp
from jax import lax
from jax.experimental import pallas as pl
from jax.experimental.pallas import tpu as pltpu
from jax.sharding import PartitionSpec as P

HEADS = 32
EPSILON = 1e-05
THETA = 130000.0
NEGATIVE = -1e30
QUERY_ROWS = 512
BF16 = jnp.bfloat16
F32 = jnp.float32


def normalize(values):
    factor = lax.rsqrt(jnp.mean(values * values, axis=-1, keepdims=True) + EPSILON)
    return (values * factor, factor)


def contract(left, right, left_dim, right_dim):
    return lax.dot_general(
        left, right, (((left_dim,), (right_dim,)), ((), ())), preferred_element_type=F32
    )


class Ring:
    def __init__(self, size):
        self.size = size
        self.order = list(range(0, size, 2)) + list(range(size - 1, 0, -2))
        places = [self.order.index(i) for i in range(size)]
        self.place = jnp.array(places, jnp.int32)[lax.axis_index("ctx")]
        self.table = jnp.array(self.order, jnp.int32)

    def owner(self, ahead):
        return self.table[lax.rem(self.place + ahead + self.size, self.size)]

    def owners(self):
        return jnp.roll(jnp.concatenate([self.table, self.table]), -self.place)[: self.size]

    def shift(self, value, by):
        pairs = [
            (self.order[i], self.order[(i + by) % self.size]) for i in range(self.size)
        ]
        return lax.ppermute(value, "ctx", pairs)

    def gather(self, value):
        size, half = self.size, self.size // 2
        pieces = [None] * size
        pieces[0] = value
        right = left = value
        for step in range(1, half):
            right = self.shift(right, 1)
            left = self.shift(left, -1)
            pieces[size - step] = right
            pieces[step] = left
        rows = value.shape[0] // 2
        pieces[half] = jnp.concatenate(
            [self.shift(right[:rows], 1), self.shift(left[rows:], -1)], axis=0
        )
        return pieces

    def scatter_sum(self, part):
        size, half = self.size, self.size // 2
        lower, upper, whole = 0, 1, 2
        right = part(half, lower).astype(BF16)
        left = part(half, upper).astype(BF16)
        right = self.shift(right, 1)
        left = self.shift(left, -1)
        for step in range(1, half):
            if step == 1:
                right = jnp.concatenate(
                    [part(half - 1, lower) + right.astype(F32), part(half - 1, upper)], axis=1
                )
                left = jnp.concatenate(
                    [part(half + 1, lower), part(half + 1, upper) + left.astype(F32)], axis=1
                )
            else:
                right = part(half - step, whole) + right.astype(F32)
                left = part(half + step, whole) + left.astype(F32)
            right = self.shift(right.astype(BF16), 1)
            left = self.shift(left.astype(BF16), -1)
        if half == 1:
            return jnp.concatenate(
                [part(0, lower) + right.astype(F32), part(0, upper) + left.astype(F32)], axis=1
            )
        return part(0, whole) + right.astype(F32) + left.astype(F32)

    def exchange(self, pieces):
        size = self.size
        out = [None] * size
        out[0] = pieces[0]
        for by in range(1, size):
            out[size - by] = self.shift(pieces[by], by)
        return out

    def place_in_order(self, pieces):
        out = jnp.zeros((self.size,) + pieces[0].shape, pieces[0].dtype)
        for ahead in range(self.size):
            out = lax.dynamic_update_index_in_dim(out, pieces[ahead], self.owner(ahead), 0)
        return out

    def take_relative(self, stacked):
        return [
            lax.dynamic_index_in_dim(stacked, self.owner(ahead), 0, keepdims=False)
            for ahead in range(self.size)
        ]


def column_blocks(weight, size):
    width = weight.shape[1] // size
    return jnp.stack([weight[:, i * width : (i + 1) * width] for i in range(size)])


def join_columns(stacked):
    return jnp.concatenate([stacked[i] for i in range(stacked.shape[0])], axis=1)


def swap_halves(values, half):
    width = values.shape[-1]
    if width == 2 * half:
        return jnp.concatenate([values[:, half:], values[:, :half]], axis=1)
    lane = lax.broadcasted_iota(jnp.int32, values.shape, 1)
    ahead = pltpu.roll(values, width - half, 1)
    behind = pltpu.roll(values, half, 1)
    return jnp.where(lax.rem(lane, 2 * half) < half, ahead, behind)


def head_only(values, lane, head, head_size):
    inside = (lane >= head * head_size) & (lane < (head + 1) * head_size)
    return jnp.where(inside, values, jnp.zeros_like(values))


def flat(ref):
    value = ref[...]
    return value.reshape((value.shape[0] * value.shape[1], value.shape[2]))


def forward_kernel(
    head_size, lengths_ref, q_ref, k_ref, v_ref, cq_ref, sq_ref, ck_ref, sk_ref, qp_ref, kp_ref,
    out_ref, qr_ref, kr_ref, vr_ref, lse_ref,
):
    length = lengths_ref[pl.program_id(0)]
    half = head_size // 2
    queries = flat(q_ref)
    keys = flat(k_ref)
    queries = (queries * cq_ref[...] + swap_halves(queries, half) * sq_ref[...]).astype(BF16)
    keys = (keys * ck_ref[...] + swap_halves(keys, half) * sk_ref[...]).astype(BF16)
    values = flat(v_ref).astype(BF16)
    qr_ref[...] = queries.reshape(qr_ref.shape)
    kr_ref[...] = keys.reshape(kr_ref.shape)
    vr_ref[...] = values.reshape(vr_ref.shape)
    rows, width = queries.shape
    lane = lax.broadcasted_iota(jnp.int32, (rows, width), 1)
    query_pos = qp_ref[:, 0:1]
    key_pos = kp_ref[0:1, :]
    allowed = (key_pos <= query_pos) & (key_pos < length)
    total = jnp.zeros((rows, width), F32)
    scale = head_size ** (-0.5)
    for head in range(width // head_size):
        one = head_only(queries, lane, head, head_size)
        scores = contract(one, keys, 1, 1) * scale
        masked = jnp.where(allowed, scores, NEGATIVE)
        peak = jnp.max(masked, axis=-1, keepdims=True)
        weights = jnp.where(allowed, jnp.exp(masked - peak), 0.0)
        mass = jnp.sum(weights, axis=-1, keepdims=True)
        lse_ref[:, head : head + 1] = peak + jnp.log(mass)
        mixed = contract(weights.astype(BF16), values, 1, 0) / mass
        total = total + head_only(mixed, lane, head, head_size)
    out_ref[...] = total.astype(BF16).reshape(out_ref.shape)


def backward_kernel(
    head_size, lengths_ref, q_ref, k_ref, v_ref, g_ref, lse_ref, cq_ref, sq_ref, ck_ref, sk_ref, qp_ref,
    kp_ref, dq_ref, dk_ref, dv_ref, dk_sum, dv_sum,
):
    length = lengths_ref[pl.program_id(0)]
    half = head_size // 2
    queries, keys, values, grads = flat(q_ref), flat(k_ref), flat(v_ref), flat(g_ref)
    rows, width = queries.shape
    lane = lax.broadcasted_iota(jnp.int32, (rows, width), 1)
    allowed = (kp_ref[0:1, :] <= qp_ref[:, 0:1]) & (kp_ref[0:1, :] < length)
    scale = head_size ** (-0.5)

    @pl.when(pl.program_id(1) == 0)
    def start():
        dk_sum[...] = jnp.zeros_like(dk_sum)
        dv_sum[...] = jnp.zeros_like(dv_sum)

    dq = jnp.zeros((rows, width), F32)
    for head in range(width // head_size):
        one = head_only(queries, lane, head, head_size)
        grad = head_only(grads, lane, head, head_size)
        scores = contract(one, keys, 1, 1) * scale
        prob = jnp.where(
            allowed,
            jnp.exp(jnp.where(allowed, scores, NEGATIVE) - lse_ref[:, head : head + 1]),
            0.0,
        )
        grad_prob = contract(grad, values, 1, 1)
        delta = jnp.sum(prob * grad_prob, axis=-1, keepdims=True)
        grad_score = (prob * (grad_prob - delta) * scale).astype(BF16)
        dq = dq + head_only(contract(grad_score, keys, 1, 0), lane, head, head_size)
        dk_sum[...] += contract(grad_score, one, 0, 0)
        dv_sum[...] += contract(prob.astype(BF16), grad, 0, 0)
    dq = dq * cq_ref[...] - swap_halves(dq, half) * sq_ref[...]
    dq_ref[...] = dq.astype(BF16).reshape(dq_ref.shape)

    @pl.when(pl.program_id(1) == pl.num_programs(1) - 1)
    def finish():
        dk = dk_sum[...]
        dk = dk * ck_ref[...] - swap_halves(dk, half) * sk_ref[...]
        dk_ref[...] = dk.astype(BF16).reshape(dk_ref.shape)
        dv_ref[...] = dv_sum[...].astype(BF16).reshape(dv_ref.shape)


class Attention:
    def __init__(self, size, groups, slots, width, head_size, lengths, owners):
        self.size, self.groups, self.slots, self.width = size, groups, slots, width
        self.head_size = head_size
        self.lengths = lengths
        self.heads = width // head_size
        self.steps = max(1, min(size, QUERY_ROWS // slots))
        half = head_size // 2
        positions = (owners[:, None] * slots + jnp.arange(slots, dtype=jnp.int32)[None]).reshape(-1)
        freqs = THETA ** (-(jnp.arange(half, dtype=F32) * 2.0) / (2.0 * half))
        angles = positions.astype(F32)[:, None] * freqs[None, :]
        cosine, sine = jnp.cos(angles), jnp.sin(angles)
        self.cosine = jnp.tile(cosine, (1, 2 * self.heads))
        self.sine = jnp.tile(jnp.concatenate([-sine, sine], axis=1), (1, self.heads))
        self.query_pos = jnp.broadcast_to(positions[:, None], (positions.shape[0], 128))
        self.key_pos = jnp.broadcast_to(positions[None, :], (8, positions.shape[0]))
        total = size * slots
        rows = self.steps * slots
        self.grid = (groups, size // self.steps)
        self.q_spec = self.tokens(self.steps, width, 0, True)
        self.k_spec = self.tokens(size, width, 0, False)
        self.table_q = pl.BlockSpec((rows, width), lambda b, i, *_: (i, 0))
        self.table_k = pl.BlockSpec((total, width), lambda b, i, *_: (0, 0))
        self.pos_q = pl.BlockSpec((rows, 128), lambda b, i, *_: (i, 0))
        self.pos_k = pl.BlockSpec((8, total), lambda b, i, *_: (0, 0))
        self.lse = pl.BlockSpec((None, rows, self.heads), lambda b, i, *_: (b, i, 0))
        self.lse_shape = jax.ShapeDtypeStruct((groups, total, self.heads), F32)
        self.shape = jax.ShapeDtypeStruct((size, groups, slots, width), BF16)
        self.work = groups * self.heads * total * total

    def tokens(self, count, width, column, moving):
        return pl.BlockSpec(
            (count, None, self.slots, width),
            (lambda b, i, *_: (i, b, 0, column)) if moving else (lambda b, i, *_: (0, b, 0, column)),
        )

    def split(self, array):
        return array.reshape(self.size, self.groups, self.slots, -1)

    def cost(self, matmuls):
        return pl.CostEstimate(
            flops=2 * matmuls * self.work * self.head_size,
            transcendentals=self.work,
            bytes_accessed=8 * self.size * self.groups * self.slots * self.width * 2,
        )

    def forward(self, projected):
        width = self.width
        if width % 128 == 0:
            arrays = (self.split(projected),) * 3
            columns = (0, 1, 2)
        else:
            arrays = tuple(
                self.split(projected[:, i * width : (i + 1) * width]) for i in range(3)
            )
            columns = (0, 0, 0)
        return pl.pallas_call(
            functools.partial(forward_kernel, self.head_size),
            grid_spec=pltpu.PrefetchScalarGridSpec(
                num_scalar_prefetch=1,
                grid=self.grid,
                in_specs=[
                    self.tokens(self.steps, width, columns[0], True),
                    self.tokens(self.size, width, columns[1], False),
                    self.tokens(self.size, width, columns[2], False),
                    self.table_q, self.table_q, self.table_k, self.table_k, self.pos_q, self.pos_k,
                ],
                out_specs=[self.q_spec, self.q_spec, self.k_spec, self.k_spec, self.lse],
            ),
            out_shape=[self.shape] * 4 + [self.lse_shape],
            cost_estimate=self.cost(2),
            name="attention_forward",
        )(
            self.lengths, *arrays, self.cosine, self.sine, self.cosine, self.sine, self.query_pos, self.key_pos
        )

    def backward(self, queries, keys, values, grads, lse):
        total = self.size * self.slots
        return pl.pallas_call(
            functools.partial(backward_kernel, self.head_size),
            grid_spec=pltpu.PrefetchScalarGridSpec(
                num_scalar_prefetch=1,
                grid=self.grid,
                in_specs=[
                    self.q_spec, self.k_spec, self.k_spec, self.q_spec, self.lse,
                    self.table_q, self.table_q, self.table_k, self.table_k, self.pos_q, self.pos_k,
                ],
                out_specs=[self.q_spec, self.k_spec, self.k_spec],
                scratch_shapes=[pltpu.VMEM((total, self.width), F32)] * 2,
            ),
            out_shape=[self.shape] * 3,
            cost_estimate=self.cost(5),
            name="attention_backward",
        )(
            self.lengths, queries, keys, values, self.split(grads), lse,
            self.cosine, self.sine, self.cosine, self.sine, self.query_pos, self.key_pos,
        )


def body(
    inputs, cotangent, lengths, query_weight, key_weight, value_weight, mix_weight, gate_weight,
    up_weight, down_weight, attn_gain, ffn_gain,
):
    groups, slots, width = inputs.shape
    head_size = width // HEADS
    size = lax.axis_size("ctx")
    shares = lax.axis_size("dp")
    rows = groups * slots
    ring = Ring(size)
    owners = ring.owners()
    local = width // size
    hidden_local = gate_weight.shape[1] // size
    gain_one = attn_gain.astype(F32)[:, None]
    gain_two = ffn_gain.astype(F32)[:, None]

    def over_shares(value):
        return lax.all_gather(value, "dp", axis=0, tiled=True)

    def scaled(weight, gain):
        return (weight.astype(F32) * gain).astype(BF16)

    def to_columns(weights):
        blocks = jnp.concatenate([column_blocks(w, size) for w in weights], axis=2)
        got = ring.place_in_order(ring.exchange(ring.take_relative(blocks)))
        return got.reshape(-1, got.shape[2])

    attn_rows = to_columns([scaled(w, gain_one) for w in (query_weight, key_weight, value_weight)])
    attn_columns = over_shares(attn_rows)
    ffn_rows = to_columns(
        [scaled(gate_weight, gain_two), scaled(up_weight, gain_two), down_weight]
    )
    gate_columns = over_shares(ffn_rows[:, :hidden_local])
    up_columns = over_shares(ffn_rows[:, hidden_local : 2 * hidden_local])
    down_columns = over_shares(ffn_rows[:, 2 * hidden_local :])
    mix_full = lax.all_gather(mix_weight, ("dp", "ctx"), axis=0, tiled=True)

    block_in = inputs.reshape(rows, width).astype(F32)
    positions = lax.axis_index("ctx") * slots + jnp.arange(slots, dtype=jnp.int32)
    valid = (positions[None, :] < lengths[:, None]).astype(F32).reshape(rows, 1)
    normed_one, factor_one = normalize(block_in)
    one_all = jnp.concatenate(ring.gather(normed_one.astype(BF16)), axis=0)
    grad_out = cotangent.reshape(rows, width).astype(F32) * valid
    grad_all = jnp.concatenate(ring.gather(grad_out.astype(BF16)), axis=0)
    projected = contract(one_all, attn_columns, 1, 0)
    attention = Attention(size, groups, slots, local, head_size, lengths, owners)
    mixed, query_rot, key_rot, value_low, lse = attention.forward(projected)
    mixed_rows = mixed.reshape(size, rows, local)
    attended = join_columns(
        ring.place_in_order(ring.exchange([mixed_rows[r] for r in range(size)]))
    )
    residual = block_in + contract(attended, mix_full, 1, 0)

    normed_two, factor_two = normalize(residual)
    two_all = jnp.concatenate(ring.gather(normed_two.astype(BF16)), axis=0)
    gate = contract(two_all, gate_columns, 1, 0)
    up = contract(two_all, up_columns, 1, 0)
    sigma = jax.nn.sigmoid(gate)
    silu_gate = gate * sigma
    hidden = (silu_gate * up).astype(BF16)

    grad_hidden = contract(grad_all, down_columns, 1, 0)
    gate_low = (grad_hidden * up * sigma * (1.0 + gate * (1.0 - sigma))).astype(BF16)
    up_low = (grad_hidden * silu_gate).astype(BF16)

    def terms(values):
        half = width // 2

        def part(ahead, columns):
            chunk = values[ahead * rows : (ahead + 1) * rows]
            return (chunk[:, :half], chunk[:, half:], chunk)[columns]

        return part

    scaled_two = ring.scatter_sum(
        terms(contract(gate_low, gate_columns, 1, 1) + contract(up_low, up_columns, 1, 1))
    )
    dres = grad_out + factor_two * (
        scaled_two - normed_two * jnp.mean(normed_two * scaled_two, axis=-1, keepdims=True)
    )
    dres_low = dres.astype(BF16)
    branch = ring.scatter_sum(terms(contract(hidden, down_columns, 1, 1)))
    activations = (valid * (residual + branch)).astype(BF16)

    grad_mixed = contract(dres_low, mix_full, 1, 1).astype(BF16)
    grad_heads = jnp.concatenate(
        ring.exchange(ring.take_relative(column_blocks(grad_mixed, size))), axis=0
    )
    dres_all = jnp.concatenate(ring.gather(dres_low), axis=0)
    dq, dk, dv = attention.backward(query_rot, key_rot, value_low, grad_heads, lse)
    projected_grad = jnp.concatenate(
        [d.reshape(size * rows, local) for d in (dq, dk, dv)], axis=1
    )
    scaled_one = ring.scatter_sum(terms(contract(projected_grad, attn_columns, 1, 1)))
    input_grad = dres + factor_one * (
        scaled_one - normed_one * jnp.mean(normed_one * scaled_one, axis=-1, keepdims=True)
    )

    def to_rows(gradient):
        summed = lax.psum_scatter(gradient.astype(BF16), "dp", scatter_dimension=0, tiled=True)
        stacked = summed.reshape(size, summed.shape[0] // size, summed.shape[1])
        return ring.place_in_order(ring.exchange(ring.take_relative(stacked)))

    down_grad = join_columns(to_rows(contract(grad_all, hidden, 0, 0))).astype(F32)
    gate_raw = join_columns(to_rows(contract(two_all, gate_low, 0, 0))).astype(F32)
    up_raw = join_columns(to_rows(contract(two_all, up_low, 0, 0))).astype(F32)
    attn_raw = to_rows(contract(one_all, projected_grad, 0, 0))
    query_raw, key_raw, value_raw = (
        join_columns(attn_raw[:, :, i * local : (i + 1) * local]).astype(F32) for i in range(3)
    )
    mix_part = lax.psum_scatter(
        contract(mixed.reshape(size * rows, local), dres_all, 0, 0).astype(BF16),
        "dp",
        scatter_dimension=0,
        tiled=True,
    )
    mix_grad = lax.ppermute(
        mix_part,
        ("dp", "ctx"),
        [(i * size + j, j * shares + i) for i in range(shares) for j in range(size)],
    ).astype(F32)

    def row_sum(*pairs):
        return sum(jnp.sum(w.astype(F32) * g, axis=1) for w, g in pairs)

    attn_gain_grad = row_sum(
        (query_weight, query_raw), (key_weight, key_raw), (value_weight, value_raw)
    )
    ffn_gain_grad = row_sum((gate_weight, gate_raw), (up_weight, up_raw))
    return (
        activations.reshape(groups, slots, width),
        input_grad.astype(BF16).reshape(groups, slots, width),
        query_raw * gain_one,
        key_raw * gain_one,
        value_raw * gain_one,
        mix_grad,
        gate_raw * gain_two,
        up_raw * gain_two,
        down_grad,
        attn_gain_grad,
        ffn_gain_grad,
    )


def solution(mesh):
    rows = P(("dp", "ctx"), None)
    tokens = P("dp", "ctx", None)
    gains = P(("dp", "ctx"))
    return jax.shard_map(
        body,
        mesh=mesh,
        in_specs=(tokens, tokens, P("dp")) + (rows,) * 7 + (gains, gains),
        out_specs=(tokens, tokens) + (rows,) * 7 + (gains, gains),
        check_vma=False,
    )
```

time: 4460 us -> 881 us (0.20)
  waiting for transfers between devices: 3600 us -> 440 us
  matrix products: 457 us -> 117 us
  blocking collectives: 209 us -> 0 us
  starting transfers between devices: 1.19 us -> 169 us
  local copies, waits for them, and re-layouts: 122 us -> 61.2 us
    reduce_scatter x5, waiting for transfers between devices: 2680 us -> 10.6 us  [the longest x4 10.6 us: to_rows(): lax.psum_scatter(gradient.astype(BF16), 'dp', scatter_dimension=0, tiled=...]
    all_gather x15 -> x5, waiting for transfers between devices: 919 us -> 0.03 us  [the longest x1 0.02 us: body(): mix_full = lax.all_gather(mix_weight, ('dp', 'ctx'), axis=0, tiled=True)]
    ppermute x0 -> x113, waiting for transfers between devices: none -> 428 us  [the longest x112 428 us: shift(): return lax.ppermute(value, 'ctx', pairs)]
    dot_general x47 -> x15, matrix products: 457 us -> 117 us  [contract(): lax.dot_general(left, right, (((left_dim,), (right_dim,)), ((), ())), pre...]
    ppermute x0 -> x113, starting transfers between devices: none -> 168 us  [the longest x112 166 us: shift(): return lax.ppermute(value, 'ctx', pairs)]
    all_gather x4 -> x0, blocking collectives: 124 us -> none  [the longest x2 62.7 us: body(): lax.all_gather(log_sent.astype(jnp.bfloat16), 'ctx', axis=1, tiled=True)]
    unnamed x2 -> x0, blocking collectives: 84.5 us -> none
    another operation x26 -> x16, local copies, waits for them, and re-layouts: 54.5 us -> 3.59 us  [the longest x2 1.05 us: __init__(): jnp.tile(jnp.concatenate([-sine, sine], axis=1), (1, self.heads))]
  transfers between devices with their start and end apart: 20 -> 123, of which waited for: 16 -> 67; matrix products, arithmetic and copies ran while one was open for 14% -> 17% of each run, Pallas kernels for 0% -> 3%
where the time goes in v1:
time: 881 us; the launch traced here: 873 us
  waiting for transfers between devices  440 us (50%)
  starting transfers between devices  169 us (19%)
  matrix products  117 us (13%)
  local copies, waits for them, and re-layouts  61.2 us (7%)
  between operations  39.1 us (4%)
  other arithmetic  24.5 us (3%)
  Pallas kernels  23.6 us (3%)
    ppermute x112, waiting for transfers between devices, shift(): return lax.ppermute(value, 'ctx', pairs)  428 us
    ppermute x112, starting transfers between devices, shift(): return lax.ppermute(value, 'ctx', pairs)  166 us
    dot_general x15, matrix products, contract(): lax.dot_general(left, right, (((left_dim,), (right_dim,)), ((), ())), pre...  117 us
    unnamed x197, local copies, waits for them, and re-layouts  33.7 us
  transfers between devices with their start and end apart: 123, of which 67 were waited for; matrix products, arithmetic and copies ran while one was open for 17% of the time, Pallas kernels for 3%

profile of v1, /device:TPU:0, one launch (start us, length us, event | category | flops | bytes accessed | tf_op | source)
XLA Modules:
  0.0 873.4 jit_solution(1621010356249602395)
XLA Ops:
  43.6 10.4 %collective-permute-done.9 = bf16[64,768]{1,0:T(8,128)(2,1)S(1)} collective-permute-done((bf16[64,768]{1,0:T(8,128)(2,1)S(1)}, bf16[64,768]{1,0:T(8,128)(2,1)S(1)}, u32[]{:S(2)}, u32[]{:S(2)}) %collective-permute-start.9) | collective-permute-done | bytes 98336 | tf_op jit(solution)/shard_map/ppermute | solution.py:48
  54.0 6.4 collective-permute-done.10
  81.9 55.9 %collective-permute-done.31 = bf16[64,3072]{1,0:T(8,128)(2,1)S(1)} collective-permute-done((bf16[64,3072]{1,0:T(8,128)(2,1)S(1)}, bf16[64,3072]{1,0:T(8,128)(2,1)S(1)}, u32[]{:S(2)}, u32[]{:S(2)}) %collective-permute-start.31) | collective-permute-done | bytes 393248 | tf_op jit(solution)/shard_map/ppermute | solution.py:48
  137.9 11.1 %collective-permute-done.32 = bf16[64,3072]{1,0:T(8,128)(2,1)S(1)} collective-permute-done((bf16[64,3072]{1,0:T(8,128)(2,1)S(1)}, bf16[64,3072]{1,0:T(8,128)(2,1)S(1)}, u32[]{:S(2)}, u32[]{:S(2)}) %collective-permute-start.32) | collective-permute-done | bytes 393248 | tf_op jit(solution)/shard_map/ppermute | solution.py:48
  155.4 6.2 collective-permute-start.3
  166.3 18.0 %collective-permute-done.3 = bf16[128,2048]{1,0:T(8,128)(2,1)S(1)} collective-permute-done((bf16[128,2048]{1,0:T(8,128)(2,1)S(1)}, bf16[128,2048]{1,0:T(8,128)(2,1)S(1)}, u32[]{:S(2)}, u32[]{:S(2)}) %collective-permute-start.3) | collective-permute-done | bytes 524320 | tf_op jit(solution)/shard_map/ppermute | solution.py:48
  195.1 18.4 %collective-permute-done.4 = bf16[128,2048]{1,0:T(8,128)(2,1)} collective-permute-done((bf16[128,2048]{1,0:T(8,128)(2,1)S(1)}, bf16[128,2048]{1,0:T(8,128)(2,1)}, u32[]{:S(2)}, u32[]{:S(2)}) %collective-permute-start.4) | collective-permute-done | bytes 524320 | tf_op jit(solution)/shard_map/ppermute | solution.py:48
  222.6 6.0 collective-permute-done.5
  233.0 6.8 collective-permute-done.49
  246.1 12.2 %collective-permute-done.7 = bf16[64,2048]{1,0:T(8,128)(2,1)S(1)} collective-permute-done((bf16[64,2048]{1,0:T(8,128)(2,1)S(1)}, bf16[64,2048]{1,0:T(8,128)(2,1)S(1)}, u32[]{:S(2)}, u32[]{:S(2)}) %collective-permute-start.7) | collective-permute-done | bytes 262176 | tf_op jit(solution)/shard_map/ppermute | solution.py:48
  263.7 8.3 fusion.51
  273.5 10.8 %attention_forward.1 = (bf16[8,2,64,256]{3,2,1,0:T(8,128)(2,1)}, bf16[8,2,64,256]{3,2,1,0:T(8,128)(2,1)}, bf16[8,2,64,256]{3,2,1,0:T(8,128)(2,1)}, bf16[8,2,64,256]{3,2,1,0:T(8,128)(2,1)}, f32[2,512,4]{2,1,0:T(8,128)}) custom-call(s32[2]{0:T(128)} %lengths_ref.3, f32[8,2,64,768]{3,2,1,0:T(8,128)} %bitcast.704, f32[8,2,64,768]{3,2,1,0:T(8,128)} %bitcast.705, ...), custom_call_target="tpu_custom_call" | custom-call | flops 536870912 | bytes 4194304 | tf_op jit(solution)/shard_map/attention_forward/pallas_call | solution.py:276
  305.0 5.6 collective-permute-done.18
  336.3 5.6 collective-permute-done.51
  343.6 6.8 collective-permute-done.26
  372.9 9.9 %fusion.53 = f32[1024,1024]{1,0:T(8,128)} fusion(bf16[1024,2048]{1,0:T(8,128)(2,1)} %constant_dynamic-update-slice_fusion.41, bf16[2048,1024]{1,0:T(8,128)(2,1)} %all-gather.12.cloned.1.call-done), kind=kOutput, calls=%fused_computation.496 | convolution fusion | flops 4294967296 | bytes 12582912 | tf_op jit(solution)/shard_map/dot_general | solution.py:25
  382.8 9.9 %fusion.52 = f32[1024,1024]{1,0:T(8,128)} fusion(bf16[1024,2048]{1,0:T(8,128)(2,1)} %constant_dynamic-update-slice_fusion.41, bf16[2048,1024]{1,0:T(8,128)(2,1)} %all-gather.10.cloned.1.call-done), kind=kOutput, calls=%fused_computation.495 | convolution fusion | flops 4294967296 | bytes 12582912 | tf_op jit(solution)/shard_map/dot_general | solution.py:25
  392.7 14.0 %multiply_convert_fusion = (bf16[1024,1024]{1,0:T(8,128)(2,1)}, bf16[1024,1024]{1,0:T(8,128)(2,1)S(1)}, bf16[1024,1024]{1,0:T(8,128)(2,1)}) fusion(f32[1024,1024]{1,0:T(8,128)} %fusion.52, f32[1024,1024]{1,0:T(8,128)} %fusion.53, bf16[1024,2048]{1,0:T(8,128)(2,1)} %copy-done.22, bf16[2048,1024]{1,0:T(8,128)(2,1)} %all-gather.14.cloned.1.call-done), kind=kOutput, calls=%fused_computation | convolution fusion | flops 4310695936 | bytes 23068672 | tf_op jit(solution)/shard_map/dot_general | solution.py:25
  406.7 7.1 fusion.54
  413.8 7.7 fusion.48
  423.7 7.0 fusion.49
  440.4 10.9 %collective-permute-done.54 = bf16[128,2048]{1,0:T(8,128)(2,1)S(1)} collective-permute-done((bf16[128,2048]{1,0:T(8,128)(2,1)S(1)}, bf16[128,2048]{1,0:T(8,128)(2,1)S(1)}, u32[]{:S(2)}, u32[]{:S(2)}) %collective-permute-start.54) | collective-permute-done | bytes 524320 | tf_op jit(solution)/shard_map/ppermute | solution.py:48
  453.6 7.8 collective-permute-done.38
  461.8 5.9 collective-permute-done.55
  469.4 9.6 %collective-permute-done.39 = bf16[128,2048]{1,0:T(8,128)(2,1)S(1)} collective-permute-done((bf16[128,2048]{1,0:T(8,128)(2,1)S(1)}, bf16[128,2048]{1,0:T(8,128)(2,1)S(1)}, u32[]{:S(2)}, u32[]{:S(2)}) %collective-permute-start.39) | collective-permute-done | bytes 524320 | tf_op jit(solution)/shard_map/ppermute | solution.py:48
  484.3 7.0 collective-permute-done.43
  498.7 9.5 %collective-permute-done.44 = bf16[128,2048]{1,0:T(8,128)(2,1)S(1)} collective-permute-done((bf16[128,2048]{1,0:T(8,128)(2,1)S(1)}, bf16[128,2048]{1,0:T(8,128)(2,1)S(1)}, u32[]{:S(2)}, u32[]{:S(2)}) %collective-permute-start.44) | collective-permute-done | bytes 524320 | tf_op jit(solution)/shard_map/ppermute | solution.py:48
  512.5 11.8 %collective-permute-done.86 = bf16[128,2048]{1,0:T(8,128)(2,1)S(1)} collective-permute-done((bf16[128,2048]{1,0:T(8,128)(2,1)S(1)}, bf16[128,2048]{1,0:T(8,128)(2,1)S(1)}, u32[]{:S(2)}, u32[]{:S(2)}) %collective-permute-start.86) | collective-permute-done | bytes 524320 | tf_op jit(solution)/shard_map/ppermute | solution.py:48
  526.4 8.3 collective-permute-done.87
  554.9 9.5 %convolution_convert_fusion = bf16[2048,1024]{1,0:T(8,128)(2,1)} fusion(bf16[1024,2048]{1,0:T(8,128)(2,1)} %copy-done.22, bf16[1024,1024]{1,0:T(8,128)(2,1)} %get-tuple-element.41), kind=kOutput, calls=%fused_computation.6 | convolution fusion | flops 4297064448 | bytes 10485760 | tf_op jit(solution)/shard_map/dot_general | solution.py:25
  564.5 9.6 %convolution_convert_fusion.2 = bf16[2048,1024]{1,0:T(8,128)(2,1)} fusion(bf16[1024,2048]{1,0:T(8,128)(2,1)} %constant_dynamic-update-slice_fusion.41, bf16[1024,1024]{1,0:T(8,128)(2,1)} %copy-done.38), kind=kOutput, calls=%fused_computation.8 | convolution fusion | flops 4297064448 | bytes 10485760 | tf_op jit(solution)/shard_map/dot_general | solution.py:25
  574.3 9.4 %convolution_convert_fusion.1 = bf16[2048,1024]{1,0:T(8,128)(2,1)} fusion(bf16[1024,2048]{1,0:T(8,128)(2,1)} %constant_dynamic-update-slice_fusion.41, bf16[1024,1024]{1,0:T(8,128)(2,1)} %get-tuple-element.39), kind=kOutput, calls=%fused_computation.7 | convolution fusion | flops 4297064448 | bytes 10485760 | tf_op jit(solution)/shard_map/dot_general | solution.py:25
  583.8 6.3 convolution_convert_fusion.5
  615.5 12.8 %attention_backward.1 = (bf16[8,2,64,256]{3,2,1,0:T(8,128)(2,1)}, bf16[8,2,64,256]{3,2,1,0:T(8,128)(2,1)}, bf16[8,2,64,256]{3,2,1,0:T(8,128)(2,1)}) custom-call(s32[2]{0:T(128)} %lengths_ref.3, bf16[8,2,64,256]{3,2,1,0:T(8,128)(2,1)} %get-tuple-element.20.q_ref, bf16[8,2,64,256]{3,2,1,0:T(8,128)(2,1)} %get-tuple-element.21.k_ref, ...), custom_call_target="tpu_custom_call" | custom-call | flops 1342177280 | bytes 4194304 | tf_op jit(solution)/shard_map/attention_backward/pallas_call | solution.py:298
  628.3 5.9 fusion.50
  644.4 8.5 collective-permute-done.69
  655.6 6.7 collective-permute-done.70
  665.8 11.8 %collective-permute-done.74 = bf16[128,2048]{1,0:T(8,128)(2,1)S(1)} collective-permute-done((bf16[128,2048]{1,0:T(8,128)(2,1)S(1)}, bf16[128,2048]{1,0:T(8,128)(2,1)S(1)}, u32[]{:S(2)}, u32[]{:S(2)}) %collective-permute-start.74) | collective-permute-done | bytes 524320 | tf_op jit(solution)/shard_map/ppermute | solution.py:48
  695.2 10.9 %collective-permute-start.112 = (bf16[64,1024]{1,0:T(8,128)(2,1)S(1)}, bf16[64,1024]{1,0:T(8,128)(2,1)S(1)}, u32[]{:S(2)}, u32[]{:S(2)}) collective-permute-start(bf16[64,1024]{1,0:T(8,128)(2,1)S(1)} %get-tuple-element.75), channel_id=1, source_target_pairs={{0,2},{2,4},{4,6},{6,7},{7,5},{5,3},{3,1},{1,0},{8,10},{10,12},{12... | collective-permute-start | bytes 393224 | tf_op jit(solution)/shard_map/ppermute | solution.py:48
  715.4 10.6 %reduce-scatter.12.cloned.1.call-done = bf16[512,1024]{1,0:T(8,128)(2,1)} async-done(((bf16[2048,1024]{1,0:T(8,128)(2,1)}), bf16[512,1024]{1,0:T(8,128)(2,1)}) %reduce-scatter.12.cloned.1.call-update) | async-done | bytes 1048592 | tf_op jit(solution)/shard_map/reduce_scatter | solution.py:418
  730.8 5.5 collective-permute-done.107
  736.9 6.1 collective-permute-done.108
  781.4 6.6 collective-permute-start.96
  791.7 6.3 collective-permute-done.97
  811.3 9.7 %collective-permute-done.100 = bf16[64,1024]{1,0:T(8,128)(2,1)S(1)} collective-permute-done((bf16[64,1024]{1,0:T(8,128)(2,1)S(1)}, bf16[64,1024]{1,0:T(8,128)(2,1)S(1)}, u32[]{:S(2)}, u32[]{:S(2)}) %collective-permute-start.100) | collective-permute-done | bytes 131104 | tf_op jit(solution)/shard_map/ppermute | solution.py:48
  821.1 6.8 collective-permute-done.101
  841.4 8.8 %collective-permute-done.77 = bf16[64,768]{1,0:T(8,128)(2,1)S(1)} collective-permute-done((bf16[64,768]{1,0:T(8,128)(2,1)S(1)}, bf16[64,768]{1,0:T(8,128)(2,1)S(1)}, u32[]{:S(2)}, u32[]{:S(2)}) %collective-permute-start.77) | collective-permute-done | bytes 98336 | tf_op jit(solution)/shard_map/ppermute | solution.py:48
  850.2 6.4 collective-permute-done.78
  (580 shorter events, 361.4 us)
Async XLA Ops:
  7.2 256.5 %all-gather.6.cloned.1.call-start = ((), (), s32[]{:S(2)}) async-start(), calls=%async_computation.5 | async-start | bytes 3932160 | tf_op jit(solution)/shard_map/all_gather | solution.py:336
  36.5 24.0 %collective-permute-start.14 = (bf16[64,768]{1,0:T(8,128)(2,1)S(1)}, bf16[64,768]{1,0:T(8,128)(2,1)S(1)}, u32[]{:S(2)}, u32[]{:S(2)}) collective-permute-start(bf16[64,768]{1,0:T(8,128)(2,1)S(1)} %get-tuple-element.131), channel_id=1, source_target_pairs={{0,2},{2,4},{4,6},{6,7},{7,5},{5,3},{3,1},{1,0},{8,10},{10,12},{12... | collective-permute-start | bytes 294920 | tf_op jit(solution)/shard_map/ppermute | solution.py:48
  36.6 23.9 %collective-permute-start.13 = (bf16[64,768]{1,0:T(8,128)(2,1)S(1)}, bf16[64,768]{1,0:T(8,128)(2,1)S(1)}, u32[]{:S(2)}, u32[]{:S(2)}) collective-permute-start(bf16[64,768]{1,0:T(8,128)(2,1)S(1)} %get-tuple-element.132), channel_id=1, source_target_pairs={{0,4},{2,6},{4,7},{6,5},{7,3},{5,1},{3,0},{1,2},{8,12},{10,14},{12... | collective-permute-start | bytes 294920 | tf_op jit(solution)/shard_map/ppermute | solution.py:48
  39.6 20.9 %collective-permute-start.12 = (bf16[64,768]{1,0:T(8,128)(2,1)S(1)}, bf16[64,768]{1,0:T(8,128)(2,1)S(1)}, u32[]{:S(2)}, u32[]{:S(2)}) collective-permute-start(bf16[64,768]{1,0:T(8,128)(2,1)S(1)} %get-tuple-element.133), channel_id=1, source_target_pairs={{0,6},{2,7},{4,5},{6,3},{7,1},{5,0},{3,2},{1,4},{8,14},{10,15},{12... | collective-permute-start | bytes 294920 | tf_op jit(solution)/shard_map/ppermute | solution.py:48
  61.5 256.0 %all-gather.8.cloned.1.call-start = ((), (), s32[]{:S(2)}) async-start(), calls=%async_computation.6 | async-start | bytes 8650752 | tf_op jit(solution)/shard_map/all_gather | solution.py:354
  62.2 310.6 %all-gather.12.cloned.1.call-start = ((), (), s32[]{:S(2)}) async-start(), calls=%async_computation.8 | async-start | bytes 5242880 | tf_op jit(solution)/shard_map/all_gather | solution.py:336
  71.7 79.9 %collective-permute-start.36 = (bf16[64,3072]{1,0:T(8,128)(2,1)S(1)}, bf16[64,3072]{1,0:T(8,128)(2,1)S(1)}, u32[]{:S(2)}, u32[]{:S(2)}) collective-permute-start(bf16[64,3072]{1,0:T(8,128)(2,1)S(1)} %get-tuple-element.61), channel_id=1, source_target_pairs={{0,2},{2,4},{4,6},{6,7},{7,5},{5,3},{3,1},{1,0},{8,10},{10,12},{12... | collective-permute-start | bytes 1179656 | tf_op jit(solution)/shard_map/ppermute | solution.py:48
  73.7 77.9 %collective-permute-start.35 = (bf16[64,3072]{1,0:T(8,128)(2,1)S(1)}, bf16[64,3072]{1,0:T(8,128)(2,1)S(1)}, u32[]{:S(2)}, u32[]{:S(2)}) collective-permute-start(bf16[64,3072]{1,0:T(8,128)(2,1)S(1)} %get-tuple-element.62), channel_id=1, source_target_pairs={{0,4},{2,6},{4,7},{6,5},{7,3},{5,1},{3,0},{1,2},{8,12},{10,14},{12... | collective-permute-start | bytes 1179656 | tf_op jit(solution)/shard_map/ppermute | solution.py:48
  73.7 77.8 %collective-permute-start.34 = (bf16[64,3072]{1,0:T(8,128)(2,1)S(1)}, bf16[64,3072]{1,0:T(8,128)(2,1)S(1)}, u32[]{:S(2)}, u32[]{:S(2)}) collective-permute-start(bf16[64,3072]{1,0:T(8,128)(2,1)S(1)} %get-tuple-element.63), channel_id=1, source_target_pairs={{0,6},{2,7},{4,5},{6,3},{7,1},{5,0},{3,2},{1,4},{8,14},{10,15},{12... | collective-permute-start | bytes 1179656 | tf_op jit(solution)/shard_map/ppermute | solution.py:48
  76.1 72.9 %collective-permute-start.33 = (bf16[64,3072]{1,0:T(8,128)(2,1)S(1)}, bf16[64,3072]{1,0:T(8,128)(2,1)S(1)}, u32[]{:S(2)}, u32[]{:S(2)}) collective-permute-start(bf16[64,3072]{1,0:T(8,128)(2,1)S(1)} %get-tuple-element.64), channel_id=1, source_target_pairs={{0,7},{2,5},{4,3},{6,1},{7,0},{5,2},{3,4},{1,6},{8,15},{10,13},{12... | collective-permute-start | bytes 1179656 | tf_op jit(solution)/shard_map/ppermute | solution.py:48
  80.8 57.0 %collective-permute-start.31 = (bf16[64,3072]{1,0:T(8,128)(2,1)S(1)}, bf16[64,3072]{1,0:T(8,128)(2,1)S(1)}, u32[]{:S(2)}, u32[]{:S(2)}) collective-permute-start(bf16[64,3072]{1,0:T(8,128)(2,1)S(1)} %get-tuple-element.66), channel_id=1, source_target_pairs={{0,3},{2,1},{4,0},{6,2},{7,4},{5,6},{3,7},{1,5},{8,11},{10,9},{12,... | collective-permute-start | bytes 1179656 | tf_op jit(solution)/shard_map/ppermute | solution.py:48
  153.5 229.3 %all-gather.10.cloned.1.call-start = ((), (), s32[]{:S(2)}) async-start(), calls=%async_computation.7 | async-start | bytes 5242880 | tf_op jit(solution)/shard_map/all_gather | solution.py:336
  154.0 238.7 %all-gather.14.cloned.1.call-start = ((), (), s32[]{:S(2)}) async-start(), calls=%async_computation.9 | async-start | bytes 5242880 | tf_op jit(solution)/shard_map/all_gather | solution.py:336
  155.4 28.9 %collective-permute-start.3 = (bf16[128,2048]{1,0:T(8,128)(2,1)S(1)}, bf16[128,2048]{1,0:T(8,128)(2,1)S(1)}, u32[]{:S(2)}, u32[]{:S(2)}) collective-permute-start(bf16[128,2048]{1,0:T(8,128)(2,1)S(1)} %get-tuple-element.177), channel_id=1, source_target_pairs={{0,2},{2,4},{4,6},{6,7},{7,5},{5,3},{3,1},{1,0},{8,10},{10,12},{12... | collective-permute-start | bytes 1572872 | tf_op jit(solution)/shard_map/ppermute | solution.py:48
  161.6 32.1 %collective-permute-start = (bf16[128,2048]{1,0:T(8,128)(2,1)S(1)}, bf16[128,2048]{1,0:T(8,128)(2,1)S(1)}, u32[]{:S(2)}, u32[]{:S(2)}) collective-permute-start(bf16[128,2048]{1,0:T(8,128)(2,1)S(1)} %get-tuple-element.177), channel_id=1, source_target_pairs={{0,1},{2,0},{4,2},{6,4},{7,6},{5,7},{3,5},{1,3},{8,9},{10,8},{12,1... | collective-permute-start | bytes 1572872 | tf_op jit(solution)/shard_map/ppermute | solution.py:48
  162.9 53.4 %collective-permute-start.48 = (bf16[128,2048]{1,0:T(8,128)(2,1)}, bf16[128,2048]{1,0:T(8,128)(2,1)S(1)}, u32[]{:S(2)}, u32[]{:S(2)}) collective-permute-start(bf16[128,2048]{1,0:T(8,128)(2,1)} %get-tuple-element.181), channel_id=1, source_target_pairs={{0,2},{2,4},{4,6},{6,7},{7,5},{5,3},{3,1},{1,0},{8,10},{10,12},{12... | collective-permute-start | bytes 1572872 | tf_op jit(solution)/shard_map/ppermute | solution.py:48
  164.9 52.8 %collective-permute-start.45 = (bf16[128,2048]{1,0:T(8,128)(2,1)}, bf16[128,2048]{1,0:T(8,128)(2,1)}, u32[]{:S(2)}, u32[]{:S(2)}) collective-permute-start(bf16[128,2048]{1,0:T(8,128)(2,1)} %get-tuple-element.181), channel_id=1, source_target_pairs={{0,1},{2,0},{4,2},{6,4},{7,6},{5,7},{3,5},{1,3},{8,9},{10,8},{12,1... | collective-permute-start | bytes 1572872 | tf_op jit(solution)/shard_map/ppermute | solution.py:48
  184.3 29.1 %collective-permute-start.4 = (bf16[128,2048]{1,0:T(8,128)(2,1)S(1)}, bf16[128,2048]{1,0:T(8,128)(2,1)}, u32[]{:S(2)}, u32[]{:S(2)}) collective-permute-start(bf16[128,2048]{1,0:T(8,128)(2,1)S(1)} %collective-permute-done.3), channel_id=1, source_target_pairs={{0,2},{2,4},{4,6},{6,7},{7,5},{5,3},{3,1},{1,0},{8,10},{10,12},{12... | collective-permute-start | bytes 1572872 | tf_op jit(solution)/shard_map/ppermute | solution.py:48
  193.7 24.7 %collective-permute-start.1 = (bf16[128,2048]{1,0:T(8,128)(2,1)S(1)}, bf16[128,2048]{1,0:T(8,128)(2,1)}, u32[]{:S(2)}, u32[]{:S(2)}) collective-permute-start(bf16[128,2048]{1,0:T(8,128)(2,1)S(1)} %collective-permute-done), channel_id=1, source_target_pairs={{0,1},{2,0},{4,2},{6,4},{7,6},{5,7},{3,5},{1,3},{8,9},{10,8},{12,1... | collective-permute-start | bytes 1572872 | tf_op jit(solution)/shard_map/ppermute | solution.py:48
  216.4 23.4 %collective-permute-start.49 = (bf16[128,2048]{1,0:T(8,128)(2,1)S(1)}, bf16[128,2048]{1,0:T(8,128)(2,1)}, u32[]{:S(2)}, u32[]{:S(2)}) collective-permute-start(bf16[128,2048]{1,0:T(8,128)(2,1)S(1)} %collective-permute-done.48), channel_id=1, source_target_pairs={{0,2},{2,4},{4,6},{6,7},{7,5},{5,3},{3,1},{1,0},{8,10},{10,12},{12... | collective-permute-start | bytes 1572872 | tf_op jit(solution)/shard_map/ppermute | solution.py:48
  217.7 24.7 %collective-permute-start.46 = (bf16[128,2048]{1,0:T(8,128)(2,1)}, bf16[128,2048]{1,0:T(8,128)(2,1)}, u32[]{:S(2)}, u32[]{:S(2)}) collective-permute-start(bf16[128,2048]{1,0:T(8,128)(2,1)} %collective-permute-done.45), channel_id=1, source_target_pairs={{0,1},{2,0},{4,2},{6,4},{7,6},{5,7},{3,5},{1,3},{8,9},{10,8},{12,1... | collective-permute-start | bytes 1572872 | tf_op jit(solution)/shard_map/ppermute | solution.py:48
  218.4 23.9 %collective-permute-start.2 = (bf16[128,2048]{1,0:T(8,128)(2,1)}, bf16[128,2048]{1,0:T(8,128)(2,1)S(1)}, u32[]{:S(2)}, u32[]{:S(2)}) collective-permute-start(bf16[128,2048]{1,0:T(8,128)(2,1)} %collective-permute-done.1), channel_id=1, source_target_pairs={{0,1},{2,0},{4,2},{6,4},{7,6},{5,7},{3,5},{1,3},{8,9},{10,8},{12,1... | collective-permute-start | bytes 1572872 | tf_op jit(solution)/shard_map/ppermute | solution.py:48
  220.7 468.0 %reduce-scatter.8.cloned.1.call-start = ((), (), s32[]{:S(2)}) async-start(), calls=%async_computation.11 | async-start | bytes 1310720 | tf_op jit(solution)/shard_map/reduce_scatter | solution.py:429
  239.8 84.8 %collective-permute-start.50 = (bf16[128,2048]{1,0:T(8,128)(2,1)}, bf16[128,2048]{1,0:T(8,128)(2,1)S(1)}, u32[]{:S(2)}, u32[]{:S(2)}) collective-permute-start(bf16[128,2048]{1,0:T(8,128)(2,1)} %collective-permute-done.49), channel_id=1, source_target_pairs={{0,2},{2,4},{4,6},{6,7},{7,5},{5,3},{3,1},{1,0},{8,10},{10,12},{12... | collective-permute-start | bytes 1572872 | tf_op jit(solution)/shard_map/ppermute | solution.py:48
  242.4 86.2 %collective-permute-start.47 = (bf16[128,2048]{1,0:T(8,128)(2,1)}, bf16[128,2048]{1,0:T(8,128)(2,1)}, u32[]{:S(2)}, u32[]{:S(2)}) collective-permute-start(bf16[128,2048]{1,0:T(8,128)(2,1)} %collective-permute-done.46), channel_id=1, source_target_pairs={{0,1},{2,0},{4,2},{6,4},{7,6},{5,7},{3,5},{1,3},{8,9},{10,8},{12,1... | collective-permute-start | bytes 1572872 | tf_op jit(solution)/shard_map/ppermute | solution.py:48
  285.3 32.0 %collective-permute-start.20 = (bf16[128,256]{1,0:T(8,128)(2,1)S(1)}, bf16[128,256]{1,0:T(8,128)(2,1)S(1)}, u32[]{:S(2)}, u32[]{:S(2)}) collective-permute-start(bf16[128,256]{1,0:T(8,128)(2,1)S(1)} %bitcast.722), channel_id=1, source_target_pairs={{0,4},{2,6},{4,7},{6,5},{7,3},{5,1},{3,0},{1,2},{8,12},{10,14},{12... | collective-permute-start | bytes 196616 | tf_op jit(solution)/shard_map/ppermute | solution.py:48
  286.4 30.9 %collective-permute-start.21 = (bf16[128,256]{1,0:T(8,128)(2,1)S(1)}, bf16[128,256]{1,0:T(8,128)(2,1)S(1)}, u32[]{:S(2)}, u32[]{:S(2)}) collective-permute-start(bf16[128,256]{1,0:T(8,128)(2,1)S(1)} %bitcast.721), channel_id=1, source_target_pairs={{0,2},{2,4},{4,6},{6,7},{7,5},{5,3},{3,1},{1,0},{8,10},{10,12},{12... | collective-permute-start | bytes 196616 | tf_op jit(solution)/shard_map/ppermute | solution.py:48
  433.2 28.6 %collective-permute-start.58 = (bf16[128,2048]{1,0:T(8,128)(2,1)S(1)}, bf16[128,2048]{1,0:T(8,128)(2,1)S(1)}, u32[]{:S(2)}, u32[]{:S(2)}) collective-permute-start(bf16[128,2048]{1,0:T(8,128)(2,1)S(1)} %pad_maximum_fusion.8), channel_id=1, source_target_pairs={{0,1},{2,0},{4,2},{6,4},{7,6},{5,7},{3,5},{1,3},{8,9},{10,8},{12,1... | collective-permute-start | bytes 1572872 | tf_op jit(solution)/shard_map/ppermute | solution.py:48
  440.3 21.0 %collective-permute-start.38 = (bf16[128,2048]{1,0:T(8,128)(2,1)S(1)}, bf16[128,2048]{1,0:T(8,128)(2,1)S(1)}, u32[]{:S(2)}, u32[]{:S(2)}) collective-permute-start(bf16[128,2048]{1,0:T(8,128)(2,1)S(1)} %pad_maximum_fusion.5), channel_id=1, source_target_pairs={{0,2},{2,4},{4,6},{6,7},{7,5},{5,3},{3,1},{1,0},{8,10},{10,12},{12... | collective-permute-start | bytes 1572872 | tf_op jit(solution)/shard_map/ppermute | solution.py:48
  554.9 138.8 %reduce-scatter.14.cloned.1.call-start = ((), (), s32[]{:S(2)}) async-start(), calls=%async_computation.14 | async-start | bytes 5242880 | tf_op jit(solution)/shard_map/reduce_scatter | solution.py:418
  564.4 148.7 %reduce-scatter.10.cloned.1.call-start = ((), (), s32[]{:S(2)}) async-start(), calls=%async_computation.12 | async-start | bytes 5242880 | tf_op jit(solution)/shard_map/reduce_scatter | solution.py:418
  574.1 151.9 %reduce-scatter.12.cloned.1.call-start = ((), (), s32[]{:S(2)}) async-start(), calls=%async_computation.13 | async-start | bytes 5242880 | tf_op jit(solution)/shard_map/reduce_scatter | solution.py:418
  583.8 247.4 %reduce-scatter.6.cloned.1.call-start = ((), (), s32[]{:S(2)}) async-start(), calls=%async_computation.10 | async-start | bytes 3932160 | tf_op jit(solution)/shard_map/reduce_scatter | solution.py:418
  590.4 24.3 %collective-permute-start.67 = (bf16[128,256]{1,0:T(8,128)(2,1)S(1)}, bf16[128,256]{1,0:T(8,128)(2,1)S(1)}, u32[]{:S(2)}, u32[]{:S(2)}) collective-permute-start(bf16[128,256]{1,0:T(8,128)(2,1)S(1)} %get-tuple-element.139), channel_id=1, source_target_pairs={{0,2},{2,4},{4,6},{6,7},{7,5},{5,3},{3,1},{1,0},{8,10},{10,12},{12... | collective-permute-start | bytes 196616 | tf_op jit(solution)/shard_map/ppermute | solution.py:48
  591.5 23.1 %collective-permute-start.66 = (bf16[128,256]{1,0:T(8,128)(2,1)S(1)}, bf16[128,256]{1,0:T(8,128)(2,1)S(1)}, u32[]{:S(2)}, u32[]{:S(2)}) collective-permute-start(bf16[128,256]{1,0:T(8,128)(2,1)S(1)} %get-tuple-element.140), channel_id=1, source_target_pairs={{0,4},{2,6},{4,7},{6,5},{7,3},{5,1},{3,0},{1,2},{8,12},{10,14},{12... | collective-permute-start | bytes 196616 | tf_op jit(solution)/shard_map/ppermute | solution.py:48
  594.7 20.0 %collective-permute-start.65 = (bf16[128,256]{1,0:T(8,128)(2,1)S(1)}, bf16[128,256]{1,0:T(8,128)(2,1)S(1)}, u32[]{:S(2)}, u32[]{:S(2)}) collective-permute-start(bf16[128,256]{1,0:T(8,128)(2,1)S(1)} %get-tuple-element.141), channel_id=1, source_target_pairs={{0,6},{2,7},{4,5},{6,3},{7,1},{5,0},{3,2},{1,4},{8,14},{10,15},{12... | collective-permute-start | bytes 196616 | tf_op jit(solution)/shard_map/ppermute | solution.py:48
  663.8 19.1 %collective-permute-start.71 = (bf16[128,2048]{1,0:T(8,128)(2,1)}, bf16[128,2048]{1,0:T(8,128)(2,1)S(1)}, u32[]{:S(2)}, u32[]{:S(2)}) collective-permute-start(bf16[128,2048]{1,0:T(8,128)(2,1)} %get-tuple-element.31), channel_id=1, source_target_pairs={{0,2},{2,4},{4,6},{6,7},{7,5},{5,3},{3,1},{1,0},{8,10},{10,12},{12... | collective-permute-start | bytes 1572872 | tf_op jit(solution)/shard_map/ppermute | solution.py:48
  695.2 57.4 %collective-permute-start.112 = (bf16[64,1024]{1,0:T(8,128)(2,1)S(1)}, bf16[64,1024]{1,0:T(8,128)(2,1)S(1)}, u32[]{:S(2)}, u32[]{:S(2)}) collective-permute-start(bf16[64,1024]{1,0:T(8,128)(2,1)S(1)} %get-tuple-element.75), channel_id=1, source_target_pairs={{0,2},{2,4},{4,6},{6,7},{7,5},{5,3},{3,1},{1,0},{8,10},{10,12},{12... | collective-permute-start | bytes 393224 | tf_op jit(solution)/shard_map/ppermute | solution.py:48
  706.1 44.2 %collective-permute-start.111 = (bf16[64,1024]{1,0:T(8,128)(2,1)S(1)}, bf16[64,1024]{1,0:T(8,128)(2,1)}, u32[]{:S(2)}, u32[]{:S(2)}) collective-permute-start(bf16[64,1024]{1,0:T(8,128)(2,1)S(1)} %get-tuple-element.76), channel_id=1, source_target_pairs={{0,4},{2,6},{4,7},{6,5},{7,3},{5,1},{3,0},{1,2},{8,12},{10,14},{12... | collective-permute-start | bytes 393224 | tf_op jit(solution)/shard_map/ppermute | solution.py:48
  706.1 39.7 %collective-permute-start.110 = (bf16[64,1024]{1,0:T(8,128)(2,1)S(1)}, bf16[64,1024]{1,0:T(8,128)(2,1)}, u32[]{:S(2)}, u32[]{:S(2)}) collective-permute-start(bf16[64,1024]{1,0:T(8,128)(2,1)S(1)} %get-tuple-element.77), channel_id=1, source_target_pairs={{0,6},{2,7},{4,5},{6,3},{7,1},{5,0},{3,2},{1,4},{8,14},{10,15},{12... | collective-permute-start | bytes 393224 | tf_op jit(solution)/shard_map/ppermute | solution.py:48
  706.1 38.7 %collective-permute-start.109 = (bf16[64,1024]{1,0:T(8,128)(2,1)S(1)}, bf16[64,1024]{1,0:T(8,128)(2,1)}, u32[]{:S(2)}, u32[]{:S(2)}) collective-permute-start(bf16[64,1024]{1,0:T(8,128)(2,1)S(1)} %get-tuple-element.78), channel_id=1, source_target_pairs={{0,7},{2,5},{4,3},{6,1},{7,0},{5,2},{3,4},{1,6},{8,15},{10,13},{12... | collective-permute-start | bytes 393224 | tf_op jit(solution)/shard_map/ppermute | solution.py:48
  743.1 85.0 %collective-permute-start.105 = (bf16[64,1024]{1,0:T(8,128)(2,1)S(1)}, bf16[64,1024]{1,0:T(8,128)(2,1)S(1)}, u32[]{:S(2)}, u32[]{:S(2)}) collective-permute-start(bf16[64,1024]{1,0:T(8,128)(2,1)S(1)} %get-tuple-element.83), channel_id=1, source_target_pairs={{0,2},{2,4},{4,6},{6,7},{7,5},{5,3},{3,1},{1,0},{8,10},{10,12},{12... | collective-permute-start | bytes 393224 | tf_op jit(solution)/shard_map/ppermute | solution.py:48
  744.8 83.2 %collective-permute-start.104 = (bf16[64,1024]{1,0:T(8,128)(2,1)S(1)}, bf16[64,1024]{1,0:T(8,128)(2,1)S(1)}, u32[]{:S(2)}, u32[]{:S(2)}) collective-permute-start(bf16[64,1024]{1,0:T(8,128)(2,1)S(1)} %get-tuple-element.84), channel_id=1, source_target_pairs={{0,4},{2,6},{4,7},{6,5},{7,3},{5,1},{3,0},{1,2},{8,12},{10,14},{12... | collective-permute-start | bytes 393224 | tf_op jit(solution)/shard_map/ppermute | solution.py:48
  745.8 82.2 %collective-permute-start.103 = (bf16[64,1024]{1,0:T(8,128)(2,1)S(1)}, bf16[64,1024]{1,0:T(8,128)(2,1)S(1)}, u32[]{:S(2)}, u32[]{:S(2)}) collective-permute-start(bf16[64,1024]{1,0:T(8,128)(2,1)S(1)} %get-tuple-element.85), channel_id=1, source_target_pairs={{0,6},{2,7},{4,5},{6,3},{7,1},{5,0},{3,2},{1,4},{8,14},{10,15},{12... | collective-permute-start | bytes 393224 | tf_op jit(solution)/shard_map/ppermute | solution.py:48
  750.3 77.6 %collective-permute-start.102 = (bf16[64,1024]{1,0:T(8,128)(2,1)S(1)}, bf16[64,1024]{1,0:T(8,128)(2,1)S(1)}, u32[]{:S(2)}, u32[]{:S(2)}) collective-permute-start(bf16[64,1024]{1,0:T(8,128)(2,1)S(1)} %get-tuple-element.86), channel_id=1, source_target_pairs={{0,7},{2,5},{4,3},{6,1},{7,0},{5,2},{3,4},{1,6},{8,15},{10,13},{12... | collective-permute-start | bytes 393224 | tf_op jit(solution)/shard_map/ppermute | solution.py:48
  834.7 22.0 %collective-permute-start.82 = (bf16[64,768]{1,0:T(8,128)(2,1)S(1)}, bf16[64,768]{1,0:T(8,128)(2,1)S(1)}, u32[]{:S(2)}, u32[]{:S(2)}) collective-permute-start(bf16[64,768]{1,0:T(8,128)(2,1)S(1)} %get-tuple-element.123), channel_id=1, source_target_pairs={{0,2},{2,4},{4,6},{6,7},{7,5},{5,3},{3,1},{1,0},{8,10},{10,12},{12... | collective-permute-start | bytes 294920 | tf_op jit(solution)/shard_map/ppermute | solution.py:48
  836.7 20.0 %collective-permute-start.81 = (bf16[64,768]{1,0:T(8,128)(2,1)S(1)}, bf16[64,768]{1,0:T(8,128)(2,1)S(1)}, u32[]{:S(2)}, u32[]{:S(2)}) collective-permute-start(bf16[64,768]{1,0:T(8,128)(2,1)S(1)} %get-tuple-element.124), channel_id=1, source_target_pairs={{0,4},{2,6},{4,7},{6,5},{7,3},{5,1},{3,0},{1,2},{8,12},{10,14},{12... | collective-permute-start | bytes 294920 | tf_op jit(solution)/shard_map/ppermute | solution.py:48
  836.7 20.0 %collective-permute-start.80 = (bf16[64,768]{1,0:T(8,128)(2,1)S(1)}, bf16[64,768]{1,0:T(8,128)(2,1)S(1)}, u32[]{:S(2)}, u32[]{:S(2)}) collective-permute-start(bf16[64,768]{1,0:T(8,128)(2,1)S(1)} %get-tuple-element.125), channel_id=1, source_target_pairs={{0,6},{2,7},{4,5},{6,3},{7,1},{5,0},{3,2},{1,4},{8,14},{10,15},{12... | collective-permute-start | bytes 294920 | tf_op jit(solution)/shard_map/ppermute | solution.py:48
  (114 other events, 1804.4 us)
Sparse Core Ops, SparseCore 0:
  61.6 27.7 all-gather.5
  92.3 112.5 all-gather.7
  207.0 37.8 all-gather.11
  246.9 34.4 all-gather.9
  283.4 34.4 all-gather.13
  555.0 26.6 reduce-scatter.7
  584.2 44.5 reduce-scatter.13
  631.4 44.5 reduce-scatter.9
  678.5 47.3 reduce-scatter.11
  728.3 37.8 reduce-scatter.5

commit v2 on v1

--- a/solution.py
+++ b/solution.py
@@ -27,6 +27,56 @@
     )
 
 
+def tie(values, done):
+    done = tuple(done)
+    if not done:
+        return list(values)
+    return list(lax.optimization_barrier((tuple(values), done))[0])
+
+
+class Shares:
+    def __init__(self, count):
+        self.count = count
+        self.index = lax.axis_index("dp")
+        self.bits = [1 << i for i in range(count.bit_length() - 1)]
+        even = [0]
+        for bit in self.bits[1:]:
+            even = even + [k ^ bit for k in even]
+        self.order = even + [k ^ 1 for k in even] if count > 1 else even
+
+    def swap(self, value, bit):
+        return lax.ppermute(value, "dp", [(i, i ^ bit) for i in range(self.count)])
+
+    def relative(self, blocks):
+        for bit in self.bits:
+            odd = (self.index & bit) != 0
+            blocks = [jnp.where(odd, blocks[k ^ bit], blocks[k]) for k in range(self.count)]
+        return blocks
+
+    def to_order(self, values):
+        blocks = self.relative(jnp.split(values, self.count, axis=1))
+        return jnp.concatenate([blocks[k] for k in self.order], axis=1)
+
+    def from_order(self, values):
+        parts = jnp.split(values, self.count, axis=1)
+        blocks = [parts[self.order.index(k)] for k in range(self.count)]
+        return jnp.concatenate(self.relative(blocks), axis=1)
+
+    def gather(self, block, done=()):
+        (value,) = tie([block], done)
+        for bit in self.bits[1:]:
+            value = jnp.concatenate([value, self.swap(value, bit)], axis=0)
+        return value, self.swap(value, 1)
+
+    def scatter_sum(self, kept, given):
+        total = kept() + self.swap(given, 1).astype(F32)
+        for bit in reversed(self.bits[1:]):
+            half = total.shape[0] // 2
+            low = total.astype(BF16)
+            total = total[:half] + self.swap(low[half:], bit).astype(F32)
+        return total.astype(BF16)
+
+
 class Ring:
     def __init__(self, size):
         self.size = size
@@ -34,6 +84,7 @@
         places = [self.order.index(i) for i in range(size)]
         self.place = jnp.array(places, jnp.int32)[lax.axis_index("ctx")]
         self.table = jnp.array(self.order, jnp.int32)
+        self.done = ()
 
     def owner(self, ahead):
         return self.table[lax.rem(self.place + ahead + self.size, self.size)]
@@ -47,29 +98,42 @@
         ]
         return lax.ppermute(value, "ctx", pairs)
 
-    def gather(self, value):
+    def both(self, right, left, done=()):
+        right, left = tie((right, left), (*self.done, *done))
+        right, left = self.shift(right, 1), self.shift(left, -1)
+        self.done = (right, left)
+        return right, left
+
+    def gather(self, value, fill=()):
         size, half = self.size, self.size // 2
+        fill = dict(enumerate(fill))
         pieces = [None] * size
         pieces[0] = value
         right = left = value
         for step in range(1, half):
-            right = self.shift(right, 1)
-            left = self.shift(left, -1)
+            right, left = self.both(right, left, fill.get(step - 1, ()))
             pieces[size - step] = right
             pieces[step] = left
         rows = value.shape[0] // 2
         pieces[half] = jnp.concatenate(
-            [self.shift(right[:rows], 1), self.shift(left[rows:], -1)], axis=0
+            self.both(right[:rows], left[rows:], fill.get(half - 1, ())), axis=0
         )
         return pieces
 
-    def scatter_sum(self, part):
+    def scatter_sum(self, lower, upper, fill=()):
         size, half = self.size, self.size // 2
-        lower, upper, whole = 0, 1, 2
-        right = part(half, lower).astype(BF16)
-        left = part(half, upper).astype(BF16)
-        right = self.shift(right, 1)
-        left = self.shift(left, -1)
+        fill = dict(enumerate(fill))
+        rows = lower.shape[0] // size
+
+        def part(ahead, source):
+            return source[ahead * rows : (ahead + 1) * rows]
+
+        def whole(ahead):
+            return jnp.concatenate([part(ahead, lower), part(ahead, upper)], axis=1)
+
+        right, left = self.both(
+            part(half, lower).astype(BF16), part(half, upper).astype(BF16), fill.get(0, ())
+        )
         for step in range(1, half):
             if step == 1:
                 right = jnp.concatenate(
@@ -79,22 +143,22 @@
                     [part(half + 1, lower), part(half + 1, upper) + left.astype(F32)], axis=1
                 )
             else:
-                right = part(half - step, whole) + right.astype(F32)
-                left = part(half + step, whole) + left.astype(F32)
-            right = self.shift(right.astype(BF16), 1)
-            left = self.shift(left.astype(BF16), -1)
+                right = whole(half - step) + right.astype(F32)
+                left = whole(half + step) + left.astype(F32)
+            right, left = self.both(right.astype(BF16), left.astype(BF16), fill.get(step, ()))
         if half == 1:
             return jnp.concatenate(
                 [part(0, lower) + right.astype(F32), part(0, upper) + left.astype(F32)], axis=1
             )
-        return part(0, whole) + right.astype(F32) + left.astype(F32)
-
-    def exchange(self, pieces):
+        return whole(0) + right.astype(F32) + left.astype(F32)
+
+    def exchange(self, pieces, done=()):
         size = self.size
         out = [None] * size
         out[0] = pieces[0]
+        sent = tie(pieces[1:], done)
         for by in range(1, size):
-            out[size - by] = self.shift(pieces[by], by)
+            out[size - by] = self.shift(sent[by - 1], by)
         return out
 
     def place_in_order(self, pieces):
@@ -323,120 +387,151 @@
     groups, slots, width = inputs.shape
     head_size = width // HEADS
     size = lax.axis_size("ctx")
-    shares = lax.axis_size("dp")
+    count = lax.axis_size("dp")
     rows = groups * slots
     ring = Ring(size)
+    shares = Shares(count)
     owners = ring.owners()
     local = width // size
     hidden_local = gate_weight.shape[1] // size
     gain_one = attn_gain.astype(F32)[:, None]
     gain_two = ffn_gain.astype(F32)[:, None]
 
-    def over_shares(value):
-        return lax.all_gather(value, "dp", axis=0, tiled=True)
-
     def scaled(weight, gain):
         return (weight.astype(F32) * gain).astype(BF16)
 
-    def to_columns(weights):
+    def send_columns(weights, done=()):
         blocks = jnp.concatenate([column_blocks(w, size) for w in weights], axis=2)
-        got = ring.place_in_order(ring.exchange(ring.take_relative(blocks)))
+        return ring.exchange(ring.take_relative(blocks), done)
+
+    def placed(pieces):
+        got = ring.place_in_order(pieces)
         return got.reshape(-1, got.shape[2])
 
-    attn_rows = to_columns([scaled(w, gain_one) for w in (query_weight, key_weight, value_weight)])
-    attn_columns = over_shares(attn_rows)
-    ffn_rows = to_columns(
-        [scaled(gate_weight, gain_two), scaled(up_weight, gain_two), down_weight]
-    )
-    gate_columns = over_shares(ffn_rows[:, :hidden_local])
-    up_columns = over_shares(ffn_rows[:, hidden_local : 2 * hidden_local])
-    down_columns = over_shares(ffn_rows[:, 2 * hidden_local :])
-    mix_full = lax.all_gather(mix_weight, ("dp", "ctx"), axis=0, tiled=True)
-
-    block_in = inputs.reshape(rows, width).astype(F32)
+    def halves(pieces):
+        half = width // 2
+        return (
+            jnp.concatenate([p[:, :half] for p in pieces], axis=0),
+            jnp.concatenate([p[:, half:] for p in pieces], axis=0),
+        )
+
+    def apply(values, weights):
+        return contract(values[0], weights[0], 1, 0) + contract(values[1], weights[1], 1, 0)
+
+    block_in = shares.to_order(inputs.reshape(rows, width)).astype(F32)
     positions = lax.axis_index("ctx") * slots + jnp.arange(slots, dtype=jnp.int32)
     valid = (positions[None, :] < lengths[:, None]).astype(F32).reshape(rows, 1)
     normed_one, factor_one = normalize(block_in)
-    one_all = jnp.concatenate(ring.gather(normed_one.astype(BF16)), axis=0)
-    grad_out = cotangent.reshape(rows, width).astype(F32) * valid
-    grad_all = jnp.concatenate(ring.gather(grad_out.astype(BF16)), axis=0)
-    projected = contract(one_all, attn_columns, 1, 0)
+    grad_out = shares.to_order(cotangent.reshape(rows, width)).astype(F32) * valid
+
+    attn_pieces = send_columns([scaled(w, gain_one) for w in (query_weight, key_weight, value_weight)])
+    one_pieces = ring.gather(normed_one.astype(BF16))
+    one_all = halves(one_pieces)
+    attn_weights = shares.gather(placed(attn_pieces))
+    to_shares = [(i * size + j, j * count + i) for i in range(count) for j in range(size)]
+    from_shares = [(there, here) for here, there in to_shares]
+    (mix_sent,) = tie([mix_weight], ring.done)
+    mix_parts = shares.gather(lax.ppermute(mix_sent, ("dp", "ctx"), from_shares))
+    ffn_pieces = send_columns(
+        [scaled(gate_weight, gain_two), scaled(up_weight, gain_two), down_weight], ring.done
+    )
+    mix_blocks = jnp.split(jnp.concatenate(mix_parts, axis=0), count, axis=0)
+    mix_rows = shares.to_order(
+        jnp.concatenate(
+            shares.relative([mix_blocks[shares.order.index(k)] for k in range(count)]), axis=0
+        )
+    )
+    projected = apply(one_all, attn_weights)
     attention = Attention(size, groups, slots, local, head_size, lengths, owners)
     mixed, query_rot, key_rot, value_low, lse = attention.forward(projected)
-    mixed_rows = mixed.reshape(size, rows, local)
-    attended = join_columns(
-        ring.place_in_order(ring.exchange([mixed_rows[r] for r in range(size)]))
-    )
-    residual = block_in + contract(attended, mix_full, 1, 0)
-
+    mixed = mixed.reshape(size * rows, local)
+    attn_out = contract(mixed, mix_rows, 1, 0)
+    residual = block_in + ring.scatter_sum(attn_out[:, : width // 2], attn_out[:, width // 2 :])
+
+    ffn_weights = shares.gather(placed([p[:, : 2 * hidden_local] for p in ffn_pieces]))
+    down_weights = shares.gather(
+        placed([p[:, 2 * hidden_local :] for p in ffn_pieces]), [ffn_weights[1]]
+    )
     normed_two, factor_two = normalize(residual)
-    two_all = jnp.concatenate(ring.gather(normed_two.astype(BF16)), axis=0)
-    gate = contract(two_all, gate_columns, 1, 0)
-    up = contract(two_all, up_columns, 1, 0)
+    two_all = halves(ring.gather(normed_two.astype(BF16)))
+    grad_all = halves(ring.gather(grad_out.astype(BF16)))
+    gate_up = apply(two_all, ffn_weights)
+    gate, up = gate_up[:, :hidden_local], gate_up[:, hidden_local:]
     sigma = jax.nn.sigmoid(gate)
     silu_gate = gate * sigma
     hidden = (silu_gate * up).astype(BF16)
-
-    grad_hidden = contract(grad_all, down_columns, 1, 0)
-    gate_low = (grad_hidden * up * sigma * (1.0 + gate * (1.0 - sigma))).astype(BF16)
-    up_low = (grad_hidden * silu_gate).astype(BF16)
-
-    def terms(values):
-        half = width // 2
-
-        def part(ahead, columns):
-            chunk = values[ahead * rows : (ahead + 1) * rows]
-            return (chunk[:, :half], chunk[:, half:], chunk)[columns]
-
-        return part
-
+    branch = ring.scatter_sum(*(contract(hidden, w, 1, 1) for w in down_weights))
+    activations = valid * (residual + branch)
+
+    grad_hidden = apply(grad_all, down_weights)
+    grad_both = jnp.concatenate(
+        [
+            (grad_hidden * up * sigma * (1.0 + gate * (1.0 - sigma))).astype(BF16),
+            (grad_hidden * silu_gate).astype(BF16),
+        ],
+        axis=1,
+    )
+
+    def summed(values, gradient):
+        given = contract(values[1], gradient, 0, 0).astype(BF16)
+        return given, lambda: shares.scatter_sum(
+            lambda: contract(values[0], gradient, 0, 0), given
+        )
+
+    down_given, down_total = summed(grad_all, hidden)
+    both_given, both_total = summed(two_all, grad_both)
+    down_sum = down_total()
+    both_sum = both_total()
     scaled_two = ring.scatter_sum(
-        terms(contract(gate_low, gate_columns, 1, 1) + contract(up_low, up_columns, 1, 1))
+        *(contract(grad_both, w, 1, 1) for w in ffn_weights),
+        fill=((), (down_given,), (both_given,)),
     )
     dres = grad_out + factor_two * (
         scaled_two - normed_two * jnp.mean(normed_two * scaled_two, axis=-1, keepdims=True)
     )
     dres_low = dres.astype(BF16)
-    branch = ring.scatter_sum(terms(contract(hidden, down_columns, 1, 1)))
-    activations = (valid * (residual + branch)).astype(BF16)
-
-    grad_mixed = contract(dres_low, mix_full, 1, 1).astype(BF16)
-    grad_heads = jnp.concatenate(
-        ring.exchange(ring.take_relative(column_blocks(grad_mixed, size))), axis=0
-    )
-    dres_all = jnp.concatenate(ring.gather(dres_low), axis=0)
+
+    def send_rows(total, done=()):
+        stacked = total.reshape(size, total.shape[0] // size, total.shape[1])
+        return ring.exchange(ring.take_relative(stacked), done)
+
+    dres_pieces = ring.gather(dres_low, fill=((), (), (down_sum,)))
+    dres_all = jnp.concatenate(dres_pieces, axis=0)
+    down_pieces = send_rows(down_sum, ring.done)
+    both_pieces = send_rows(both_sum, ring.done)
+    grad_heads = contract(dres_all, mix_rows, 1, 1).astype(BF16)
     dq, dk, dv = attention.backward(query_rot, key_rot, value_low, grad_heads, lse)
     projected_grad = jnp.concatenate(
         [d.reshape(size * rows, local) for d in (dq, dk, dv)], axis=1
     )
-    scaled_one = ring.scatter_sum(terms(contract(projected_grad, attn_columns, 1, 1)))
+    attn_given, attn_total = summed(one_all, projected_grad)
+    attn_sum = attn_total()
+    attn_pieces = send_rows(attn_sum)
+    mix_terms = shares.from_order(contract(mixed, dres_all, 0, 0))
+    mix_blocks = shares.relative(jnp.split(mix_terms, count, axis=0))
+    mix_blocks = [mix_blocks[k] for k in shares.order]
+    mix_given = jnp.concatenate(mix_blocks[count // 2 :], axis=0).astype(BF16)
+    mix_sum = shares.scatter_sum(
+        lambda: jnp.concatenate(mix_blocks[: count // 2], axis=0), mix_given
+    )
+    scaled_one = ring.scatter_sum(
+        *(contract(projected_grad, w, 1, 1) for w in attn_weights),
+        fill=((attn_given,),),
+    )
     input_grad = dres + factor_one * (
         scaled_one - normed_one * jnp.mean(normed_one * scaled_one, axis=-1, keepdims=True)
     )
-
-    def to_rows(gradient):
-        summed = lax.psum_scatter(gradient.astype(BF16), "dp", scatter_dimension=0, tiled=True)
-        stacked = summed.reshape(size, summed.shape[0] // size, summed.shape[1])
-        return ring.place_in_order(ring.exchange(ring.take_relative(stacked)))
-
-    down_grad = join_columns(to_rows(contract(grad_all, hidden, 0, 0))).astype(F32)
-    gate_raw = join_columns(to_rows(contract(two_all, gate_low, 0, 0))).astype(F32)
-    up_raw = join_columns(to_rows(contract(two_all, up_low, 0, 0))).astype(F32)
-    attn_raw = to_rows(contract(one_all, projected_grad, 0, 0))
+    mix_grad = lax.ppermute(mix_sum, ("dp", "ctx"), to_shares).astype(F32)
+
+    def joined(pieces, columns):
+        return join_columns(ring.place_in_order([p[:, columns] for p in pieces])).astype(F32)
+
+    down_grad = joined(down_pieces, slice(None))
+    gate_raw = joined(both_pieces, slice(0, hidden_local))
+    up_raw = joined(both_pieces, slice(hidden_local, 2 * hidden_local))
     query_raw, key_raw, value_raw = (
-        join_columns(attn_raw[:, :, i * local : (i + 1) * local]).astype(F32) for i in range(3)
-    )
-    mix_part = lax.psum_scatter(
-        contract(mixed.reshape(size * rows, local), dres_all, 0, 0).astype(BF16),
-        "dp",
-        scatter_dimension=0,
-        tiled=True,
-    )
-    mix_grad = lax.ppermute(
-        mix_part,
-        ("dp", "ctx"),
-        [(i * size + j, j * shares + i) for i in range(shares) for j in range(size)],
-    ).astype(F32)
+        joined(attn_pieces, slice(i * local, (i + 1) * local)) for i in range(3)
+    )
 
     def row_sum(*pairs):
         return sum(jnp.sum(w.astype(F32) * g, axis=1) for w, g in pairs)
@@ -446,8 +541,8 @@
     )
     ffn_gain_grad = row_sum((gate_weight, gate_raw), (up_weight, up_raw))
     return (
-        activations.reshape(groups, slots, width),
-        input_grad.astype(BF16).reshape(groups, slots, width),
+        shares.from_order(activations.astype(BF16)).reshape(groups, slots, width),
+        shares.from_order(input_grad.astype(BF16)).reshape(groups, slots, width),
         query_raw * gain_one,
         key_raw * gain_one,
         value_raw * gain_one,

time: 881 us -> 784 us (0.89)
  waiting for transfers between devices: 440 us -> 348 us
  starting transfers between devices: 169 us -> 209 us
  matrix products: 117 us -> 88.1 us
  local copies, waits for them, and re-layouts: 61.2 us -> 47.1 us
  between operations: 39.1 us -> 26.3 us
  other arithmetic: 24.5 us -> 35.1 us
    ppermute x112 -> x99, waiting for transfers between devices: 428 us -> 287 us  [shift(): return lax.ppermute(value, 'ctx', pairs)]
    ppermute x1 -> x18, waiting for transfers between devices: 0.01 us -> 60.9 us  [the longest x16 60.9 us: swap(): return lax.ppermute(value, 'dp', [(i, i ^ bit) for i in range(self.count)])]
    dot_general x15 -> x21, matrix products: 117 us -> 88.1 us  [contract(): lax.dot_general(left, right, (((left_dim,), (right_dim,)), ((), ())), pre...]
    ppermute x1 -> x18, starting transfers between devices: 1.65 us -> 22.4 us  [the longest x16 21.1 us: swap(): return lax.ppermute(value, 'dp', [(i, i ^ bit) for i in range(self.count)])]
    ppermute x112 -> x99, starting transfers between devices: 166 us -> 187 us  [shift(): return lax.ppermute(value, 'ctx', pairs)]
    unnamed x197 -> x280, local copies, waits for them, and re-layouts: 33.7 us -> 13.7 us
    dynamic_update_slice x50 -> x48, local copies, waits for them, and re-layouts: 4.35 us -> 15.3 us  [place_in_order(): lax.dynamic_update_index_in_dim(out, pieces[ahead], self.owner(ahead), 0)]
    reduce_scatter x5 -> x0, waiting for transfers between devices: 10.6 us -> none  [the longest x4 10.6 us: to_rows(): lax.psum_scatter(gradient.astype(BF16), 'dp', scatter_dimension=0, tiled=...]
  transfers between devices with their start and end apart: 123 -> 117, of which waited for: 67 -> 67; matrix products, arithmetic and copies ran while one was open for 17% -> 18% of each run, Pallas kernels for 3% -> 3%
where the time goes in v2:
time: 784 us; the launch traced here: 777 us
  waiting for transfers between devices  348 us (44%)
  starting transfers between devices  209 us (27%)
  matrix products  88.1 us (11%)
  local copies, waits for them, and re-layouts  47.1 us (6%)
  other arithmetic  35.1 us (4%)
  between operations  26.3 us (3%)
  Pallas kernels  23.3 us (3%)
    ppermute x99, waiting for transfers between devices, shift(): return lax.ppermute(value, 'ctx', pairs)  287 us
    ppermute x99, starting transfers between devices, shift(): return lax.ppermute(value, 'ctx', pairs)  187 us
    dot_general x21, matrix products, contract(): lax.dot_general(left, right, (((left_dim,), (right_dim,)), ((), ())), pre...  88.1 us
    ppermute x16, waiting for transfers between devices, swap(): return lax.ppermute(value, 'dp', [(i, i ^ bit) for i in range(self.count)])  60.9 us
    ppermute x16, starting transfers between devices, swap(): return lax.ppermute(value, 'dp', [(i, i ^ bit) for i in range(self.count)])  21.1 us
  transfers between devices with their start and end apart: 117, of which 67 were waited for; matrix products, arithmetic and copies ran while one was open for 18% of the time, Pallas kernels for 3%

profile of v2, /device:TPU:0, one launch (start us, length us, event | category | flops | bytes accessed | tf_op | source)
XLA Modules:
  0.0 777.3 jit_solution(508549762025400177)
XLA Ops:
  83.9 5.3 collective-permute-done.5
  106.9 14.1 %collective-permute-start.39 = (bf16[64,3072]{1,0:T(8,128)(2,1)}, bf16[64,3072]{1,0:T(8,128)(2,1)}, u32[]{:S(2)}, u32[]{:S(2)}) collective-permute-start(bf16[64,3072]{1,0:T(8,128)(2,1)} %get-tuple-element.131), channel_id=1, source_target_pairs={{0,7},{2,5},{4,3},{6,1},{7,0},{5,2},{3,4},{1,6},{8,15},{10,13},{12... | collective-permute-start | bytes 1179656 | tf_op jit(solution)/shard_map/ppermute | solution.py:99
  120.9 16.2 %collective-permute-start.18 = (bf16[64,2048]{1,0:T(8,128)(2,1)S(1)}, bf16[64,2048]{1,0:T(8,128)(2,1)S(1)}, u32[]{:S(2)}, u32[]{:S(2)}) collective-permute-start(bf16[64,2048]{1,0:T(8,128)(2,1)S(1)} %collective-permute-done.17), channel_id=1, source_target_pairs={{0,16},{8,24},{16,0},{24,8},{1,17},{9,25},{17,1},{25,9},{2,18},{10... | collective-permute-start | bytes 786440 | tf_op jit(solution)/shard_map/ppermute | solution.py:48
  141.4 29.3 %collective-permute-start.40 = (bf16[64,3072]{1,0:T(8,128)(2,1)}, bf16[64,3072]{1,0:T(8,128)(2,1)}, u32[]{:S(2)}, u32[]{:S(2)}) collective-permute-start(bf16[64,3072]{1,0:T(8,128)(2,1)} %get-tuple-element.132), channel_id=1, source_target_pairs={{0,6},{2,7},{4,5},{6,3},{7,1},{5,0},{3,2},{1,4},{8,14},{10,15},{12... | collective-permute-start | bytes 1179656 | tf_op jit(solution)/shard_map/ppermute | solution.py:99
  179.6 10.5 %attention_forward.1 = (bf16[8,2,64,256]{3,2,1,0:T(8,128)(2,1)}, bf16[8,2,64,256]{3,2,1,0:T(8,128)(2,1)}, bf16[8,2,64,256]{3,2,1,0:T(8,128)(2,1)}, bf16[8,2,64,256]{3,2,1,0:T(8,128)(2,1)}, f32[2,512,4]{2,1,0:T(8,128)}) custom-call(s32[2]{0:T(128)} %lengths_ref.3, f32[8,2,64,768]{3,2,1,0:T(8,128)} %bitcast.751, f32[8,2,64,768]{3,2,1,0:T(8,128)} %bitcast.752, ...), custom_call_target="tpu_custom_call" | custom-call | flops 536870912 | bytes 4194304 | tf_op jit(solution)/shard_map/attention_forward/pallas_call | solution.py:340
  196.8 5.7 collective-permute-done.20
  207.4 17.9 %collective-permute-done.22 = bf16[128,2048]{1,0:T(8,128)(2,1)S(1)} collective-permute-done((bf16[128,2048]{1,0:T(8,128)(2,1)S(1)}, bf16[128,2048]{1,0:T(8,128)(2,1)S(1)}, u32[]{:S(2)}, u32[]{:S(2)}) %collective-permute-start.22) | collective-permute-done | bytes 524320 | tf_op jit(solution)/shard_map/ppermute | solution.py:99
  225.7 6.9 collective-permute-start.24
  237.0 8.5 %collective-permute-done.24 = bf16[128,2048]{1,0:T(8,128)(2,1)S(1)} collective-permute-done((bf16[128,2048]{1,0:T(8,128)(2,1)S(1)}, bf16[128,2048]{1,0:T(8,128)(2,1)S(1)}, u32[]{:S(2)}, u32[]{:S(2)}) %collective-permute-start.24) | collective-permute-done | bytes 524320 | tf_op jit(solution)/shard_map/ppermute | solution.py:99
  245.8 5.4 collective-permute-start.26
  255.5 9.7 %collective-permute-done.26 = bf16[128,2048]{1,0:T(8,128)(2,1)S(1)} collective-permute-done((bf16[128,2048]{1,0:T(8,128)(2,1)S(1)}, bf16[128,2048]{1,0:T(8,128)(2,1)S(1)}, u32[]{:S(2)}, u32[]{:S(2)}) %collective-permute-start.26) | collective-permute-done | bytes 524320 | tf_op jit(solution)/shard_map/ppermute | solution.py:99
  270.6 7.3 collective-permute-done.28
  282.0 18.5 %collective-permute-done.43 = bf16[512,2048]{1,0:T(8,128)(2,1)S(1)} collective-permute-done((bf16[512,2048]{1,0:T(8,128)(2,1)S(1)}, bf16[512,2048]{1,0:T(8,128)(2,1)S(1)}, u32[]{:S(2)}, u32[]{:S(2)}) %collective-permute-start.43) | collective-permute-done | bytes 2097184 | tf_op jit(solution)/shard_map/ppermute | solution.py:48
  304.2 11.3 %collective-permute-done.33 = bf16[128,2048]{1,0:T(8,128)(2,1)S(1)} collective-permute-done((bf16[128,2048]{1,0:T(8,128)(2,1)S(1)}, bf16[128,2048]{1,0:T(8,128)(2,1)S(1)}, u32[]{:S(2)}, u32[]{:S(2)}) %collective-permute-start.33) | collective-permute-done | bytes 524320 | tf_op jit(solution)/shard_map/ppermute | solution.py:99
  317.7 5.7 collective-permute-done.34
  326.5 9.5 %collective-permute-done.47 = bf16[128,2048]{1,0:T(8,128)(2,1)S(1)} collective-permute-done((bf16[128,2048]{1,0:T(8,128)(2,1)S(1)}, bf16[128,2048]{1,0:T(8,128)(2,1)S(1)}, u32[]{:S(2)}, u32[]{:S(2)}) %collective-permute-start.47) | collective-permute-done | bytes 524320 | tf_op jit(solution)/shard_map/ppermute | solution.py:99
  339.0 8.9 %collective-permute-done.49 = bf16[128,2048]{1,0:T(8,128)(2,1)S(1)} collective-permute-done((bf16[128,2048]{1,0:T(8,128)(2,1)S(1)}, bf16[128,2048]{1,0:T(8,128)(2,1)S(1)}, u32[]{:S(2)}, u32[]{:S(2)}) %collective-permute-start.49) | collective-permute-done | bytes 524320 | tf_op jit(solution)/shard_map/ppermute | solution.py:99
  351.6 9.6 %collective-permute-done.51 = bf16[128,2048]{1,0:T(8,128)(2,1)S(1)} collective-permute-done((bf16[128,2048]{1,0:T(8,128)(2,1)S(1)}, bf16[128,2048]{1,0:T(8,128)(2,1)S(1)}, u32[]{:S(2)}, u32[]{:S(2)}) %collective-permute-start.51) | collective-permute-done | bytes 524320 | tf_op jit(solution)/shard_map/ppermute | solution.py:99
  370.3 17.9 %collective-permute-done.45 = bf16[512,1024]{1,0:T(8,128)(2,1)S(1)} collective-permute-done((bf16[512,1024]{1,0:T(8,128)(2,1)S(1)}, bf16[512,1024]{1,0:T(8,128)(2,1)S(1)}, u32[]{:S(2)}, u32[]{:S(2)}) %collective-permute-start.45) | collective-permute-done | bytes 1048608 | tf_op jit(solution)/shard_map/ppermute | solution.py:48
  388.3 6.7 fusion.142
  395.1 8.9 %convolution_add_fusion = f32[1024,2048]{1,0:T(8,128)} fusion(f32[1024,2048]{1,0:T(8,128)} %fusion.142, bf16[1024,1024]{1,0:T(8,128)(2,1)S(1)} %get-tuple-element.353, bf16[512,2048]{1,0:T(8,128)(2,1)S(1)} %collective-permute-done.43, bf16[512,2048]{1,0:T(8,128)(2,1)S(1)} %bitcast.757), kind=kOutput, calls=%fused_computation.12 | convolution fusion | flops 4305453056 | bytes 23068672 | tf_op jit(solution)/shard_map/dot_general | solution.py:25
  406.3 7.8 %multiply_convert_fusion.1 = (bf16[1024,1024]{1,0:T(8,128)(2,1)}, bf16[1024,1024]{1,0:T(8,128)(2,1)}, bf16[1024,1024]{1,0:T(8,128)(2,1)S(1)}) fusion(f32[1024,2048]{1,0:T(8,128)} %convolution_add_fusion, f32[1024,1024]{1,0:T(8,128)S(1)} %fusion.143, bf16[1024,1024]{1,0:T(8,128)(2,1)S(1)} %get-tuple-element.329, ...), kind=kOutput, calls=%fused_computation.8 | convolution fusion | flops 2164260864 | bytes 23068672 | tf_op jit(solution)/shard_map/dot_general | solution.py:25
  421.3 6.5 collective-permute-done.56
  431.0 11.2 %collective-permute-done.58 = bf16[128,2048]{1,0:T(8,128)(2,1)S(1)} collective-permute-done((bf16[128,2048]{1,0:T(8,128)(2,1)S(1)}, bf16[128,2048]{1,0:T(8,128)(2,1)S(1)}, u32[]{:S(2)}, u32[]{:S(2)}) %collective-permute-start.58) | collective-permute-done | bytes 524320 | tf_op jit(solution)/shard_map/ppermute | solution.py:99
  445.2 6.3 fusion.136
  459.0 6.7 fusion.135
  470.9 5.4 convolution_convert_fusion.1
  476.7 8.2 %collective-permute-done.63 = bf16[128,1024]{1,0:T(8,128)(2,1)S(1)} collective-permute-done((bf16[128,1024]{1,0:T(8,128)(2,1)S(1)}, bf16[128,1024]{1,0:T(8,128)(2,1)S(1)}, u32[]{:S(2)}, u32[]{:S(2)}) %collective-permute-start.63) | collective-permute-done | bytes 262176 | tf_op jit(solution)/shard_map/ppermute | solution.py:99
  487.9 7.0 convolution_convert_fusion
  502.7 10.3 %collective-permute-done.68 = bf16[128,2048]{1,0:T(8,128)(2,1)S(1)} collective-permute-done((bf16[128,2048]{1,0:T(8,128)(2,1)S(1)}, bf16[128,2048]{1,0:T(8,128)(2,1)S(1)}, u32[]{:S(2)}, u32[]{:S(2)}) %collective-permute-start.68) | collective-permute-done | bytes 524320 | tf_op jit(solution)/shard_map/ppermute | solution.py:99
  520.7 8.4 %collective-permute-done.69 = bf16[128,2048]{1,0:T(8,128)(2,1)S(1)} collective-permute-done((bf16[128,2048]{1,0:T(8,128)(2,1)S(1)}, bf16[128,2048]{1,0:T(8,128)(2,1)S(1)}, u32[]{:S(2)}, u32[]{:S(2)}) %collective-permute-start.69) | collective-permute-done | bytes 524320 | tf_op jit(solution)/shard_map/ppermute | solution.py:99
  534.0 10.6 %collective-permute-done.76 = bf16[512,1024]{1,0:T(8,128)(2,1)S(1)} collective-permute-done((bf16[512,1024]{1,0:T(8,128)(2,1)S(1)}, bf16[512,1024]{1,0:T(8,128)(2,1)S(1)}, u32[]{:S(2)}, u32[]{:S(2)}) %collective-permute-start.76) | collective-permute-done | bytes 1048608 | tf_op jit(solution)/shard_map/ppermute | solution.py:48
  549.0 8.1 %collective-permute-done.73 = bf16[128,2048]{1,0:T(8,128)(2,1)S(1)} collective-permute-done((bf16[128,2048]{1,0:T(8,128)(2,1)S(1)}, bf16[128,2048]{1,0:T(8,128)(2,1)S(1)}, u32[]{:S(2)}, u32[]{:S(2)}) %collective-permute-start.73) | collective-permute-done | bytes 524320 | tf_op jit(solution)/shard_map/ppermute | solution.py:99
  560.6 7.8 convert_add_fusion
  588.3 12.8 %attention_backward.1 = (bf16[8,2,64,256]{3,2,1,0:T(8,128)(2,1)}, bf16[8,2,64,256]{3,2,1,0:T(8,128)(2,1)}, bf16[8,2,64,256]{3,2,1,0:T(8,128)(2,1)}) custom-call(s32[2]{0:T(128)} %lengths_ref.3, bf16[8,2,64,256]{3,2,1,0:T(8,128)(2,1)} %get-tuple-element.160.q_ref, bf16[8,2,64,256]{3,2,1,0:T(8,128)(2,1)} %get-tuple-element.161.k_ref, ...), custom_call_target="tpu_custom_call" | custom-call | flops 1342177280 | bytes 4194304 | tf_op jit(solution)/shard_map/attention_backward/pallas_call | solution.py:362
  620.4 5.6 collective-permute-start.116
  631.3 5.3 collective-permute-done.82
  637.1 6.8 collective-permute-done.81
  653.8 5.3 collective-permute-done.84
  661.2 5.5 collective-permute-done.103
  667.5 22.3 %collective-permute-done.104 = bf16[64,2048]{1,0:T(8,128)(2,1)S(1)} collective-permute-done((bf16[64,2048]{1,0:T(8,128)(2,1)S(1)}, bf16[64,2048]{1,0:T(8,128)(2,1)S(1)}, u32[]{:S(2)}, u32[]{:S(2)}) %collective-permute-start.104) | collective-permute-done | bytes 262176 | tf_op jit(solution)/shard_map/ppermute | solution.py:99
  689.9 7.9 %collective-permute-start.108 = (bf16[64,2048]{1,0:T(8,128)(2,1)S(1)}, bf16[64,2048]{1,0:T(8,128)(2,1)S(1)}, u32[]{:S(2)}, u32[]{:S(2)}) collective-permute-start(bf16[64,2048]{1,0:T(8,128)(2,1)S(1)} %get-tuple-element.188), channel_id=1, source_target_pairs={{0,4},{2,6},{4,7},{6,5},{7,3},{5,1},{3,0},{1,2},{8,12},{10,14},{12... | collective-permute-start | bytes 786440 | tf_op jit(solution)/shard_map/ppermute | solution.py:99
  698.1 7.1 collective-permute-done.107
  719.8 9.1 %collective-permute-done.86 = bf16[128,2048]{1,0:T(8,128)(2,1)S(1)} collective-permute-done((bf16[128,2048]{1,0:T(8,128)(2,1)S(1)}, bf16[128,2048]{1,0:T(8,128)(2,1)S(1)}, u32[]{:S(2)}, u32[]{:S(2)}) %collective-permute-start.86) | collective-permute-done | bytes 524320 | tf_op jit(solution)/shard_map/ppermute | solution.py:99
  733.4 7.3 collective-permute-done.87
  742.6 7.3 collective-permute-done.90
  750.8 6.6 collective-permute-start.92
  767.0 5.5 collective-permute-done.95
  (687 shorter events, 298.1 us)
Async XLA Ops:
  3.7 60.2 %collective-permute-start = (bf16[128,2048]{1,0:T(8,128)(2,1)}, bf16[128,2048]{1,0:T(8,128)(2,1)}, u32[]{:S(2)}, u32[]{:S(2)}) collective-permute-start(bf16[128,2048]{1,0:T(8,128)(2,1)} %fusion.10), channel_id=1, source_target_pairs={{0,1},{2,0},{4,2},{6,4},{7,6},{5,7},{3,5},{1,3},{8,9},{10,8},{12,1... | collective-permute-start | bytes 1572872 | tf_op jit(solution)/shard_map/ppermute | solution.py:99
  6.7 57.2 %collective-permute-start.1 = (bf16[128,2048]{1,0:T(8,128)(2,1)}, bf16[128,2048]{1,0:T(8,128)(2,1)}, u32[]{:S(2)}, u32[]{:S(2)}) collective-permute-start(bf16[128,2048]{1,0:T(8,128)(2,1)} %fusion.10), channel_id=1, source_target_pairs={{0,2},{2,4},{4,6},{6,7},{7,5},{5,3},{3,1},{1,0},{8,10},{10,12},{12... | collective-permute-start | bytes 1572872 | tf_op jit(solution)/shard_map/ppermute | solution.py:99
  30.6 16.7 %collective-permute-start.8 = (bf16[64,768]{1,0:T(8,128)(2,1)}, bf16[64,768]{1,0:T(8,128)(2,1)}, u32[]{:S(2)}, u32[]{:S(2)}) collective-permute-start(bf16[64,768]{1,0:T(8,128)(2,1)} %get-tuple-element.323), channel_id=1, source_target_pairs={{0,1},{2,0},{4,2},{6,4},{7,6},{5,7},{3,5},{1,3},{8,9},{10,8},{12,1... | collective-permute-start | bytes 294920 | tf_op jit(solution)/shard_map/ppermute | solution.py:99
  32.6 17.9 %collective-permute-start.9 = (bf16[64,768]{1,0:T(8,128)(2,1)}, bf16[64,768]{1,0:T(8,128)(2,1)}, u32[]{:S(2)}, u32[]{:S(2)}) collective-permute-start(bf16[64,768]{1,0:T(8,128)(2,1)} %get-tuple-element.322), channel_id=1, source_target_pairs={{0,3},{2,1},{4,0},{6,2},{7,4},{5,6},{3,7},{1,5},{8,11},{10,9},{12,... | collective-permute-start | bytes 294920 | tf_op jit(solution)/shard_map/ppermute | solution.py:99
  35.2 17.7 %collective-permute-start.10 = (bf16[64,768]{1,0:T(8,128)(2,1)}, bf16[64,768]{1,0:T(8,128)(2,1)}, u32[]{:S(2)}, u32[]{:S(2)}) collective-permute-start(bf16[64,768]{1,0:T(8,128)(2,1)} %get-tuple-element.321), channel_id=1, source_target_pairs={{0,5},{2,3},{4,1},{6,0},{7,2},{5,4},{3,6},{1,7},{8,13},{10,11},{12... | collective-permute-start | bytes 294920 | tf_op jit(solution)/shard_map/ppermute | solution.py:99
  66.0 16.6 %collective-permute-start.15 = (bf16[512,768]{1,0:T(8,128)(2,1)S(1)}, bf16[512,768]{1,0:T(8,128)(2,1)}, u32[]{:S(2)}, u32[]{:S(2)}) collective-permute-start(bf16[512,768]{1,0:T(8,128)(2,1)S(1)} %bitcast.765), channel_id=1, source_target_pairs={{0,16},{8,24},{16,0},{24,8},{1,17},{9,25},{17,1},{25,9},{2,18},{10... | collective-permute-start | bytes 2359304 | tf_op jit(solution)/shard_map/ppermute | solution.py:48
  83.9 87.7 %collective-permute-start.16 = (bf16[1024,768]{1,0:T(8,128)(2,1)S(1)}, bf16[1024,768]{1,0:T(8,128)(2,1)S(1)}, u32[]{:S(2)}, u32[]{:S(2)}) collective-permute-start(bf16[1024,768]{1,0:T(8,128)(2,1)S(1)} %pad_maximum_fusion.4), channel_id=1, source_target_pairs={{0,8},{8,0},{16,24},{24,16},{1,9},{9,1},{17,25},{25,17},{2,10},{10... | collective-permute-start | bytes 4718600 | tf_op jit(solution)/shard_map/ppermute | solution.py:48
  97.7 23.2 %collective-permute-start.36 = (bf16[64,3072]{1,0:T(8,128)(2,1)S(1)}, bf16[64,3072]{1,0:T(8,128)(2,1)S(1)}, u32[]{:S(2)}, u32[]{:S(2)}) collective-permute-start(bf16[64,3072]{1,0:T(8,128)(2,1)S(1)} %copy-done.38), channel_id=1, source_target_pairs={{0,1},{2,0},{4,2},{6,4},{7,6},{5,7},{3,5},{1,3},{8,9},{10,8},{12,1... | collective-permute-start | bytes 1179656 | tf_op jit(solution)/shard_map/ppermute | solution.py:99
  99.5 94.3 %collective-permute-start.37 = (bf16[64,3072]{1,0:T(8,128)(2,1)}, bf16[64,3072]{1,0:T(8,128)(2,1)}, u32[]{:S(2)}, u32[]{:S(2)}) collective-permute-start(bf16[64,3072]{1,0:T(8,128)(2,1)} %get-tuple-element.129), channel_id=1, source_target_pairs={{0,3},{2,1},{4,0},{6,2},{7,4},{5,6},{3,7},{1,5},{8,11},{10,9},{12,... | collective-permute-start | bytes 1179656 | tf_op jit(solution)/shard_map/ppermute | solution.py:99
  101.0 102.3 %collective-permute-start.38 = (bf16[64,3072]{1,0:T(8,128)(2,1)}, bf16[64,3072]{1,0:T(8,128)(2,1)}, u32[]{:S(2)}, u32[]{:S(2)}) collective-permute-start(bf16[64,3072]{1,0:T(8,128)(2,1)} %get-tuple-element.130), channel_id=1, source_target_pairs={{0,5},{2,3},{4,1},{6,0},{7,2},{5,4},{3,6},{1,7},{8,13},{10,11},{12... | collective-permute-start | bytes 1179656 | tf_op jit(solution)/shard_map/ppermute | solution.py:99
  106.9 99.0 %collective-permute-start.39 = (bf16[64,3072]{1,0:T(8,128)(2,1)}, bf16[64,3072]{1,0:T(8,128)(2,1)}, u32[]{:S(2)}, u32[]{:S(2)}) collective-permute-start(bf16[64,3072]{1,0:T(8,128)(2,1)} %get-tuple-element.131), channel_id=1, source_target_pairs={{0,7},{2,5},{4,3},{6,1},{7,0},{5,2},{3,4},{1,6},{8,15},{10,13},{12... | collective-permute-start | bytes 1179656 | tf_op jit(solution)/shard_map/ppermute | solution.py:99
  120.9 20.5 %collective-permute-start.18 = (bf16[64,2048]{1,0:T(8,128)(2,1)S(1)}, bf16[64,2048]{1,0:T(8,128)(2,1)S(1)}, u32[]{:S(2)}, u32[]{:S(2)}) collective-permute-start(bf16[64,2048]{1,0:T(8,128)(2,1)S(1)} %collective-permute-done.17), channel_id=1, source_target_pairs={{0,16},{8,24},{16,0},{24,8},{1,17},{9,25},{17,1},{25,9},{2,18},{10... | collective-permute-start | bytes 786440 | tf_op jit(solution)/shard_map/ppermute | solution.py:48
  141.4 94.5 %collective-permute-start.40 = (bf16[64,3072]{1,0:T(8,128)(2,1)}, bf16[64,3072]{1,0:T(8,128)(2,1)}, u32[]{:S(2)}, u32[]{:S(2)}) collective-permute-start(bf16[64,3072]{1,0:T(8,128)(2,1)} %get-tuple-element.132), channel_id=1, source_target_pairs={{0,6},{2,7},{4,5},{6,3},{7,1},{5,0},{3,2},{1,4},{8,14},{10,15},{12... | collective-permute-start | bytes 1179656 | tf_op jit(solution)/shard_map/ppermute | solution.py:99
  171.6 18.5 %collective-permute-start.19 = (bf16[128,2048]{1,0:T(8,128)(2,1)}, bf16[128,2048]{1,0:T(8,128)(2,1)}, u32[]{:S(2)}, u32[]{:S(2)}) collective-permute-start(bf16[128,2048]{1,0:T(8,128)(2,1)} %pad_maximum_fusion.10), channel_id=1, source_target_pairs={{0,8},{8,0},{16,24},{24,16},{1,9},{9,1},{17,25},{25,17},{2,10},{10... | collective-permute-start | bytes 1572872 | tf_op jit(solution)/shard_map/ppermute | solution.py:48
  202.5 34.4 %collective-permute-start.41 = (bf16[64,3072]{1,0:T(8,128)(2,1)S(1)}, bf16[64,3072]{1,0:T(8,128)(2,1)S(1)}, u32[]{:S(2)}, u32[]{:S(2)}) collective-permute-start(bf16[64,3072]{1,0:T(8,128)(2,1)S(1)} %copy-done.37), channel_id=1, source_target_pairs={{0,4},{2,6},{4,7},{6,5},{7,3},{5,1},{3,0},{1,2},{8,12},{10,14},{12... | collective-permute-start | bytes 1179656 | tf_op jit(solution)/shard_map/ppermute | solution.py:99
  202.8 22.6 %collective-permute-start.22 = (bf16[128,2048]{1,0:T(8,128)(2,1)S(1)}, bf16[128,2048]{1,0:T(8,128)(2,1)S(1)}, u32[]{:S(2)}, u32[]{:S(2)}) collective-permute-start(bf16[128,2048]{1,0:T(8,128)(2,1)S(1)} %pad_maximum_fusion.11), channel_id=1, source_target_pairs={{0,2},{2,4},{4,6},{6,7},{7,5},{5,3},{3,1},{1,0},{8,10},{10,12},{12... | collective-permute-start | bytes 1572872 | tf_op jit(solution)/shard_map/ppermute | solution.py:99
  203.4 22.0 %collective-permute-start.23 = (bf16[128,2048]{1,0:T(8,128)(2,1)S(1)}, bf16[128,2048]{1,0:T(8,128)(2,1)S(1)}, u32[]{:S(2)}, u32[]{:S(2)}) collective-permute-start(bf16[128,2048]{1,0:T(8,128)(2,1)S(1)} %pad_maximum_fusion.12), channel_id=1, source_target_pairs={{0,1},{2,0},{4,2},{6,4},{7,6},{5,7},{3,5},{1,3},{8,9},{10,8},{12,1... | collective-permute-start | bytes 1572872 | tf_op jit(solution)/shard_map/ppermute | solution.py:99
  205.9 48.4 %collective-permute-start.42 = (bf16[64,3072]{1,0:T(8,128)(2,1)S(1)}, bf16[64,3072]{1,0:T(8,128)(2,1)S(1)}, u32[]{:S(2)}, u32[]{:S(2)}) collective-permute-start(bf16[64,3072]{1,0:T(8,128)(2,1)S(1)} %copy-done.36), channel_id=1, source_target_pairs={{0,2},{2,4},{4,6},{6,7},{7,5},{5,3},{3,1},{1,0},{8,10},{10,12},{12... | collective-permute-start | bytes 1179656 | tf_op jit(solution)/shard_map/ppermute | solution.py:99
  225.7 19.8 %collective-permute-start.24 = (bf16[128,2048]{1,0:T(8,128)(2,1)S(1)}, bf16[128,2048]{1,0:T(8,128)(2,1)S(1)}, u32[]{:S(2)}, u32[]{:S(2)}) collective-permute-start(bf16[128,2048]{1,0:T(8,128)(2,1)S(1)} %get-tuple-element.116), channel_id=1, source_target_pairs={{0,2},{2,4},{4,6},{6,7},{7,5},{5,3},{3,1},{1,0},{8,10},{10,12},{12... | collective-permute-start | bytes 1572872 | tf_op jit(solution)/shard_map/ppermute | solution.py:99
  245.8 19.4 %collective-permute-start.26 = (bf16[128,2048]{1,0:T(8,128)(2,1)S(1)}, bf16[128,2048]{1,0:T(8,128)(2,1)S(1)}, u32[]{:S(2)}, u32[]{:S(2)}) collective-permute-start(bf16[128,2048]{1,0:T(8,128)(2,1)S(1)} %get-tuple-element.118), channel_id=1, source_target_pairs={{0,2},{2,4},{4,6},{6,7},{7,5},{5,3},{3,1},{1,0},{8,10},{10,12},{12... | collective-permute-start | bytes 1572872 | tf_op jit(solution)/shard_map/ppermute | solution.py:99
  254.3 46.1 %collective-permute-start.43 = (bf16[512,2048]{1,0:T(8,128)(2,1)S(1)}, bf16[512,2048]{1,0:T(8,128)(2,1)S(1)}, u32[]{:S(2)}, u32[]{:S(2)}) collective-permute-start(bf16[512,2048]{1,0:T(8,128)(2,1)S(1)} %bitcast.755), channel_id=1, source_target_pairs={{0,16},{8,24},{16,0},{24,8},{1,17},{9,25},{17,1},{25,9},{2,18},{10... | collective-permute-start | bytes 6291464 | tf_op jit(solution)/shard_map/ppermute | solution.py:48
  279.1 22.1 %collective-permute-start.30 = (bf16[128,2048]{1,0:T(8,128)(2,1)S(1)}, bf16[128,2048]{1,0:T(8,128)(2,1)S(1)}, u32[]{:S(2)}, u32[]{:S(2)}) collective-permute-start(bf16[128,2048]{1,0:T(8,128)(2,1)S(1)} %collective-permute-done.28), channel_id=1, source_target_pairs={{0,1},{2,0},{4,2},{6,4},{7,6},{5,7},{3,5},{1,3},{8,9},{10,8},{12,1... | collective-permute-start | bytes 1572872 | tf_op jit(solution)/shard_map/ppermute | solution.py:99
  280.8 20.4 %collective-permute-start.31 = (bf16[128,2048]{1,0:T(8,128)(2,1)S(1)}, bf16[128,2048]{1,0:T(8,128)(2,1)S(1)}, u32[]{:S(2)}, u32[]{:S(2)}) collective-permute-start(bf16[128,2048]{1,0:T(8,128)(2,1)S(1)} %collective-permute-done.29), channel_id=1, source_target_pairs={{0,2},{2,4},{4,6},{6,7},{7,5},{5,3},{3,1},{1,0},{8,10},{10,12},{12... | collective-permute-start | bytes 1572872 | tf_op jit(solution)/shard_map/ppermute | solution.py:99
  301.1 68.6 %collective-permute-start.44 = (bf16[1024,2048]{1,0:T(8,128)(2,1)S(1)}, bf16[1024,2048]{1,0:T(8,128)(2,1)S(1)}, u32[]{:S(2)}, u32[]{:S(2)}) collective-permute-start(bf16[1024,2048]{1,0:T(8,128)(2,1)S(1)} %pad_maximum_fusion), channel_id=1, source_target_pairs={{0,8},{8,0},{16,24},{24,16},{1,9},{9,1},{17,25},{25,17},{2,10},{10... | collective-permute-start | bytes 12582920 | tf_op jit(solution)/shard_map/ppermute | solution.py:48
  301.2 14.3 %collective-permute-start.33 = (bf16[128,2048]{1,0:T(8,128)(2,1)S(1)}, bf16[128,2048]{1,0:T(8,128)(2,1)S(1)}, u32[]{:S(2)}, u32[]{:S(2)}) collective-permute-start(bf16[128,2048]{1,0:T(8,128)(2,1)S(1)} %collective-permute-done.31), channel_id=1, source_target_pairs={{0,2},{2,4},{4,6},{6,7},{7,5},{5,3},{3,1},{1,0},{8,10},{10,12},{12... | collective-permute-start | bytes 1572872 | tf_op jit(solution)/shard_map/ppermute | solution.py:99
  301.2 14.3 %collective-permute-start.32 = (bf16[128,2048]{1,0:T(8,128)(2,1)S(1)}, bf16[128,2048]{1,0:T(8,128)(2,1)S(1)}, u32[]{:S(2)}, u32[]{:S(2)}) collective-permute-start(bf16[128,2048]{1,0:T(8,128)(2,1)S(1)} %collective-permute-done.30), channel_id=1, source_target_pairs={{0,1},{2,0},{4,2},{6,4},{7,6},{5,7},{3,5},{1,3},{8,9},{10,8},{12,1... | collective-permute-start | bytes 1572872 | tf_op jit(solution)/shard_map/ppermute | solution.py:99
  369.7 18.5 %collective-permute-start.45 = (bf16[512,1024]{1,0:T(8,128)(2,1)S(1)}, bf16[512,1024]{1,0:T(8,128)(2,1)S(1)}, u32[]{:S(2)}, u32[]{:S(2)}) collective-permute-start(bf16[512,1024]{1,0:T(8,128)(2,1)S(1)} %bitcast.761), channel_id=1, source_target_pairs={{0,16},{8,24},{16,0},{24,8},{1,17},{9,25},{17,1},{25,9},{2,18},{10... | collective-permute-start | bytes 3145736 | tf_op jit(solution)/shard_map/ppermute | solution.py:48
  388.2 15.8 %collective-permute-start.46 = (bf16[1024,1024]{1,0:T(8,128)(2,1)S(1)}, bf16[1024,1024]{1,0:T(8,128)(2,1)S(1)}, u32[]{:S(2)}, u32[]{:S(2)}) collective-permute-start(bf16[1024,1024]{1,0:T(8,128)(2,1)S(1)} %constant_dynamic-update-slice_fusion.84), channel_id=1, source_target_pairs={{0,8},{8,0},{16,24},{24,16},{1,9},{9,1},{17,25},{25,17},{2,10},{10... | collective-permute-start | bytes 6291464 | tf_op jit(solution)/shard_map/ppermute | solution.py:48
  476.3 41.5 %collective-permute-start.75 = (bf16[1024,1024]{1,0:T(8,128)(2,1)}, bf16[1024,1024]{1,0:T(8,128)(2,1)S(1)}, u32[]{:S(2)}, u32[]{:S(2)}) collective-permute-start(bf16[1024,1024]{1,0:T(8,128)(2,1)} %convolution_convert_fusion.1), channel_id=1, source_target_pairs={{0,8},{8,0},{16,24},{24,16},{1,9},{9,1},{17,25},{25,17},{2,10},{10... | collective-permute-start | bytes 6291464 | tf_op jit(solution)/shard_map/ppermute | solution.py:48
  501.2 59.4 %collective-permute-start.101 = (bf16[1024,2048]{1,0:T(8,128)(2,1)S(1)}, bf16[1024,2048]{1,0:T(8,128)(2,1)}, u32[]{:S(2)}, u32[]{:S(2)}) collective-permute-start(bf16[1024,2048]{1,0:T(8,128)(2,1)S(1)} %convolution_convert_fusion), channel_id=1, source_target_pairs={{0,8},{8,0},{16,24},{24,16},{1,9},{9,1},{17,25},{25,17},{2,10},{10... | collective-permute-start | bytes 12582920 | tf_op jit(solution)/shard_map/ppermute | solution.py:48
  501.2 14.3 %collective-permute-start.67 = (bf16[128,2048]{1,0:T(8,128)(2,1)S(1)}, bf16[128,2048]{1,0:T(8,128)(2,1)S(1)}, u32[]{:S(2)}, u32[]{:S(2)}) collective-permute-start(bf16[128,2048]{1,0:T(8,128)(2,1)S(1)} %fusion.32), channel_id=1, source_target_pairs={{0,2},{2,4},{4,6},{6,7},{7,5},{5,3},{3,1},{1,0},{8,10},{10,12},{12... | collective-permute-start | bytes 1572872 | tf_op jit(solution)/shard_map/ppermute | solution.py:99
  520.4 24.2 %collective-permute-start.76 = (bf16[512,1024]{1,0:T(8,128)(2,1)S(1)}, bf16[512,1024]{1,0:T(8,128)(2,1)S(1)}, u32[]{:S(2)}, u32[]{:S(2)}) collective-permute-start(bf16[512,1024]{1,0:T(8,128)(2,1)S(1)} %slice.1943), channel_id=1, source_target_pairs={{0,16},{8,24},{16,0},{24,8},{1,17},{9,25},{17,1},{25,9},{2,18},{10... | collective-permute-start | bytes 3145736 | tf_op jit(solution)/shard_map/ppermute | solution.py:48
  570.2 76.4 %collective-permute-start.102 = (bf16[512,2048]{1,0:T(8,128)(2,1)}, bf16[512,2048]{1,0:T(8,128)(2,1)}, u32[]{:S(2)}, u32[]{:S(2)}) collective-permute-start(bf16[512,2048]{1,0:T(8,128)(2,1)} %slice.1942), channel_id=1, source_target_pairs={{0,16},{8,24},{16,0},{24,8},{1,17},{9,25},{17,1},{25,9},{2,18},{10... | collective-permute-start | bytes 6291464 | tf_op jit(solution)/shard_map/ppermute | solution.py:48
  583.6 27.6 %collective-permute-start.110 = (bf16[64,1024]{1,0:T(8,128)(2,1)}, bf16[64,1024]{1,0:T(8,128)(2,1)}, u32[]{:S(2)}, u32[]{:S(2)}) collective-permute-start(bf16[64,1024]{1,0:T(8,128)(2,1)} %get-tuple-element.190), channel_id=1, source_target_pairs={{0,1},{2,0},{4,2},{6,4},{7,6},{5,7},{3,5},{1,3},{8,9},{10,8},{12,1... | collective-permute-start | bytes 393224 | tf_op jit(solution)/shard_map/ppermute | solution.py:99
  585.1 29.5 %collective-permute-start.111 = (bf16[64,1024]{1,0:T(8,128)(2,1)}, bf16[64,1024]{1,0:T(8,128)(2,1)}, u32[]{:S(2)}, u32[]{:S(2)}) collective-permute-start(bf16[64,1024]{1,0:T(8,128)(2,1)} %get-tuple-element.191), channel_id=1, source_target_pairs={{0,3},{2,1},{4,0},{6,2},{7,4},{5,6},{3,7},{1,5},{8,11},{10,9},{12,... | collective-permute-start | bytes 393224 | tf_op jit(solution)/shard_map/ppermute | solution.py:99
  585.5 32.4 %collective-permute-start.112 = (bf16[64,1024]{1,0:T(8,128)(2,1)}, bf16[64,1024]{1,0:T(8,128)(2,1)}, u32[]{:S(2)}, u32[]{:S(2)}) collective-permute-start(bf16[64,1024]{1,0:T(8,128)(2,1)} %get-tuple-element.192), channel_id=1, source_target_pairs={{0,5},{2,3},{4,1},{6,0},{7,2},{5,4},{3,6},{1,7},{8,13},{10,11},{12... | collective-permute-start | bytes 393224 | tf_op jit(solution)/shard_map/ppermute | solution.py:99
  605.1 126.2 %collective-permute-start.89 = (bf16[1024,768]{1,0:T(8,128)(2,1)S(1)}, bf16[1024,768]{1,0:T(8,128)(2,1)S(1)}, u32[]{:S(2)}, u32[]{:S(2)}) collective-permute-start(bf16[1024,768]{1,0:T(8,128)(2,1)S(1)} %convolution_convert_fusion.2), channel_id=1, source_target_pairs={{0,8},{8,0},{16,24},{24,16},{1,9},{9,1},{17,25},{25,17},{2,10},{10... | collective-permute-start | bytes 4718600 | tf_op jit(solution)/shard_map/ppermute | solution.py:48
  620.4 91.0 %collective-permute-start.116 = (bf16[64,1024]{1,0:T(8,128)(2,1)S(1)}, bf16[64,1024]{1,0:T(8,128)(2,1)S(1)}, u32[]{:S(2)}, u32[]{:S(2)}) collective-permute-start(bf16[64,1024]{1,0:T(8,128)(2,1)S(1)} %get-tuple-element.196), channel_id=1, source_target_pairs={{0,2},{2,4},{4,6},{6,7},{7,5},{5,3},{3,1},{1,0},{8,10},{10,12},{12... | collective-permute-start | bytes 393224 | tf_op jit(solution)/shard_map/ppermute | solution.py:99
  644.3 14.8 %collective-permute-start.84 = (bf16[128,2048]{1,0:T(8,128)(2,1)S(1)}, bf16[128,2048]{1,0:T(8,128)(2,1)S(1)}, u32[]{:S(2)}, u32[]{:S(2)}) collective-permute-start(bf16[128,2048]{1,0:T(8,128)(2,1)S(1)} %pad_maximum_fusion.20), channel_id=1, source_target_pairs={{0,1},{2,0},{4,2},{6,4},{7,6},{5,7},{3,5},{1,3},{8,9},{10,8},{12,1... | collective-permute-start | bytes 1572872 | tf_op jit(solution)/shard_map/ppermute | solution.py:99
  644.9 14.3 %collective-permute-start.83 = (bf16[128,2048]{1,0:T(8,128)(2,1)S(1)}, bf16[128,2048]{1,0:T(8,128)(2,1)S(1)}, u32[]{:S(2)}, u32[]{:S(2)}) collective-permute-start(bf16[128,2048]{1,0:T(8,128)(2,1)S(1)} %pad_maximum_fusion.19), channel_id=1, source_target_pairs={{0,2},{2,4},{4,6},{6,7},{7,5},{5,3},{3,1},{1,0},{8,10},{10,12},{12... | collective-permute-start | bytes 1572872 | tf_op jit(solution)/shard_map/ppermute | solution.py:99
  659.2 30.7 %collective-permute-start.104 = (bf16[64,2048]{1,0:T(8,128)(2,1)S(1)}, bf16[64,2048]{1,0:T(8,128)(2,1)S(1)}, u32[]{:S(2)}, u32[]{:S(2)}) collective-permute-start(bf16[64,2048]{1,0:T(8,128)(2,1)S(1)} %get-tuple-element.184), channel_id=1, source_target_pairs={{0,3},{2,1},{4,0},{6,2},{7,4},{5,6},{3,7},{1,5},{8,11},{10,9},{12,... | collective-permute-start | bytes 786440 | tf_op jit(solution)/shard_map/ppermute | solution.py:99
  659.3 30.6 %collective-permute-start.105 = (bf16[64,2048]{1,0:T(8,128)(2,1)S(1)}, bf16[64,2048]{1,0:T(8,128)(2,1)S(1)}, u32[]{:S(2)}, u32[]{:S(2)}) collective-permute-start(bf16[64,2048]{1,0:T(8,128)(2,1)S(1)} %get-tuple-element.185), channel_id=1, source_target_pairs={{0,5},{2,3},{4,1},{6,0},{7,2},{5,4},{3,6},{1,7},{8,13},{10,11},{12... | collective-permute-start | bytes 786440 | tf_op jit(solution)/shard_map/ppermute | solution.py:99
  666.7 31.1 %collective-permute-start.106 = (bf16[64,2048]{1,0:T(8,128)(2,1)S(1)}, bf16[64,2048]{1,0:T(8,128)(2,1)S(1)}, u32[]{:S(2)}, u32[]{:S(2)}) collective-permute-start(bf16[64,2048]{1,0:T(8,128)(2,1)S(1)} %get-tuple-element.186), channel_id=1, source_target_pairs={{0,7},{2,5},{4,3},{6,1},{7,0},{5,2},{3,4},{1,6},{8,15},{10,13},{12... | collective-permute-start | bytes 786440 | tf_op jit(solution)/shard_map/ppermute | solution.py:99
  689.8 15.4 %collective-permute-start.107 = (bf16[64,2048]{1,0:T(8,128)(2,1)S(1)}, bf16[64,2048]{1,0:T(8,128)(2,1)S(1)}, u32[]{:S(2)}, u32[]{:S(2)}) collective-permute-start(bf16[64,2048]{1,0:T(8,128)(2,1)S(1)} %get-tuple-element.187), channel_id=1, source_target_pairs={{0,6},{2,7},{4,5},{6,3},{7,1},{5,0},{3,2},{1,4},{8,14},{10,15},{12... | collective-permute-start | bytes 786440 | tf_op jit(solution)/shard_map/ppermute | solution.py:99
  689.9 17.6 %collective-permute-start.108 = (bf16[64,2048]{1,0:T(8,128)(2,1)S(1)}, bf16[64,2048]{1,0:T(8,128)(2,1)S(1)}, u32[]{:S(2)}, u32[]{:S(2)}) collective-permute-start(bf16[64,2048]{1,0:T(8,128)(2,1)S(1)} %get-tuple-element.188), channel_id=1, source_target_pairs={{0,4},{2,6},{4,7},{6,5},{7,3},{5,1},{3,0},{1,2},{8,12},{10,14},{12... | collective-permute-start | bytes 786440 | tf_op jit(solution)/shard_map/ppermute | solution.py:99
  707.4 21.4 %collective-permute-start.86 = (bf16[128,2048]{1,0:T(8,128)(2,1)S(1)}, bf16[128,2048]{1,0:T(8,128)(2,1)S(1)}, u32[]{:S(2)}, u32[]{:S(2)}) collective-permute-start(bf16[128,2048]{1,0:T(8,128)(2,1)S(1)} %fusion.38), channel_id=1, source_target_pairs={{0,1},{2,0},{4,2},{6,4},{7,6},{5,7},{3,5},{1,3},{8,9},{10,8},{12,1... | collective-permute-start | bytes 1572872 | tf_op jit(solution)/shard_map/ppermute | solution.py:99
  711.4 17.6 %collective-permute-start.85 = (bf16[128,2048]{1,0:T(8,128)(2,1)S(1)}, bf16[128,2048]{1,0:T(8,128)(2,1)S(1)}, u32[]{:S(2)}, u32[]{:S(2)}) collective-permute-start(bf16[128,2048]{1,0:T(8,128)(2,1)S(1)} %fusion.37), channel_id=1, source_target_pairs={{0,2},{2,4},{4,6},{6,7},{7,5},{5,3},{3,1},{1,0},{8,10},{10,12},{12... | collective-permute-start | bytes 1572872 | tf_op jit(solution)/shard_map/ppermute | solution.py:99
  733.3 16.6 %collective-permute-start.90 = (bf16[512,768]{1,0:T(8,128)(2,1)S(1)}, bf16[512,768]{1,0:T(8,128)(2,1)S(1)}, u32[]{:S(2)}, u32[]{:S(2)}) collective-permute-start(bf16[512,768]{1,0:T(8,128)(2,1)S(1)} %slice.1944), channel_id=1, source_target_pairs={{0,16},{8,24},{16,0},{24,8},{1,17},{9,25},{17,1},{25,9},{2,18},{10... | collective-permute-start | bytes 2359304 | tf_op jit(solution)/shard_map/ppermute | solution.py:48
  (151 other events, 2793.3 us)

commit v3 on v2

--- a/solution.py
+++ b/solution.py
@@ -62,10 +62,10 @@
         blocks = [parts[self.order.index(k)] for k in range(self.count)]
         return jnp.concatenate(self.relative(blocks), axis=1)
 
-    def gather(self, block, done=()):
+    def gather(self, block, done=(), later=()):
         (value,) = tie([block], done)
         for bit in self.bits[1:]:
-            value = jnp.concatenate([value, self.swap(value, bit)], axis=0)
+            value = jnp.concatenate([value, *tie([self.swap(value, bit)], later)], axis=0)
         return value, self.swap(value, 1)
 
     def scatter_sum(self, kept, given):
@@ -81,16 +81,17 @@
     def __init__(self, size):
         self.size = size
         self.order = list(range(0, size, 2)) + list(range(size - 1, 0, -2))
-        places = [self.order.index(i) for i in range(size)]
-        self.place = jnp.array(places, jnp.int32)[lax.axis_index("ctx")]
-        self.table = jnp.array(self.order, jnp.int32)
+        index = lax.axis_index("ctx")
+        self.place = jnp.where(index % 2 == 0, index // 2, size - (index + 1) // 2)
         self.done = ()
+        self.steps = []
 
     def owner(self, ahead):
-        return self.table[lax.rem(self.place + ahead + self.size, self.size)]
+        place = lax.rem(self.place + ahead, self.size)
+        return jnp.where(place < self.size // 2, 2 * place, 2 * (self.size - place) - 1)
 
     def owners(self):
-        return jnp.roll(jnp.concatenate([self.table, self.table]), -self.place)[: self.size]
+        return self.owner(jnp.arange(self.size, dtype=jnp.int32))
 
     def shift(self, value, by):
         pairs = [
@@ -102,6 +103,7 @@
         right, left = tie((right, left), (*self.done, *done))
         right, left = self.shift(right, 1), self.shift(left, -1)
         self.done = (right, left)
+        self.steps.append(self.done)
         return right, left
 
     def gather(self, value, fill=()):
@@ -424,17 +426,17 @@
     normed_one, factor_one = normalize(block_in)
     grad_out = shares.to_order(cotangent.reshape(rows, width)).astype(F32) * valid
 
+    to_shares = [(i * size + j, j * count + i) for i in range(count) for j in range(size)]
+    from_shares = [(there, here) for here, there in to_shares]
     attn_pieces = send_columns([scaled(w, gain_one) for w in (query_weight, key_weight, value_weight)])
+    mix_share = lax.ppermute(mix_weight, ("dp", "ctx"), from_shares)
     one_pieces = ring.gather(normed_one.astype(BF16))
     one_all = halves(one_pieces)
     attn_weights = shares.gather(placed(attn_pieces))
-    to_shares = [(i * size + j, j * count + i) for i in range(count) for j in range(size)]
-    from_shares = [(there, here) for here, there in to_shares]
-    (mix_sent,) = tie([mix_weight], ring.done)
-    mix_parts = shares.gather(lax.ppermute(mix_sent, ("dp", "ctx"), from_shares))
     ffn_pieces = send_columns(
-        [scaled(gate_weight, gain_two), scaled(up_weight, gain_two), down_weight], ring.done
-    )
+        [scaled(gate_weight, gain_two), scaled(up_weight, gain_two)], ring.steps[-2]
+    )
+    mix_parts = shares.gather(mix_share, attn_weights[1:])
     mix_blocks = jnp.split(jnp.concatenate(mix_parts, axis=0), count, axis=0)
     mix_rows = shares.to_order(
         jnp.concatenate(
@@ -448,18 +450,22 @@
     attn_out = contract(mixed, mix_rows, 1, 0)
     residual = block_in + ring.scatter_sum(attn_out[:, : width // 2], attn_out[:, width // 2 :])
 
-    ffn_weights = shares.gather(placed([p[:, : 2 * hidden_local] for p in ffn_pieces]))
-    down_weights = shares.gather(
-        placed([p[:, 2 * hidden_local :] for p in ffn_pieces]), [ffn_weights[1]]
-    )
+    down_pieces = send_columns([down_weight], ring.steps[-2])
     normed_two, factor_two = normalize(residual)
     two_all = halves(ring.gather(normed_two.astype(BF16)))
-    grad_all = halves(ring.gather(grad_out.astype(BF16)))
-    gate_up = apply(two_all, ffn_weights)
+    ffn_weights = shares.gather(placed(ffn_pieces), later=ring.steps[-2])
+    low_part = contract(two_all[0], ffn_weights[0], 1, 0)
+    gate_up = low_part + contract(two_all[1], ffn_weights[1], 1, 0)
     gate, up = gate_up[:, :hidden_local], gate_up[:, hidden_local:]
     sigma = jax.nn.sigmoid(gate)
     silu_gate = gate * sigma
     hidden = (silu_gate * up).astype(BF16)
+    grad_all = halves(
+        ring.gather(grad_out.astype(BF16), fill=((), (low_part,), (gate_up,), (hidden,)))
+    )
+    down_weights = shares.gather(
+        placed(tie(down_pieces, ring.steps[-4])), ffn_weights[1:], later=(hidden,)
+    )
     branch = ring.scatter_sum(*(contract(hidden, w, 1, 1) for w in down_weights))
     activations = valid * (residual + branch)
 
@@ -506,7 +512,6 @@
     )
     attn_given, attn_total = summed(one_all, projected_grad)
     attn_sum = attn_total()
-    attn_pieces = send_rows(attn_sum)
     mix_terms = shares.from_order(contract(mixed, dres_all, 0, 0))
     mix_blocks = shares.relative(jnp.split(mix_terms, count, axis=0))
     mix_blocks = [mix_blocks[k] for k in shares.order]
@@ -521,11 +526,13 @@
     input_grad = dres + factor_one * (
         scaled_one - normed_one * jnp.mean(normed_one * scaled_one, axis=-1, keepdims=True)
     )
+    attn_pieces = send_rows(attn_sum, ring.steps[-2])
     mix_grad = lax.ppermute(mix_sum, ("dp", "ctx"), to_shares).astype(F32)
 
     def joined(pieces, columns):
         return join_columns(ring.place_in_order([p[:, columns] for p in pieces])).astype(F32)
 
+    down_pieces, both_pieces = (tie(p, ring.done) for p in (down_pieces, both_pieces))
     down_grad = joined(down_pieces, slice(None))
     gate_raw = joined(both_pieces, slice(0, hidden_local))
     up_raw = joined(both_pieces, slice(hidden_local, 2 * hidden_local))

time: 784 us -> 709 us (0.904)
  waiting for transfers between devices: 348 us -> 287 us
  between operations: 26.3 us -> 4.5 us
  starting transfers between devices: 209 us -> 218 us
    ppermute x16, waiting for transfers between devices: 60.9 us -> 19.2 us  [swap(): return lax.ppermute(value, 'dp', [(i, i ^ bit) for i in range(self.count)])]
    ppermute x99 -> x106, starting transfers between devices: 187 us -> 207 us  [shift(): return lax.ppermute(value, 'ctx', pairs)]
    ppermute x99 -> x106, waiting for transfers between devices: 287 us -> 267 us  [shift(): return lax.ppermute(value, 'ctx', pairs)]
    ppermute x16, starting transfers between devices: 21.1 us -> 8.63 us  [swap(): return lax.ppermute(value, 'dp', [(i, i ^ bit) for i in range(self.count)])]
    dynamic_update_slice x48, local copies, waits for them, and re-layouts: 15.3 us -> 7.25 us  [place_in_order(): lax.dynamic_update_index_in_dim(out, pieces[ahead], self.owner(ahead), 0)]
    unnamed x280 -> x292, local copies, waits for them, and re-layouts: 13.7 us -> 20 us
  transfers between devices with their start and end apart: 117 -> 124, of which waited for: 67 -> 61; matrix products, arithmetic and copies ran while one was open for 18% -> 22% of each run, Pallas kernels for 3% -> 3%
where the time goes in v3:
time: 709 us; the launch traced here: 704 us
  waiting for transfers between devices  287 us (40%)
  starting transfers between devices  218 us (31%)
  matrix products  86.9 us (12%)
  local copies, waits for them, and re-layouts  46.5 us (7%)
  other arithmetic  37.9 us (5%)
  Pallas kernels  23.7 us (3%)
    ppermute x106, waiting for transfers between devices, shift(): return lax.ppermute(value, 'ctx', pairs)  267 us
    ppermute x106, starting transfers between devices, shift(): return lax.ppermute(value, 'ctx', pairs)  207 us
    dot_general x21, matrix products, contract(): lax.dot_general(left, right, (((left_dim,), (right_dim,)), ((), ())), pre...  86.9 us
    unnamed x292, local copies, waits for them, and re-layouts  20 us
    ppermute x16, waiting for transfers between devices, swap(): return lax.ppermute(value, 'dp', [(i, i ^ bit) for i in range(self.count)])  19.2 us
  transfers between devices with their start and end apart: 124, of which 61 were waited for; matrix products, arithmetic and copies ran while one was open for 22% of the time, Pallas kernels for 3%

profile of v3, /device:TPU:0, one launch (start us, length us, event | category | flops | bytes accessed | tf_op | source)
XLA Modules:
  0.0 703.7 jit_solution(7018393728846994081)
XLA Ops:
  22.4 5.6 collective-permute-start.11
  50.0 15.7 %collective-permute-done.2 = bf16[128,2048]{1,0:T(8,128)(2,1)} collective-permute-done((bf16[128,2048]{1,0:T(8,128)(2,1)}, bf16[128,2048]{1,0:T(8,128)(2,1)}, u32[]{:S(2)}, u32[]{:S(2)}) %collective-permute-start.2) | collective-permute-done | bytes 524320 | tf_op jit(solution)/shard_map/ppermute | solution.py:100
  99.6 5.0 collective-permute-start.39
  112.5 4.6 convolution_add_fusion.2
  118.6 10.7 %attention_forward.1 = (bf16[8,2,64,256]{3,2,1,0:T(8,128)(2,1)}, bf16[8,2,64,256]{3,2,1,0:T(8,128)(2,1)}, bf16[8,2,64,256]{3,2,1,0:T(8,128)(2,1)}, bf16[8,2,64,256]{3,2,1,0:T(8,128)(2,1)}, f32[2,512,4]{2,1,0:T(8,128)}) custom-call(s32[2]{0:T(128)} %lengths_ref.3, f32[8,2,64,768]{3,2,1,0:T(8,128)} %bitcast.694, f32[8,2,64,768]{3,2,1,0:T(8,128)} %bitcast.695, ...), custom_call_target="tpu_custom_call" | custom-call | flops 536870912 | bytes 4194304 | tf_op jit(solution)/shard_map/attention_forward/pallas_call | solution.py:342
  136.0 5.7 collective-permute-done.21
  147.5 8.0 %collective-permute-done.23 = bf16[128,2048]{1,0:T(8,128)(2,1)S(1)} collective-permute-done((bf16[128,2048]{1,0:T(8,128)(2,1)S(1)}, bf16[128,2048]{1,0:T(8,128)(2,1)S(1)}, u32[]{:S(2)}, u32[]{:S(2)}) %collective-permute-start.23) | collective-permute-done | bytes 524320 | tf_op jit(solution)/shard_map/ppermute | solution.py:100
  155.5 6.5 collective-permute-start.42
  163.1 5.9 collective-permute-start.25
  172.9 8.7 %collective-permute-done.25 = bf16[128,2048]{1,0:T(8,128)(2,1)S(1)} collective-permute-done((bf16[128,2048]{1,0:T(8,128)(2,1)S(1)}, bf16[128,2048]{1,0:T(8,128)(2,1)S(1)}, u32[]{:S(2)}, u32[]{:S(2)}) %collective-permute-start.25) | collective-permute-done | bytes 524320 | tf_op jit(solution)/shard_map/ppermute | solution.py:100
  181.7 5.3 collective-permute-done.24
  187.3 9.7 %collective-permute-start.27 = (bf16[128,2048]{1,0:T(8,128)(2,1)S(1)}, bf16[128,2048]{1,0:T(8,128)(2,1)S(1)}, u32[]{:S(2)}, u32[]{:S(2)}) collective-permute-start(bf16[128,2048]{1,0:T(8,128)(2,1)S(1)} %get-tuple-element.159), channel_id=1, source_target_pairs={{0,1},{2,0},{4,2},{6,4},{7,6},{5,7},{3,5},{1,3},{8,9},{10,8},{12,1... | collective-permute-start | bytes 1572872 | tf_op jit(solution)/shard_map/ppermute | solution.py:100
  197.1 11.2 %collective-permute-done.27 = bf16[128,2048]{1,0:T(8,128)(2,1)S(1)} collective-permute-done((bf16[128,2048]{1,0:T(8,128)(2,1)S(1)}, bf16[128,2048]{1,0:T(8,128)(2,1)S(1)}, u32[]{:S(2)}, u32[]{:S(2)}) %collective-permute-start.27) | collective-permute-done | bytes 524320 | tf_op jit(solution)/shard_map/ppermute | solution.py:100
  215.3 9.7 %collective-permute-done.29 = bf16[128,2048]{1,0:T(8,128)(2,1)} collective-permute-done((bf16[128,2048]{1,0:T(8,128)(2,1)}, bf16[128,2048]{1,0:T(8,128)(2,1)}, u32[]{:S(2)}, u32[]{:S(2)}) %collective-permute-start.29) | collective-permute-done | bytes 524320 | tf_op jit(solution)/shard_map/ppermute | solution.py:100
  232.6 5.4 collective-permute-done.31
  246.1 4.8 collective-permute-done.33
  250.9 6.5 collective-permute-done.32
  272.1 8.4 %collective-permute-done.47 = bf16[64,1024]{1,0:T(8,128)(2,1)S(1)} collective-permute-done((bf16[64,1024]{1,0:T(8,128)(2,1)S(1)}, bf16[64,1024]{1,0:T(8,128)(2,1)S(1)}, u32[]{:S(2)}, u32[]{:S(2)}) %collective-permute-start.47) | collective-permute-done | bytes 131104 | tf_op jit(solution)/shard_map/ppermute | solution.py:100
  280.5 10.5 %collective-permute-start.49 = (bf16[64,1024]{1,0:T(8,128)(2,1)S(1)}, bf16[64,1024]{1,0:T(8,128)(2,1)S(1)}, u32[]{:S(2)}, u32[]{:S(2)}) collective-permute-start(bf16[64,1024]{1,0:T(8,128)(2,1)S(1)} %get-tuple-element.180), channel_id=1, source_target_pairs={{0,6},{2,7},{4,5},{6,3},{7,1},{5,0},{3,2},{1,4},{8,14},{10,15},{12... | collective-permute-start | bytes 393224 | tf_op jit(solution)/shard_map/ppermute | solution.py:100
  291.6 8.2 %fusion.106 = f32[1024,2048]{1,0:T(8,128)} fusion(bf16[1024,1024]{1,0:T(8,128)(2,1)S(1)} %get-tuple-element.441, bf16[512,2048]{1,0:T(8,128)(2,1)} %collective-permute-done.43, bf16[512,2048]{1,0:T(8,128)(2,1)S(1)} %bitcast.700), kind=kOutput, calls=%fused_computation.656 | convolution fusion | flops 4303355904 | bytes 14680064 | tf_op jit(solution)/shard_map/dot_general | solution.py:25
  302.3 6.8 collective-permute-done.57
  311.1 6.9 convolution_add_fusion
  321.5 10.0 %collective-permute-done.58 = bf16[128,2048]{1,0:T(8,128)(2,1)S(1)} collective-permute-done((bf16[128,2048]{1,0:T(8,128)(2,1)S(1)}, bf16[128,2048]{1,0:T(8,128)(2,1)S(1)}, u32[]{:S(2)}, u32[]{:S(2)}) %collective-permute-start.58) | collective-permute-done | bytes 524320 | tf_op jit(solution)/shard_map/ppermute | solution.py:100
  355.6 6.4 multiply_convert_fusion.1
  368.0 6.4 fusion.122
  382.5 6.7 fusion.121
  399.0 8.2 %collective-permute-done.71 = bf16[128,1024]{1,0:T(8,128)(2,1)S(1)} collective-permute-done((bf16[128,1024]{1,0:T(8,128)(2,1)S(1)}, bf16[128,1024]{1,0:T(8,128)(2,1)S(1)}, u32[]{:S(2)}, u32[]{:S(2)}) %collective-permute-start.71) | collective-permute-done | bytes 262176 | tf_op jit(solution)/shard_map/ppermute | solution.py:100
  409.7 7.0 convolution_convert_fusion
  416.7 4.7 collective-permute-done.72
  425.4 10.6 %collective-permute-done.74 = bf16[128,2048]{1,0:T(8,128)(2,1)S(1)} collective-permute-done((bf16[128,2048]{1,0:T(8,128)(2,1)S(1)}, bf16[128,2048]{1,0:T(8,128)(2,1)S(1)}, u32[]{:S(2)}, u32[]{:S(2)}) %collective-permute-start.74) | collective-permute-done | bytes 524320 | tf_op jit(solution)/shard_map/ppermute | solution.py:100
  444.4 8.4 %collective-permute-done.77 = bf16[128,2048]{1,0:T(8,128)(2,1)S(1)} collective-permute-done((bf16[128,2048]{1,0:T(8,128)(2,1)S(1)}, bf16[128,2048]{1,0:T(8,128)(2,1)S(1)}, u32[]{:S(2)}, u32[]{:S(2)}) %collective-permute-start.77) | collective-permute-done | bytes 524320 | tf_op jit(solution)/shard_map/ppermute | solution.py:100
  456.9 11.5 %collective-permute-done.83 = bf16[512,1024]{1,0:T(8,128)(2,1)S(1)} collective-permute-done((bf16[512,1024]{1,0:T(8,128)(2,1)S(1)}, bf16[512,1024]{1,0:T(8,128)(2,1)S(1)}, u32[]{:S(2)}, u32[]{:S(2)}) %collective-permute-start.83) | collective-permute-done | bytes 1048608 | tf_op jit(solution)/shard_map/ppermute | solution.py:48
  472.6 8.3 %collective-permute-done.80 = bf16[128,2048]{1,0:T(8,128)(2,1)S(1)} collective-permute-done((bf16[128,2048]{1,0:T(8,128)(2,1)S(1)}, bf16[128,2048]{1,0:T(8,128)(2,1)S(1)}, u32[]{:S(2)}, u32[]{:S(2)}) %collective-permute-start.80) | collective-permute-done | bytes 524320 | tf_op jit(solution)/shard_map/ppermute | solution.py:100
  483.2 6.7 convert_add_fusion
  506.8 13.0 %attention_backward.1 = (bf16[8,2,64,256]{3,2,1,0:T(8,128)(2,1)}, bf16[8,2,64,256]{3,2,1,0:T(8,128)(2,1)}, bf16[8,2,64,256]{3,2,1,0:T(8,128)(2,1)}) custom-call(s32[2]{0:T(128)} %lengths_ref.3, bf16[8,2,64,256]{3,2,1,0:T(8,128)(2,1)} %get-tuple-element.217.q_ref, bf16[8,2,64,256]{3,2,1,0:T(8,128)(2,1)} %get-tuple-element.218.k_ref, ...), custom_call_target="tpu_custom_call" | custom-call | flops 1342177280 | bytes 4194304 | tf_op jit(solution)/shard_map/attention_backward/pallas_call | solution.py:364
  532.1 6.1 collective-permute-done.88
  544.2 8.1 %collective-permute-done.90 = bf16[128,2048]{1,0:T(8,128)(2,1)S(1)} collective-permute-done((bf16[128,2048]{1,0:T(8,128)(2,1)S(1)}, bf16[128,2048]{1,0:T(8,128)(2,1)S(1)}, u32[]{:S(2)}, u32[]{:S(2)}) %collective-permute-start.90) | collective-permute-done | bytes 524320 | tf_op jit(solution)/shard_map/ppermute | solution.py:100
  556.6 5.3 collective-permute-start.110
  561.9 23.2 %collective-permute-start.111 = (bf16[64,2048]{1,0:T(8,128)(2,1)S(1)}, bf16[64,2048]{1,0:T(8,128)(2,1)S(1)}, u32[]{:S(2)}, u32[]{:S(2)}) collective-permute-start(bf16[64,2048]{1,0:T(8,128)(2,1)S(1)} %get-tuple-element.248), channel_id=1, source_target_pairs={{0,3},{2,1},{4,0},{6,2},{7,4},{5,6},{3,7},{1,5},{8,11},{10,9},{12,... | collective-permute-start | bytes 786440 | tf_op jit(solution)/shard_map/ppermute | solution.py:100
  586.2 4.6 collective-permute-start.113
  590.9 15.3 %collective-permute-done.110 = bf16[64,2048]{1,0:T(8,128)(2,1)S(1)} collective-permute-done((bf16[64,2048]{1,0:T(8,128)(2,1)S(1)}, bf16[64,2048]{1,0:T(8,128)(2,1)S(1)}, u32[]{:S(2)}, u32[]{:S(2)}) %collective-permute-start.110) | collective-permute-done | bytes 262176 | tf_op jit(solution)/shard_map/ppermute | solution.py:100
  619.7 4.7 collective-permute-done.114
  630.5 4.6 collective-permute-start.119
  636.1 9.7 %collective-permute-done.94 = bf16[128,2048]{1,0:T(8,128)(2,1)S(1)} collective-permute-done((bf16[128,2048]{1,0:T(8,128)(2,1)S(1)}, bf16[128,2048]{1,0:T(8,128)(2,1)S(1)}, u32[]{:S(2)}, u32[]{:S(2)}) %collective-permute-start.94) | collective-permute-done | bytes 524320 | tf_op jit(solution)/shard_map/ppermute | solution.py:100
  645.8 6.9 collective-permute-start.121
  656.8 6.4 collective-permute-start.97
  686.1 8.6 %collective-permute-done.99 = bf16[64,768]{1,0:T(8,128)(2,1)S(1)} collective-permute-done((bf16[64,768]{1,0:T(8,128)(2,1)S(1)}, bf16[64,768]{1,0:T(8,128)(2,1)S(1)}, u32[]{:S(2)}, u32[]{:S(2)}) %collective-permute-start.99) | collective-permute-done | bytes 98336 | tf_op jit(solution)/shard_map/ppermute | solution.py:100
  694.8 4.8 collective-permute-done.102
  (713 shorter events, 313.1 us)
Async XLA Ops:
  3.5 40.8 %collective-permute-start = (bf16[128,2048]{1,0:T(8,128)(2,1)}, bf16[128,2048]{1,0:T(8,128)(2,1)}, u32[]{:S(2)}, u32[]{:S(2)}) collective-permute-start(bf16[128,2048]{1,0:T(8,128)(2,1)} %fusion.10), channel_id=1, source_target_pairs={{0,1},{2,0},{4,2},{6,4},{7,6},{5,7},{3,5},{1,3},{8,9},{10,8},{12,1... | collective-permute-start | bytes 1572872 | tf_op jit(solution)/shard_map/ppermute | solution.py:100
  6.5 37.8 %collective-permute-start.1 = (bf16[128,2048]{1,0:T(8,128)(2,1)}, bf16[128,2048]{1,0:T(8,128)(2,1)}, u32[]{:S(2)}, u32[]{:S(2)}) collective-permute-start(bf16[128,2048]{1,0:T(8,128)(2,1)} %fusion.10), channel_id=1, source_target_pairs={{0,2},{2,4},{4,6},{6,7},{7,5},{5,3},{3,1},{1,0},{8,10},{10,12},{12... | collective-permute-start | bytes 1572872 | tf_op jit(solution)/shard_map/ppermute | solution.py:100
  11.1 20.6 %collective-permute-start.9 = (bf16[64,768]{1,0:T(8,128)(2,1)}, bf16[64,768]{1,0:T(8,128)(2,1)}, u32[]{:S(2)}, u32[]{:S(2)}) collective-permute-start(bf16[64,768]{1,0:T(8,128)(2,1)} %get-tuple-element.409), channel_id=1, source_target_pairs={{0,3},{2,1},{4,0},{6,2},{7,4},{5,6},{3,7},{1,5},{8,11},{10,9},{12,... | collective-permute-start | bytes 294920 | tf_op jit(solution)/shard_map/ppermute | solution.py:100
  13.7 19.0 %collective-permute-start.10 = (bf16[64,768]{1,0:T(8,128)(2,1)}, bf16[64,768]{1,0:T(8,128)(2,1)}, u32[]{:S(2)}, u32[]{:S(2)}) collective-permute-start(bf16[64,768]{1,0:T(8,128)(2,1)} %get-tuple-element.408), channel_id=1, source_target_pairs={{0,5},{2,3},{4,1},{6,0},{7,2},{5,4},{3,6},{1,7},{8,13},{10,11},{12... | collective-permute-start | bytes 294920 | tf_op jit(solution)/shard_map/ppermute | solution.py:100
  42.7 56.9 %collective-permute-start.17 = (bf16[64,2048]{1,0:T(8,128)(2,1)}, bf16[64,2048]{1,0:T(8,128)(2,1)S(1)}, u32[]{:S(2)}, u32[]{:S(2)}) collective-permute-start(bf16[64,2048]{1,0:T(8,128)(2,1)} %param.18), channel_id=1, source_target_pairs={{0,0},{4,1},{8,2},{12,3},{16,4},{20,5},{24,6},{28,7},{1,8},{5,9},{... | collective-permute-start | bytes 786440 | tf_op jit(solution)/shard_map/ppermute | solution.py:432
  44.3 21.3 %collective-permute-start.2 = (bf16[128,2048]{1,0:T(8,128)(2,1)}, bf16[128,2048]{1,0:T(8,128)(2,1)}, u32[]{:S(2)}, u32[]{:S(2)}) collective-permute-start(bf16[128,2048]{1,0:T(8,128)(2,1)} %collective-permute-done), channel_id=1, source_target_pairs={{0,1},{2,0},{4,2},{6,4},{7,6},{5,7},{3,5},{1,3},{8,9},{10,8},{12,1... | collective-permute-start | bytes 1572872 | tf_op jit(solution)/shard_map/ppermute | solution.py:100
  45.9 19.8 %collective-permute-start.3 = (bf16[128,2048]{1,0:T(8,128)(2,1)}, bf16[128,2048]{1,0:T(8,128)(2,1)}, u32[]{:S(2)}, u32[]{:S(2)}) collective-permute-start(bf16[128,2048]{1,0:T(8,128)(2,1)} %collective-permute-done.1), channel_id=1, source_target_pairs={{0,2},{2,4},{4,6},{6,7},{7,5},{5,3},{3,1},{1,0},{8,10},{10,12},{12... | collective-permute-start | bytes 1572872 | tf_op jit(solution)/shard_map/ppermute | solution.py:100
  47.7 30.7 %collective-permute-start.15 = (bf16[512,768]{1,0:T(8,128)(2,1)S(1)}, bf16[512,768]{1,0:T(8,128)(2,1)}, u32[]{:S(2)}, u32[]{:S(2)}) collective-permute-start(bf16[512,768]{1,0:T(8,128)(2,1)S(1)} %bitcast.708), channel_id=1, source_target_pairs={{0,16},{8,24},{16,0},{24,8},{1,17},{9,25},{17,1},{25,9},{2,18},{10... | collective-permute-start | bytes 2359304 | tf_op jit(solution)/shard_map/ppermute | solution.py:48
  79.9 24.8 %collective-permute-start.16 = (bf16[1024,768]{1,0:T(8,128)(2,1)S(1)}, bf16[1024,768]{1,0:T(8,128)(2,1)S(1)}, u32[]{:S(2)}, u32[]{:S(2)}) collective-permute-start(bf16[1024,768]{1,0:T(8,128)(2,1)S(1)} %pad_maximum_fusion.3), channel_id=1, source_target_pairs={{0,8},{8,0},{16,24},{24,16},{1,9},{9,1},{17,25},{25,17},{2,10},{10... | collective-permute-start | bytes 4718600 | tf_op jit(solution)/shard_map/ppermute | solution.py:48
  86.6 46.6 %collective-permute-start.36 = (bf16[64,2048]{1,0:T(8,128)(2,1)}, bf16[64,2048]{1,0:T(8,128)(2,1)}, u32[]{:S(2)}, u32[]{:S(2)}) collective-permute-start(bf16[64,2048]{1,0:T(8,128)(2,1)} %get-tuple-element.168), channel_id=1, source_target_pairs={{0,1},{2,0},{4,2},{6,4},{7,6},{5,7},{3,5},{1,3},{8,9},{10,8},{12,1... | collective-permute-start | bytes 786440 | tf_op jit(solution)/shard_map/ppermute | solution.py:100
  90.7 51.7 %collective-permute-start.37 = (bf16[64,2048]{1,0:T(8,128)(2,1)}, bf16[64,2048]{1,0:T(8,128)(2,1)}, u32[]{:S(2)}, u32[]{:S(2)}) collective-permute-start(bf16[64,2048]{1,0:T(8,128)(2,1)} %get-tuple-element.169), channel_id=1, source_target_pairs={{0,3},{2,1},{4,0},{6,2},{7,4},{5,6},{3,7},{1,5},{8,11},{10,9},{12,... | collective-permute-start | bytes 786440 | tf_op jit(solution)/shard_map/ppermute | solution.py:100
  95.8 49.3 %collective-permute-start.38 = (bf16[64,2048]{1,0:T(8,128)(2,1)}, bf16[64,2048]{1,0:T(8,128)(2,1)}, u32[]{:S(2)}, u32[]{:S(2)}) collective-permute-start(bf16[64,2048]{1,0:T(8,128)(2,1)} %get-tuple-element.170), channel_id=1, source_target_pairs={{0,5},{2,3},{4,1},{6,0},{7,2},{5,4},{3,6},{1,7},{8,13},{10,11},{12... | collective-permute-start | bytes 786440 | tf_op jit(solution)/shard_map/ppermute | solution.py:100
  99.6 69.4 %collective-permute-start.39 = (bf16[64,2048]{1,0:T(8,128)(2,1)}, bf16[64,2048]{1,0:T(8,128)(2,1)}, u32[]{:S(2)}, u32[]{:S(2)}) collective-permute-start(bf16[64,2048]{1,0:T(8,128)(2,1)} %get-tuple-element.171), channel_id=1, source_target_pairs={{0,7},{2,5},{4,3},{6,1},{7,0},{5,2},{3,4},{1,6},{8,15},{10,13},{12... | collective-permute-start | bytes 786440 | tf_op jit(solution)/shard_map/ppermute | solution.py:100
  141.7 31.2 %collective-permute-start.40 = (bf16[64,2048]{1,0:T(8,128)(2,1)S(1)}, bf16[64,2048]{1,0:T(8,128)(2,1)S(1)}, u32[]{:S(2)}, u32[]{:S(2)}) collective-permute-start(bf16[64,2048]{1,0:T(8,128)(2,1)S(1)} %copy-done.46), channel_id=1, source_target_pairs={{0,6},{2,7},{4,5},{6,3},{7,1},{5,0},{3,2},{1,4},{8,14},{10,15},{12... | collective-permute-start | bytes 786440 | tf_op jit(solution)/shard_map/ppermute | solution.py:100
  142.4 20.4 %collective-permute-start.22 = (bf16[128,2048]{1,0:T(8,128)(2,1)S(1)}, bf16[128,2048]{1,0:T(8,128)(2,1)S(1)}, u32[]{:S(2)}, u32[]{:S(2)}) collective-permute-start(bf16[128,2048]{1,0:T(8,128)(2,1)S(1)} %pad_maximum_fusion.10), channel_id=1, source_target_pairs={{0,2},{2,4},{4,6},{6,7},{7,5},{5,3},{3,1},{1,0},{8,10},{10,12},{12... | collective-permute-start | bytes 1572872 | tf_op jit(solution)/shard_map/ppermute | solution.py:100
  145.1 51.9 %collective-permute-start.41 = (bf16[64,2048]{1,0:T(8,128)(2,1)S(1)}, bf16[64,2048]{1,0:T(8,128)(2,1)S(1)}, u32[]{:S(2)}, u32[]{:S(2)}) collective-permute-start(bf16[64,2048]{1,0:T(8,128)(2,1)S(1)} %copy-done.45), channel_id=1, source_target_pairs={{0,4},{2,6},{4,7},{6,5},{7,3},{5,1},{3,0},{1,2},{8,12},{10,14},{12... | collective-permute-start | bytes 786440 | tf_op jit(solution)/shard_map/ppermute | solution.py:100
  155.5 41.5 %collective-permute-start.42 = (bf16[64,2048]{1,0:T(8,128)(2,1)S(1)}, bf16[64,2048]{1,0:T(8,128)(2,1)S(1)}, u32[]{:S(2)}, u32[]{:S(2)}) collective-permute-start(bf16[64,2048]{1,0:T(8,128)(2,1)S(1)} %copy-done.44), channel_id=1, source_target_pairs={{0,2},{2,4},{4,6},{6,7},{7,5},{5,3},{3,1},{1,0},{8,10},{10,12},{12... | collective-permute-start | bytes 786440 | tf_op jit(solution)/shard_map/ppermute | solution.py:100
  163.1 18.6 %collective-permute-start.25 = (bf16[128,2048]{1,0:T(8,128)(2,1)S(1)}, bf16[128,2048]{1,0:T(8,128)(2,1)S(1)}, u32[]{:S(2)}, u32[]{:S(2)}) collective-permute-start(bf16[128,2048]{1,0:T(8,128)(2,1)S(1)} %get-tuple-element.157), channel_id=1, source_target_pairs={{0,1},{2,0},{4,2},{6,4},{7,6},{5,7},{3,5},{1,3},{8,9},{10,8},{12,1... | collective-permute-start | bytes 1572872 | tf_op jit(solution)/shard_map/ppermute | solution.py:100
  187.3 21.0 %collective-permute-start.27 = (bf16[128,2048]{1,0:T(8,128)(2,1)S(1)}, bf16[128,2048]{1,0:T(8,128)(2,1)S(1)}, u32[]{:S(2)}, u32[]{:S(2)}) collective-permute-start(bf16[128,2048]{1,0:T(8,128)(2,1)S(1)} %get-tuple-element.159), channel_id=1, source_target_pairs={{0,1},{2,0},{4,2},{6,4},{7,6},{5,7},{3,5},{1,3},{8,9},{10,8},{12,1... | collective-permute-start | bytes 1572872 | tf_op jit(solution)/shard_map/ppermute | solution.py:100
  197.0 49.1 %collective-permute-start.43 = (bf16[512,2048]{1,0:T(8,128)(2,1)S(1)}, bf16[512,2048]{1,0:T(8,128)(2,1)}, u32[]{:S(2)}, u32[]{:S(2)}) collective-permute-start(bf16[512,2048]{1,0:T(8,128)(2,1)S(1)} %bitcast.698), channel_id=1, source_target_pairs={{0,16},{8,24},{16,0},{24,8},{1,17},{9,25},{17,1},{25,9},{2,18},{10... | collective-permute-start | bytes 6291464 | tf_op jit(solution)/shard_map/ppermute | solution.py:48
  230.3 36.5 %collective-permute-start.45 = (bf16[64,1024]{1,0:T(8,128)(2,1)S(1)}, bf16[64,1024]{1,0:T(8,128)(2,1)S(1)}, u32[]{:S(2)}, u32[]{:S(2)}) collective-permute-start(bf16[64,1024]{1,0:T(8,128)(2,1)S(1)} %get-tuple-element.176), channel_id=1, source_target_pairs={{0,1},{2,0},{4,2},{6,4},{7,6},{5,7},{3,5},{1,3},{8,9},{10,8},{12,1... | collective-permute-start | bytes 393224 | tf_op jit(solution)/shard_map/ppermute | solution.py:100
  231.8 38.7 %collective-permute-start.46 = (bf16[64,1024]{1,0:T(8,128)(2,1)S(1)}, bf16[64,1024]{1,0:T(8,128)(2,1)S(1)}, u32[]{:S(2)}, u32[]{:S(2)}) collective-permute-start(bf16[64,1024]{1,0:T(8,128)(2,1)S(1)} %get-tuple-element.177), channel_id=1, source_target_pairs={{0,3},{2,1},{4,0},{6,2},{7,4},{5,6},{3,7},{1,5},{8,11},{10,9},{12,... | collective-permute-start | bytes 393224 | tf_op jit(solution)/shard_map/ppermute | solution.py:100
  261.7 47.4 %collective-permute-start.44 = (bf16[1024,2048]{1,0:T(8,128)(2,1)S(1)}, bf16[1024,2048]{1,0:T(8,128)(2,1)S(1)}, u32[]{:S(2)}, u32[]{:S(2)}) collective-permute-start(bf16[1024,2048]{1,0:T(8,128)(2,1)S(1)} %pad_maximum_fusion), channel_id=1, source_target_pairs={{0,8},{8,0},{16,24},{24,16},{1,9},{9,1},{17,25},{25,17},{2,10},{10... | collective-permute-start | bytes 12582920 | tf_op jit(solution)/shard_map/ppermute | solution.py:48
  264.4 26.6 %collective-permute-start.53 = (bf16[128,2048]{1,0:T(8,128)(2,1)S(1)}, bf16[128,2048]{1,0:T(8,128)(2,1)S(1)}, u32[]{:S(2)}, u32[]{:S(2)}) collective-permute-start(bf16[128,2048]{1,0:T(8,128)(2,1)S(1)} %fusion.40), channel_id=1, source_target_pairs={{0,1},{2,0},{4,2},{6,4},{7,6},{5,7},{3,5},{1,3},{8,9},{10,8},{12,1... | collective-permute-start | bytes 1572872 | tf_op jit(solution)/shard_map/ppermute | solution.py:100
  266.6 24.5 %collective-permute-start.52 = (bf16[128,2048]{1,0:T(8,128)(2,1)S(1)}, bf16[128,2048]{1,0:T(8,128)(2,1)S(1)}, u32[]{:S(2)}, u32[]{:S(2)}) collective-permute-start(bf16[128,2048]{1,0:T(8,128)(2,1)S(1)} %fusion.40), channel_id=1, source_target_pairs={{0,2},{2,4},{4,6},{6,7},{7,5},{5,3},{3,1},{1,0},{8,10},{10,12},{12... | collective-permute-start | bytes 1572872 | tf_op jit(solution)/shard_map/ppermute | solution.py:100
  270.5 29.3 %collective-permute-start.48 = (bf16[64,1024]{1,0:T(8,128)(2,1)S(1)}, bf16[64,1024]{1,0:T(8,128)(2,1)S(1)}, u32[]{:S(2)}, u32[]{:S(2)}) collective-permute-start(bf16[64,1024]{1,0:T(8,128)(2,1)S(1)} %get-tuple-element.179), channel_id=1, source_target_pairs={{0,7},{2,5},{4,3},{6,1},{7,0},{5,2},{3,4},{1,6},{8,15},{10,13},{12... | collective-permute-start | bytes 393224 | tf_op jit(solution)/shard_map/ppermute | solution.py:100
  280.5 20.9 %collective-permute-start.49 = (bf16[64,1024]{1,0:T(8,128)(2,1)S(1)}, bf16[64,1024]{1,0:T(8,128)(2,1)S(1)}, u32[]{:S(2)}, u32[]{:S(2)}) collective-permute-start(bf16[64,1024]{1,0:T(8,128)(2,1)S(1)} %get-tuple-element.180), channel_id=1, source_target_pairs={{0,6},{2,7},{4,5},{6,3},{7,1},{5,0},{3,2},{1,4},{8,14},{10,15},{12... | collective-permute-start | bytes 393224 | tf_op jit(solution)/shard_map/ppermute | solution.py:100
  309.1 24.8 %collective-permute-start.54 = (bf16[512,1024]{1,0:T(8,128)(2,1)S(1)}, bf16[512,1024]{1,0:T(8,128)(2,1)S(1)}, u32[]{:S(2)}, u32[]{:S(2)}) collective-permute-start(bf16[512,1024]{1,0:T(8,128)(2,1)S(1)} %bitcast.704), channel_id=1, source_target_pairs={{0,16},{8,24},{16,0},{24,8},{1,17},{9,25},{17,1},{25,9},{2,18},{10... | collective-permute-start | bytes 3145736 | tf_op jit(solution)/shard_map/ppermute | solution.py:48
  398.2 43.3 %collective-permute-start.82 = (bf16[1024,1024]{1,0:T(8,128)(2,1)}, bf16[1024,1024]{1,0:T(8,128)(2,1)S(1)}, u32[]{:S(2)}, u32[]{:S(2)}) collective-permute-start(bf16[1024,1024]{1,0:T(8,128)(2,1)} %convolution_convert_fusion.1), channel_id=1, source_target_pairs={{0,8},{8,0},{16,24},{24,16},{1,9},{9,1},{17,25},{25,17},{2,10},{10... | collective-permute-start | bytes 6291464 | tf_op jit(solution)/shard_map/ppermute | solution.py:48
  424.8 58.4 %collective-permute-start.108 = (bf16[1024,2048]{1,0:T(8,128)(2,1)S(1)}, bf16[1024,2048]{1,0:T(8,128)(2,1)}, u32[]{:S(2)}, u32[]{:S(2)}) collective-permute-start(bf16[1024,2048]{1,0:T(8,128)(2,1)S(1)} %convolution_convert_fusion), channel_id=1, source_target_pairs={{0,8},{8,0},{16,24},{24,16},{1,9},{9,1},{17,25},{25,17},{2,10},{10... | collective-permute-start | bytes 12582920 | tf_op jit(solution)/shard_map/ppermute | solution.py:48
  444.1 24.2 %collective-permute-start.83 = (bf16[512,1024]{1,0:T(8,128)(2,1)S(1)}, bf16[512,1024]{1,0:T(8,128)(2,1)S(1)}, u32[]{:S(2)}, u32[]{:S(2)}) collective-permute-start(bf16[512,1024]{1,0:T(8,128)(2,1)S(1)} %slice.1762), channel_id=1, source_target_pairs={{0,16},{8,24},{16,0},{24,8},{1,17},{9,25},{17,1},{25,9},{2,18},{10... | collective-permute-start | bytes 3145736 | tf_op jit(solution)/shard_map/ppermute | solution.py:48
  490.3 51.5 %collective-permute-start.109 = (bf16[512,2048]{1,0:T(8,128)(2,1)S(1)}, bf16[512,2048]{1,0:T(8,128)(2,1)}, u32[]{:S(2)}, u32[]{:S(2)}) collective-permute-start(bf16[512,2048]{1,0:T(8,128)(2,1)S(1)} %slice.1761), channel_id=1, source_target_pairs={{0,16},{8,24},{16,0},{24,8},{1,17},{9,25},{17,1},{25,9},{2,18},{10... | collective-permute-start | bytes 6291464 | tf_op jit(solution)/shard_map/ppermute | solution.py:48
  528.9 88.7 %collective-permute-start.96 = (bf16[1024,768]{1,0:T(8,128)(2,1)S(1)}, bf16[1024,768]{1,0:T(8,128)(2,1)S(1)}, u32[]{:S(2)}, u32[]{:S(2)}) collective-permute-start(bf16[1024,768]{1,0:T(8,128)(2,1)S(1)} %convolution_convert_fusion.2), channel_id=1, source_target_pairs={{0,8},{8,0},{16,24},{24,16},{1,9},{9,1},{17,25},{25,17},{2,10},{10... | collective-permute-start | bytes 4718600 | tf_op jit(solution)/shard_map/ppermute | solution.py:48
  553.6 32.4 %collective-permute-start.92 = (bf16[128,2048]{1,0:T(8,128)(2,1)S(1)}, bf16[128,2048]{1,0:T(8,128)(2,1)S(1)}, u32[]{:S(2)}, u32[]{:S(2)}) collective-permute-start(bf16[128,2048]{1,0:T(8,128)(2,1)S(1)} %fusion.37), channel_id=1, source_target_pairs={{0,2},{2,4},{4,6},{6,7},{7,5},{5,3},{3,1},{1,0},{8,10},{10,12},{12... | collective-permute-start | bytes 1572872 | tf_op jit(solution)/shard_map/ppermute | solution.py:100
  555.2 30.9 %collective-permute-start.93 = (bf16[128,2048]{1,0:T(8,128)(2,1)S(1)}, bf16[128,2048]{1,0:T(8,128)(2,1)S(1)}, u32[]{:S(2)}, u32[]{:S(2)}) collective-permute-start(bf16[128,2048]{1,0:T(8,128)(2,1)S(1)} %fusion.38), channel_id=1, source_target_pairs={{0,1},{2,0},{4,2},{6,4},{7,6},{5,7},{3,5},{1,3},{8,9},{10,8},{12,1... | collective-permute-start | bytes 1572872 | tf_op jit(solution)/shard_map/ppermute | solution.py:100
  556.6 49.6 %collective-permute-start.110 = (bf16[64,2048]{1,0:T(8,128)(2,1)S(1)}, bf16[64,2048]{1,0:T(8,128)(2,1)S(1)}, u32[]{:S(2)}, u32[]{:S(2)}) collective-permute-start(bf16[64,2048]{1,0:T(8,128)(2,1)S(1)} %get-tuple-element.247), channel_id=1, source_target_pairs={{0,1},{2,0},{4,2},{6,4},{7,6},{5,7},{3,5},{1,3},{8,9},{10,8},{12,1... | collective-permute-start | bytes 786440 | tf_op jit(solution)/shard_map/ppermute | solution.py:100
  561.9 45.8 %collective-permute-start.111 = (bf16[64,2048]{1,0:T(8,128)(2,1)S(1)}, bf16[64,2048]{1,0:T(8,128)(2,1)S(1)}, u32[]{:S(2)}, u32[]{:S(2)}) collective-permute-start(bf16[64,2048]{1,0:T(8,128)(2,1)S(1)} %get-tuple-element.248), channel_id=1, source_target_pairs={{0,3},{2,1},{4,0},{6,2},{7,4},{5,6},{3,7},{1,5},{8,11},{10,9},{12,... | collective-permute-start | bytes 786440 | tf_op jit(solution)/shard_map/ppermute | solution.py:100
  586.0 24.3 %collective-permute-start.112 = (bf16[64,2048]{1,0:T(8,128)(2,1)S(1)}, bf16[64,2048]{1,0:T(8,128)(2,1)S(1)}, u32[]{:S(2)}, u32[]{:S(2)}) collective-permute-start(bf16[64,2048]{1,0:T(8,128)(2,1)S(1)} %get-tuple-element.249), channel_id=1, source_target_pairs={{0,5},{2,3},{4,1},{6,0},{7,2},{5,4},{3,6},{1,7},{8,13},{10,11},{12... | collective-permute-start | bytes 786440 | tf_op jit(solution)/shard_map/ppermute | solution.py:100
  586.2 26.9 %collective-permute-start.113 = (bf16[64,2048]{1,0:T(8,128)(2,1)S(1)}, bf16[64,2048]{1,0:T(8,128)(2,1)S(1)}, u32[]{:S(2)}, u32[]{:S(2)}) collective-permute-start(bf16[64,2048]{1,0:T(8,128)(2,1)S(1)} %get-tuple-element.250), channel_id=1, source_target_pairs={{0,7},{2,5},{4,3},{6,1},{7,0},{5,2},{3,4},{1,6},{8,15},{10,13},{12... | collective-permute-start | bytes 786440 | tf_op jit(solution)/shard_map/ppermute | solution.py:100
  607.7 18.2 %collective-permute-start.115 = (bf16[64,2048]{1,0:T(8,128)(2,1)S(1)}, bf16[64,2048]{1,0:T(8,128)(2,1)S(1)}, u32[]{:S(2)}, u32[]{:S(2)}) collective-permute-start(bf16[64,2048]{1,0:T(8,128)(2,1)S(1)} %get-tuple-element.252), channel_id=1, source_target_pairs={{0,4},{2,6},{4,7},{6,5},{7,3},{5,1},{3,0},{1,2},{8,12},{10,14},{12... | collective-permute-start | bytes 786440 | tf_op jit(solution)/shard_map/ppermute | solution.py:100
  610.3 20.2 %collective-permute-start.116 = (bf16[64,2048]{1,0:T(8,128)(2,1)S(1)}, bf16[64,2048]{1,0:T(8,128)(2,1)S(1)}, u32[]{:S(2)}, u32[]{:S(2)}) collective-permute-start(bf16[64,2048]{1,0:T(8,128)(2,1)S(1)} %get-tuple-element.253), channel_id=1, source_target_pairs={{0,2},{2,4},{4,6},{6,7},{7,5},{5,3},{3,1},{1,0},{8,10},{10,12},{12... | collective-permute-start | bytes 786440 | tf_op jit(solution)/shard_map/ppermute | solution.py:100
  613.0 22.1 %collective-permute-start.95 = (bf16[128,2048]{1,0:T(8,128)(2,1)S(1)}, bf16[128,2048]{1,0:T(8,128)(2,1)S(1)}, u32[]{:S(2)}, u32[]{:S(2)}) collective-permute-start(bf16[128,2048]{1,0:T(8,128)(2,1)S(1)} %fusion.39), channel_id=1, source_target_pairs={{0,1},{2,0},{4,2},{6,4},{7,6},{5,7},{3,5},{1,3},{8,9},{10,8},{12,1... | collective-permute-start | bytes 1572872 | tf_op jit(solution)/shard_map/ppermute | solution.py:100
  617.6 28.2 %collective-permute-start.94 = (bf16[128,2048]{1,0:T(8,128)(2,1)S(1)}, bf16[128,2048]{1,0:T(8,128)(2,1)S(1)}, u32[]{:S(2)}, u32[]{:S(2)}) collective-permute-start(bf16[128,2048]{1,0:T(8,128)(2,1)S(1)} %fusion.36), channel_id=1, source_target_pairs={{0,2},{2,4},{4,6},{6,7},{7,5},{5,3},{3,1},{1,0},{8,10},{10,12},{12... | collective-permute-start | bytes 1572872 | tf_op jit(solution)/shard_map/ppermute | solution.py:100
  624.4 29.1 %collective-permute-start.117 = (bf16[64,1024]{1,0:T(8,128)(2,1)S(1)}, bf16[64,1024]{1,0:T(8,128)(2,1)S(1)}, u32[]{:S(2)}, u32[]{:S(2)}) collective-permute-start(bf16[64,1024]{1,0:T(8,128)(2,1)S(1)} %copy-done.51), channel_id=1, source_target_pairs={{0,1},{2,0},{4,2},{6,4},{7,6},{5,7},{3,5},{1,3},{8,9},{10,8},{12,1... | collective-permute-start | bytes 393224 | tf_op jit(solution)/shard_map/ppermute | solution.py:100
  625.9 27.6 %collective-permute-start.118 = (bf16[64,1024]{1,0:T(8,128)(2,1)S(1)}, bf16[64,1024]{1,0:T(8,128)(2,1)S(1)}, u32[]{:S(2)}, u32[]{:S(2)}) collective-permute-start(bf16[64,1024]{1,0:T(8,128)(2,1)S(1)} %copy-done.50), channel_id=1, source_target_pairs={{0,3},{2,1},{4,0},{6,2},{7,4},{5,6},{3,7},{1,5},{8,11},{10,9},{12,... | collective-permute-start | bytes 393224 | tf_op jit(solution)/shard_map/ppermute | solution.py:100
  630.5 26.2 %collective-permute-start.119 = (bf16[64,1024]{1,0:T(8,128)(2,1)S(1)}, bf16[64,1024]{1,0:T(8,128)(2,1)S(1)}, u32[]{:S(2)}, u32[]{:S(2)}) collective-permute-start(bf16[64,1024]{1,0:T(8,128)(2,1)S(1)} %copy-done.49), channel_id=1, source_target_pairs={{0,5},{2,3},{4,1},{6,0},{7,2},{5,4},{3,6},{1,7},{8,13},{10,11},{12... | collective-permute-start | bytes 393224 | tf_op jit(solution)/shard_map/ppermute | solution.py:100
  635.1 28.0 %collective-permute-start.120 = (bf16[64,1024]{1,0:T(8,128)(2,1)S(1)}, bf16[64,1024]{1,0:T(8,128)(2,1)S(1)}, u32[]{:S(2)}, u32[]{:S(2)}) collective-permute-start(bf16[64,1024]{1,0:T(8,128)(2,1)S(1)} %copy-done.48), channel_id=1, source_target_pairs={{0,7},{2,5},{4,3},{6,1},{7,0},{5,2},{3,4},{1,6},{8,15},{10,13},{12... | collective-permute-start | bytes 393224 | tf_op jit(solution)/shard_map/ppermute | solution.py:100
  656.8 20.2 %collective-permute-start.97 = (bf16[512,768]{1,0:T(8,128)(2,1)S(1)}, bf16[512,768]{1,0:T(8,128)(2,1)S(1)}, u32[]{:S(2)}, u32[]{:S(2)}) collective-permute-start(bf16[512,768]{1,0:T(8,128)(2,1)S(1)} %slice.1763), channel_id=1, source_target_pairs={{0,16},{8,24},{16,0},{24,8},{1,17},{9,25},{17,1},{25,9},{2,18},{10... | collective-permute-start | bytes 2359304 | tf_op jit(solution)/shard_map/ppermute | solution.py:48
  (164 other events, 2518.7 us)

commit v4 on v3

--- a/solution.py
+++ b/solution.py
@@ -62,18 +62,24 @@
         blocks = [parts[self.order.index(k)] for k in range(self.count)]
         return jnp.concatenate(self.relative(blocks), axis=1)
 
-    def gather(self, block, done=(), later=()):
+    def gather_far(self, block, done=()):
         (value,) = tie([block], done)
         for bit in self.bits[1:]:
-            value = jnp.concatenate([value, *tie([self.swap(value, bit)], later)], axis=0)
+            value = jnp.concatenate([value, self.swap(value, bit)], axis=0)
+        return value
+
+    def gather(self, block, done=()):
+        value = self.gather_far(block, done)
         return value, self.swap(value, 1)
 
-    def scatter_sum(self, kept, given):
-        total = kept() + self.swap(given, 1).astype(F32)
+    def scatter_core(self, kept, given):
+        return kept + self.swap(given, 1).astype(F32)
+
+    def scatter_rest(self, total):
         for bit in reversed(self.bits[1:]):
             half = total.shape[0] // 2
-            low = total.astype(BF16)
-            total = total[:half] + self.swap(low[half:], bit).astype(F32)
+            low = total[half:].astype(BF16)
+            total = total[:half] + self.swap(low, bit).astype(F32)
         return total.astype(BF16)
 
 
@@ -147,33 +153,14 @@
             else:
                 right = whole(half - step) + right.astype(F32)
                 left = whole(half + step) + left.astype(F32)
-            right, left = self.both(right.astype(BF16), left.astype(BF16), fill.get(step, ()))
+            right, left = self.both(
+                right.astype(BF16), left.astype(BF16), fill.get(step, ())
+            )
         if half == 1:
             return jnp.concatenate(
                 [part(0, lower) + right.astype(F32), part(0, upper) + left.astype(F32)], axis=1
             )
         return whole(0) + right.astype(F32) + left.astype(F32)
-
-    def exchange(self, pieces, done=()):
-        size = self.size
-        out = [None] * size
-        out[0] = pieces[0]
-        sent = tie(pieces[1:], done)
-        for by in range(1, size):
-            out[size - by] = self.shift(sent[by - 1], by)
-        return out
-
-    def place_in_order(self, pieces):
-        out = jnp.zeros((self.size,) + pieces[0].shape, pieces[0].dtype)
-        for ahead in range(self.size):
-            out = lax.dynamic_update_index_in_dim(out, pieces[ahead], self.owner(ahead), 0)
-        return out
-
-    def take_relative(self, stacked):
-        return [
-            lax.dynamic_index_in_dim(stacked, self.owner(ahead), 0, keepdims=False)
-            for ahead in range(self.size)
-        ]
 
 
 def column_blocks(weight, size):
@@ -402,13 +389,15 @@
     def scaled(weight, gain):
         return (weight.astype(F32) * gain).astype(BF16)
 
-    def send_columns(weights, done=()):
+    def exchange(blocks, done=()):
+        return lax.all_to_all(tie([blocks], done)[0], "ctx", 0, 0, tiled=True)
+
+    def to_columns(weights, done=()):
         blocks = jnp.concatenate([column_blocks(w, size) for w in weights], axis=2)
-        return ring.exchange(ring.take_relative(blocks), done)
-
-    def placed(pieces):
-        got = ring.place_in_order(pieces)
-        return got.reshape(-1, got.shape[2])
+        return exchange(blocks, done).reshape(-1, blocks.shape[2])
+
+    def to_rows(total, done=()):
+        return exchange(total.reshape(size, -1, total.shape[1]), done)
 
     def halves(pieces):
         half = width // 2
@@ -428,32 +417,35 @@
 
     to_shares = [(i * size + j, j * count + i) for i in range(count) for j in range(size)]
     from_shares = [(there, here) for here, there in to_shares]
-    attn_pieces = send_columns([scaled(w, gain_one) for w in (query_weight, key_weight, value_weight)])
-    mix_share = lax.ppermute(mix_weight, ("dp", "ctx"), from_shares)
-    one_pieces = ring.gather(normed_one.astype(BF16))
-    one_all = halves(one_pieces)
-    attn_weights = shares.gather(placed(attn_pieces))
-    ffn_pieces = send_columns(
-        [scaled(gate_weight, gain_two), scaled(up_weight, gain_two)], ring.steps[-2]
-    )
-    mix_parts = shares.gather(mix_share, attn_weights[1:])
+    attn_columns = to_columns([scaled(w, gain_one) for w in (query_weight, key_weight, value_weight)])
+    one_all = halves(ring.gather(normed_one.astype(BF16)))
+    mix_share = lax.ppermute(tie([mix_weight], ring.steps[-2])[0], ("dp", "ctx"), from_shares)
+    attn_weights = shares.gather(attn_columns)
+    projected = apply(one_all, attn_weights)
+    ffn_columns = to_columns(
+        [scaled(gate_weight, gain_two), scaled(up_weight, gain_two), down_weight], ring.done
+    )
+    ffn_half = shares.gather_far(ffn_columns[:, : 2 * hidden_local])
+    down_half = shares.gather_far(ffn_columns[:, 2 * hidden_local :], (ffn_half,))
+    attention = Attention(size, groups, slots, local, head_size, lengths, owners)
+    mixed, query_rot, key_rot, value_low, lse = attention.forward(projected)
+    mixed = mixed.reshape(size * rows, local)
+    mix_parts = shares.gather(mix_share, (mixed,))
     mix_blocks = jnp.split(jnp.concatenate(mix_parts, axis=0), count, axis=0)
     mix_rows = shares.to_order(
         jnp.concatenate(
             shares.relative([mix_blocks[shares.order.index(k)] for k in range(count)]), axis=0
         )
     )
-    projected = apply(one_all, attn_weights)
-    attention = Attention(size, groups, slots, local, head_size, lengths, owners)
-    mixed, query_rot, key_rot, value_low, lse = attention.forward(projected)
-    mixed = mixed.reshape(size * rows, local)
     attn_out = contract(mixed, mix_rows, 1, 0)
-    residual = block_in + ring.scatter_sum(attn_out[:, : width // 2], attn_out[:, width // 2 :])
-
-    down_pieces = send_columns([down_weight], ring.steps[-2])
+    residual = block_in + ring.scatter_sum(
+        attn_out[:, : width // 2], attn_out[:, width // 2 :], ((ffn_columns,),)
+    )
+
+    ffn_weights = (ffn_half, shares.swap(ffn_half, 1))
     normed_two, factor_two = normalize(residual)
-    two_all = halves(ring.gather(normed_two.astype(BF16)))
-    ffn_weights = shares.gather(placed(ffn_pieces), later=ring.steps[-2])
+    two_all = halves(ring.gather(normed_two.astype(BF16), ((), (ffn_half,))))
+    down_weights = (down_half, shares.swap(down_half, 1))
     low_part = contract(two_all[0], ffn_weights[0], 1, 0)
     gate_up = low_part + contract(two_all[1], ffn_weights[1], 1, 0)
     gate, up = gate_up[:, :hidden_local], gate_up[:, hidden_local:]
@@ -461,10 +453,7 @@
     silu_gate = gate * sigma
     hidden = (silu_gate * up).astype(BF16)
     grad_all = halves(
-        ring.gather(grad_out.astype(BF16), fill=((), (low_part,), (gate_up,), (hidden,)))
-    )
-    down_weights = shares.gather(
-        placed(tie(down_pieces, ring.steps[-4])), ffn_weights[1:], later=(hidden,)
+        ring.gather(grad_out.astype(BF16), fill=((), (low_part, down_half), (gate_up,), (hidden,)))
     )
     branch = ring.scatter_sum(*(contract(hidden, w, 1, 1) for w in down_weights))
     activations = valid * (residual + branch)
@@ -480,64 +469,60 @@
 
     def summed(values, gradient):
         given = contract(values[1], gradient, 0, 0).astype(BF16)
-        return given, lambda: shares.scatter_sum(
-            lambda: contract(values[0], gradient, 0, 0), given
-        )
-
-    down_given, down_total = summed(grad_all, hidden)
-    both_given, both_total = summed(two_all, grad_both)
-    down_sum = down_total()
-    both_sum = both_total()
+        return given, shares.scatter_core(contract(values[0], gradient, 0, 0), given)
+
+    down_given, down_half = summed(grad_all, hidden)
+    both_given, both_half = summed(two_all, grad_both)
+    down_sum = shares.scatter_rest(down_half)
+    both_sum = shares.scatter_rest(tie([both_half], (down_sum,))[0])
     scaled_two = ring.scatter_sum(
         *(contract(grad_both, w, 1, 1) for w in ffn_weights),
-        fill=((), (down_given,), (both_given,)),
+        fill=((), (down_given,), (both_given,), (down_half,)),
     )
     dres = grad_out + factor_two * (
         scaled_two - normed_two * jnp.mean(normed_two * scaled_two, axis=-1, keepdims=True)
     )
     dres_low = dres.astype(BF16)
 
-    def send_rows(total, done=()):
-        stacked = total.reshape(size, total.shape[0] // size, total.shape[1])
-        return ring.exchange(ring.take_relative(stacked), done)
-
-    dres_pieces = ring.gather(dres_low, fill=((), (), (down_sum,)))
+    dres_pieces = ring.gather(dres_low, fill=((both_half,),))
     dres_all = jnp.concatenate(dres_pieces, axis=0)
-    down_pieces = send_rows(down_sum, ring.done)
-    both_pieces = send_rows(both_sum, ring.done)
+    down_rows = to_rows(down_sum, ring.steps[-2])
+    both_rows = to_rows(both_sum, ring.steps[-2])
     grad_heads = contract(dres_all, mix_rows, 1, 1).astype(BF16)
-    dq, dk, dv = attention.backward(query_rot, key_rot, value_low, grad_heads, lse)
+    dq, dk, dv = attention.backward(
+        query_rot, key_rot, value_low, *tie([grad_heads], (both_sum, down_rows)), lse
+    )
     projected_grad = jnp.concatenate(
         [d.reshape(size * rows, local) for d in (dq, dk, dv)], axis=1
     )
-    attn_given, attn_total = summed(one_all, projected_grad)
-    attn_sum = attn_total()
+    (projected_grad,) = tie([projected_grad], (both_rows,))
+    attn_given, attn_half = summed(one_all, projected_grad)
+    attn_rows = to_rows(shares.scatter_rest(attn_half))
     mix_terms = shares.from_order(contract(mixed, dres_all, 0, 0))
     mix_blocks = shares.relative(jnp.split(mix_terms, count, axis=0))
     mix_blocks = [mix_blocks[k] for k in shares.order]
     mix_given = jnp.concatenate(mix_blocks[count // 2 :], axis=0).astype(BF16)
-    mix_sum = shares.scatter_sum(
-        lambda: jnp.concatenate(mix_blocks[: count // 2], axis=0), mix_given
+    mix_sum = shares.scatter_rest(
+        shares.scatter_core(jnp.concatenate(mix_blocks[: count // 2], axis=0), mix_given)
     )
     scaled_one = ring.scatter_sum(
         *(contract(projected_grad, w, 1, 1) for w in attn_weights),
-        fill=((attn_given,),),
+        fill=((attn_given,), (attn_half,), (), (attn_rows,)),
     )
     input_grad = dres + factor_one * (
         scaled_one - normed_one * jnp.mean(normed_one * scaled_one, axis=-1, keepdims=True)
     )
-    attn_pieces = send_rows(attn_sum, ring.steps[-2])
+    (mix_sum,) = tie([mix_sum], ring.steps[-2])
     mix_grad = lax.ppermute(mix_sum, ("dp", "ctx"), to_shares).astype(F32)
 
-    def joined(pieces, columns):
-        return join_columns(ring.place_in_order([p[:, columns] for p in pieces])).astype(F32)
-
-    down_pieces, both_pieces = (tie(p, ring.done) for p in (down_pieces, both_pieces))
-    down_grad = joined(down_pieces, slice(None))
-    gate_raw = joined(both_pieces, slice(0, hidden_local))
-    up_raw = joined(both_pieces, slice(hidden_local, 2 * hidden_local))
+    def joined(rows, columns):
+        return join_columns(rows[:, :, columns]).astype(F32)
+
+    down_grad = joined(down_rows, slice(None))
+    gate_raw = joined(both_rows, slice(0, hidden_local))
+    up_raw = joined(both_rows, slice(hidden_local, 2 * hidden_local))
     query_raw, key_raw, value_raw = (
-        joined(attn_pieces, slice(i * local, (i + 1) * local)) for i in range(3)
+        joined(attn_rows, slice(i * local, (i + 1) * local)) for i in range(3)
     )
 
     def row_sum(*pairs):

time: 709 us -> 670 us (0.945)
  starting transfers between devices: 218 us -> 124 us
  other arithmetic: 37.9 us -> 57.9 us
  matrix products: 86.9 us -> 103 us
  waiting for transfers between devices: 287 us -> 299 us
  local copies, waits for them, and re-layouts: 46.5 us -> 54.1 us
    ppermute x106 -> x64, starting transfers between devices: 207 us -> 75.2 us  [shift(): return lax.ppermute(value, 'ctx', pairs)]
    ppermute x106 -> x64, waiting for transfers between devices: 267 us -> 200 us  [shift(): return lax.ppermute(value, 'ctx', pairs)]
    all_to_all x0 -> x5, waiting for transfers between devices: none -> 62.5 us  [exchange(): return lax.all_to_all(tie([blocks], done)[0], 'ctx', 0, 0, tiled=True)]
    all_to_all x0 -> x5, starting transfers between devices: none -> 35 us  [exchange(): return lax.all_to_all(tie([blocks], done)[0], 'ctx', 0, 0, tiled=True)]
    unnamed x292 -> x255, local copies, waits for them, and re-layouts: 20 us -> 38.9 us
    ppermute x16, waiting for transfers between devices: 19.2 us -> 36.7 us  [swap(): return lax.ppermute(value, 'dp', [(i, i ^ bit) for i in range(self.count)])]
    dot_general x21, matrix products: 86.9 us -> 103 us  [contract(): lax.dot_general(left, right, (((left_dim,), (right_dim,)), ((), ())), pre...]
    dynamic_update_slice x48 -> x0, local copies, waits for them, and re-layouts: 7.25 us -> none  [place_in_order(): lax.dynamic_update_index_in_dim(out, pieces[ahead], self.owner(ahead), 0)]
  transfers between devices with their start and end apart: 124 -> 87, of which waited for: 61 -> 58; matrix products, arithmetic and copies ran while one was open for 22% -> 29% of each run, Pallas kernels for 3% -> 4%
where the time goes in v4:
time: 670 us; the launch traced here: 664 us
  waiting for transfers between devices  299 us (45%)
  starting transfers between devices  124 us (19%)
  matrix products  103 us (15%)
  other arithmetic  57.9 us (9%)
  local copies, waits for them, and re-layouts  54.1 us (8%)
  Pallas kernels  23.5 us (4%)
    ppermute x64, waiting for transfers between devices, shift(): return lax.ppermute(value, 'ctx', pairs)  200 us
    dot_general x21, matrix products, contract(): lax.dot_general(left, right, (((left_dim,), (right_dim,)), ((), ())), pre...  103 us
    ppermute x64, starting transfers between devices, shift(): return lax.ppermute(value, 'ctx', pairs)  75.2 us
    all_to_all x5, waiting for transfers between devices, exchange(): return lax.all_to_all(tie([blocks], done)[0], 'ctx', 0, 0, tiled=True)  62.5 us
    unnamed x255, local copies, waits for them, and re-layouts  38.9 us
    ppermute x16, waiting for transfers between devices, swap(): return lax.ppermute(value, 'dp', [(i, i ^ bit) for i in range(self.count)])  36.7 us
    all_to_all x5, starting transfers between devices, exchange(): return lax.all_to_all(tie([blocks], done)[0], 'ctx', 0, 0, tiled=True)  35 us
  transfers between devices with their start and end apart: 87, of which 58 were waited for; matrix products, arithmetic and copies ran while one was open for 29% of the time, Pallas kernels for 4%

profile of v4, /device:TPU:0, one launch (start us, length us, event | category | flops | bytes accessed | tf_op | source)
XLA Modules:
  0.0 664.1 jit_solution(3537138081055912588)
XLA Ops:
  7.8 6.4 all-to-all-start
  26.2 17.5 %collective-permute-done.2 = bf16[128,2048]{1,0:T(8,128)(2,1)S(1)} collective-permute-done((bf16[128,2048]{1,0:T(8,128)(2,1)}, bf16[128,2048]{1,0:T(8,128)(2,1)S(1)}, u32[]{:S(2)}, u32[]{:S(2)}) %collective-permute-start.2) | collective-permute-done | bytes 524320 | tf_op jit(solution)/shard_map/ppermute | solution.py:106
  43.9 5.6 collective-permute-start.5
  54.6 5.6 collective-permute-done.4
  69.2 9.7 %all-to-all-start.1 = ((bf16[8,64,3072]{2,1,0:T(8,128)(2,1)}), bf16[8,64,3072]{2,1,0:T(8,128)(2,1)S(1)}, u32[]{:S(2)}, u32[]{:S(2)}) async-start(bf16[8,64,3072]{2,1,0:T(8,128)(2,1)} %pad_maximum_fusion.2), calls=%async_computation.1 | async-start | bytes 6291456 | tf_op jit(solution)/shard_map/all_to_all | solution.py:393
  85.9 4.7 fusion.85
  90.6 4.9 convolution_add_fusion.2
  96.9 10.5 %attention_forward.1 = (bf16[8,2,64,256]{3,2,1,0:T(8,128)(2,1)}, bf16[8,2,64,256]{3,2,1,0:T(8,128)(2,1)}, bf16[8,2,64,256]{3,2,1,0:T(8,128)(2,1)}, bf16[8,2,64,256]{3,2,1,0:T(8,128)(2,1)}, f32[2,512,4]{2,1,0:T(8,128)}) custom-call(s32[2]{0:T(128)} %lengths_ref.3, f32[8,2,64,768]{3,2,1,0:T(8,128)} %bitcast.417, f32[8,2,64,768]{3,2,1,0:T(8,128)} %bitcast.418, ...), custom_call_target="tpu_custom_call" | custom-call | flops 536870912 | bytes 4194304 | tf_op jit(solution)/shard_map/attention_forward/pallas_call | solution.py:329
  110.6 6.7 %collective-permute-done.11 = bf16[64,2048]{1,0:T(8,128)(2,1)S(1)} collective-permute-done((bf16[64,2048]{1,0:T(8,128)(2,1)}, bf16[64,2048]{1,0:T(8,128)(2,1)S(1)}, u32[]{:S(2)}, u32[]{:S(2)}) %collective-permute-start.11) | collective-permute-done | bytes 262176 | tf_op jit(solution)/shard_map/ppermute | solution.py:48
  122.4 4.5 fusion.78
  127.9 22.0 %all-to-all-done.1 = bf16[8,64,3072]{2,1,0:T(8,128)(2,1)S(1)} async-done(((bf16[8,64,3072]{2,1,0:T(8,128)(2,1)}), bf16[8,64,3072]{2,1,0:T(8,128)(2,1)S(1)}, u32[]{:S(2)}, u32[]{:S(2)}) %all-to-all-start.1) | async-done | bytes 3145760 | tf_op jit(solution)/shard_map/all_to_all | solution.py:393
  152.0 5.7 collective-permute-done.13
  161.3 10.3 %collective-permute-done.15 = bf16[128,2048]{1,0:T(8,128)(2,1)S(1)} collective-permute-done((bf16[128,2048]{1,0:T(8,128)(2,1)S(1)}, bf16[128,2048]{1,0:T(8,128)(2,1)S(1)}, u32[]{:S(2)}, u32[]{:S(2)}) %collective-permute-start.15) | collective-permute-done | bytes 524320 | tf_op jit(solution)/shard_map/ppermute | solution.py:106
  178.9 6.3 collective-permute-done.17
  190.6 8.8 %collective-permute-done.19 = bf16[128,2048]{1,0:T(8,128)(2,1)} collective-permute-done((bf16[128,2048]{1,0:T(8,128)(2,1)}, bf16[128,2048]{1,0:T(8,128)(2,1)}, u32[]{:S(2)}, u32[]{:S(2)}) %collective-permute-start.19) | collective-permute-done | bytes 524320 | tf_op jit(solution)/shard_map/ppermute | solution.py:106
  204.2 18.0 %collective-permute-done.23 = bf16[512,2048]{1,0:T(8,128)(2,1)} collective-permute-done((bf16[512,2048]{1,0:T(8,128)(2,1)}, bf16[512,2048]{1,0:T(8,128)(2,1)}, u32[]{:S(2)}, u32[]{:S(2)}) %collective-permute-start.23) | collective-permute-done | bytes 2097184 | tf_op jit(solution)/shard_map/ppermute | solution.py:48
  228.7 9.2 %collective-permute-done.24 = bf16[128,2048]{1,0:T(8,128)(2,1)S(1)} collective-permute-done((bf16[128,2048]{1,0:T(8,128)(2,1)S(1)}, bf16[128,2048]{1,0:T(8,128)(2,1)S(1)}, u32[]{:S(2)}, u32[]{:S(2)}) %collective-permute-start.24) | collective-permute-done | bytes 524320 | tf_op jit(solution)/shard_map/ppermute | solution.py:106
  240.9 8.5 %collective-permute-done.26 = bf16[128,2048]{1,0:T(8,128)(2,1)S(1)} collective-permute-done((bf16[128,2048]{1,0:T(8,128)(2,1)S(1)}, bf16[128,2048]{1,0:T(8,128)(2,1)S(1)}, u32[]{:S(2)}, u32[]{:S(2)}) %collective-permute-start.26) | collective-permute-done | bytes 524320 | tf_op jit(solution)/shard_map/ppermute | solution.py:106
  253.5 7.0 %collective-permute-done.28 = bf16[64,2048]{1,0:T(8,128)(2,1)S(1)} collective-permute-done((bf16[64,2048]{1,0:T(8,128)(2,1)S(1)}, bf16[64,2048]{1,0:T(8,128)(2,1)S(1)}, u32[]{:S(2)}, u32[]{:S(2)}) %collective-permute-start.28) | collective-permute-done | bytes 262176 | tf_op jit(solution)/shard_map/ppermute | solution.py:106
  264.3 9.0 %fusion.64 = f32[1024,2048]{1,0:T(8,128)} fusion(bf16[1024,1024]{1,0:T(8,128)(2,1)S(1)} %get-tuple-element.327, bf16[512,2048]{1,0:T(8,128)(2,1)} %collective-permute-done.23, bf16[512,2048]{1,0:T(8,128)(2,1)} %slice.1036), kind=kOutput, calls=%fused_computation.489 | convolution fusion | flops 4303355904 | bytes 14680064 | tf_op jit(solution)/shard_map/dot_general | solution.py:25
  278.6 6.9 %collective-permute-done.36 = bf16[128,2048]{1,0:T(8,128)(2,1)S(1)} collective-permute-done((bf16[128,2048]{1,0:T(8,128)(2,1)S(1)}, bf16[128,2048]{1,0:T(8,128)(2,1)S(1)}, u32[]{:S(2)}, u32[]{:S(2)}) %collective-permute-start.36) | collective-permute-done | bytes 524320 | tf_op jit(solution)/shard_map/ppermute | solution.py:106
  287.6 8.2 %convolution_add_fusion = f32[1024,2048]{1,0:T(8,128)S(1)} fusion(f32[1024,2048]{1,0:T(8,128)} %fusion.64, bf16[1024,1024]{1,0:T(8,128)(2,1)S(1)} %get-tuple-element.326, bf16[1024,2048]{1,0:T(8,128)(2,1)} %copy-done.68), kind=kOutput, calls=%fused_computation.11 | convolution fusion | flops 4297064448 | bytes 23068672 | tf_op jit(solution)/shard_map/dot_general | solution.py:25
  310.0 6.8 %collective-permute-done.39 = bf16[64,2048]{1,0:T(8,128)(2,1)S(1)} collective-permute-done((bf16[64,2048]{1,0:T(8,128)(2,1)S(1)}, bf16[64,2048]{1,0:T(8,128)(2,1)S(1)}, u32[]{:S(2)}, u32[]{:S(2)}) %collective-permute-start.39) | collective-permute-done | bytes 262176 | tf_op jit(solution)/shard_map/ppermute | solution.py:106
  323.3 7.3 %fusion.86 = f32[1024,1024]{1,0:T(8,128)} fusion(bf16[1024,1024]{1,0:T(8,128)(2,1)} %get-tuple-element.303, bf16[1024,1024]{1,0:T(8,128)(2,1)} %collective-permute-done.32), kind=kOutput, calls=%fused_computation.511 | convolution fusion | flops 2147483648 | bytes 8388608 | tf_op jit(solution)/shard_map/dot_general | solution.py:25
  333.5 6.8 %multiply_convert_fusion.1 = (bf16[1024,1024]{1,0:T(8,128)(2,1)}, bf16[1024,1024]{1,0:T(8,128)(2,1)}) fusion(f32[1024,2048]{1,0:T(8,128)S(1)} %convolution_add_fusion, f32[1024,1024]{1,0:T(8,128)} %fusion.86, bf16[1024,1024]{1,0:T(8,128)(2,1)S(1)} %get-tuple-element.302, bf16[1024,1024]{1,0:T(8,128)(2,1)S(1)} %constant_dynamic-update-slice_fusion.84), kind=kOutput, calls=%fused_computation.7 | convolution fusion | flops 2162163712 | bytes 20971520 | tf_op jit(solution)/shard_map/dot_general | solution.py:25
  340.3 4.7 collective-permute-done.43
  347.7 6.3 fusion.80
  361.0 8.0 %fusion.79 = (bf16[1024,1024]{1,0:T(8,128)(2,1)S(1)}, f32[1024,1024]{1,0:T(8,128)S(1)}) fusion(bf16[512,2048]{1,0:T(8,128)(2,1)} %collective-permute-done.23, bf16[512,2048]{1,0:T(8,128)(2,1)} %slice.1036, bf16[1024,1024]{1,0:T(8,128)(2,1)} %get-tuple-element.177, bf16[1024,1024]{1,0:T(8,128)(2,1)} %get-tuple-element.176), kind=kOutput, calls=%fused_computation.504 | convolution fusion | flops 4312793088 | bytes 14680064 | tf_op jit(solution)/shard_map/dot_general | solution.py:25
  376.3 7.5 %collective-permute-done.50 = bf16[128,1024]{1,0:T(8,128)(2,1)S(1)} collective-permute-done((bf16[128,1024]{1,0:T(8,128)(2,1)S(1)}, bf16[128,1024]{1,0:T(8,128)(2,1)S(1)}, u32[]{:S(2)}, u32[]{:S(2)}) %collective-permute-start.50) | collective-permute-done | bytes 262176 | tf_op jit(solution)/shard_map/ppermute | solution.py:106
  386.2 6.3 convolution_convert_fusion
  392.5 5.2 collective-permute-done.51
  404.7 6.2 collective-permute-done.53
  414.5 8.7 %collective-permute-done.56 = bf16[128,2048]{1,0:T(8,128)(2,1)S(1)} collective-permute-done((bf16[128,2048]{1,0:T(8,128)(2,1)S(1)}, bf16[128,2048]{1,0:T(8,128)(2,1)S(1)}, u32[]{:S(2)}, u32[]{:S(2)}) %collective-permute-start.56) | collective-permute-done | bytes 524320 | tf_op jit(solution)/shard_map/ppermute | solution.py:106
  426.4 6.3 convert_add_fusion
  434.8 9.3 %collective-permute-done.59 = bf16[128,2048]{1,0:T(8,128)(2,1)S(1)} collective-permute-done((bf16[128,2048]{1,0:T(8,128)(2,1)S(1)}, bf16[128,2048]{1,0:T(8,128)(2,1)S(1)}, u32[]{:S(2)}, u32[]{:S(2)}) %collective-permute-start.59) | collective-permute-done | bytes 524320 | tf_op jit(solution)/shard_map/ppermute | solution.py:106
  449.1 8.4 %collective-permute-done.61 = bf16[128,2048]{1,0:T(8,128)(2,1)S(1)} collective-permute-done((bf16[128,2048]{1,0:T(8,128)(2,1)S(1)}, bf16[128,2048]{1,0:T(8,128)(2,1)S(1)}, u32[]{:S(2)}, u32[]{:S(2)}) %collective-permute-start.61) | collective-permute-done | bytes 524320 | tf_op jit(solution)/shard_map/ppermute | solution.py:106
  467.4 5.6 collective-permute-done.64
  484.6 7.8 %collective-permute-done.66 = bf16[64,2048]{1,0:T(8,128)(2,1)S(1)} collective-permute-done((bf16[64,2048]{1,0:T(8,128)(2,1)S(1)}, bf16[64,2048]{1,0:T(8,128)(2,1)S(1)}, u32[]{:S(2)}, u32[]{:S(2)}) %collective-permute-start.66) | collective-permute-done | bytes 262176 | tf_op jit(solution)/shard_map/ppermute | solution.py:106
  505.4 11.0 %all-to-all-start.3 = ((bf16[8,64,2048]{2,1,0:T(8,128)(2,1)}), bf16[8,64,2048]{2,1,0:T(8,128)(2,1)}, u32[]{:S(2)}, u32[]{:S(2)}) async-start(bf16[8,64,2048]{2,1,0:T(8,128)(2,1)} %bitcast.422), calls=%async_computation.3 | async-start | bytes 4194304 | tf_op jit(solution)/shard_map/all_to_all | solution.py:393
  521.1 4.4 collective-permute-done.80
  527.1 12.9 %attention_backward.1 = (bf16[8,2,64,256]{3,2,1,0:T(8,128)(2,1)}, bf16[8,2,64,256]{3,2,1,0:T(8,128)(2,1)}, bf16[8,2,64,256]{3,2,1,0:T(8,128)(2,1)}) custom-call(s32[2]{0:T(128)} %lengths_ref.3, bf16[8,2,64,256]{3,2,1,0:T(8,128)(2,1)} %get-tuple-element.142.q_ref, bf16[8,2,64,256]{3,2,1,0:T(8,128)(2,1)} %get-tuple-element.143.k_ref, ...), custom_call_target="tpu_custom_call" | custom-call | flops 1342177280 | bytes 4194304 | tf_op jit(solution)/shard_map/attention_backward/pallas_call | solution.py:351
  541.5 22.8 %all-to-all-done.3 = bf16[8,64,2048]{2,1,0:T(8,128)(2,1)} async-done(((bf16[8,64,2048]{2,1,0:T(8,128)(2,1)}), bf16[8,64,2048]{2,1,0:T(8,128)(2,1)}, u32[]{:S(2)}, u32[]{:S(2)}) %all-to-all-start.3) | async-done | bytes 2097184 | tf_op jit(solution)/shard_map/all_to_all | solution.py:393
  592.4 8.2 %collective-permute-done.72 = bf16[128,2048]{1,0:T(8,128)(2,1)S(1)} collective-permute-done((bf16[128,2048]{1,0:T(8,128)(2,1)S(1)}, bf16[128,2048]{1,0:T(8,128)(2,1)S(1)}, u32[]{:S(2)}, u32[]{:S(2)}) %collective-permute-start.72) | collective-permute-done | bytes 524320 | tf_op jit(solution)/shard_map/ppermute | solution.py:106
  606.0 4.9 collective-permute-done.76
  612.0 4.2 all-to-all-start.4
  616.3 4.4 fusion.3
  625.2 17.6 %all-to-all-done.4 = bf16[8,64,768]{2,1,0:T(8,128)(2,1)} async-done(((bf16[8,64,768]{2,1,0:T(8,128)(2,1)}), bf16[8,64,768]{2,1,0:T(8,128)(2,1)}, u32[]{:S(2)}, u32[]{:S(2)}) %all-to-all-start.4) | async-done | bytes 786464 | tf_op jit(solution)/shard_map/all_to_all | solution.py:393
  642.9 4.8 collective-permute-start.77
  (537 shorter events, 258.2 us)
Async XLA Ops:
  3.1 17.3 %collective-permute-start.1 = (bf16[128,2048]{1,0:T(8,128)(2,1)}, bf16[128,2048]{1,0:T(8,128)(2,1)}, u32[]{:S(2)}, u32[]{:S(2)}) collective-permute-start(bf16[128,2048]{1,0:T(8,128)(2,1)} %fusion.9), channel_id=1, source_target_pairs={{0,2},{2,4},{4,6},{6,7},{7,5},{5,3},{3,1},{1,0},{8,10},{10,12},{12... | collective-permute-start | bytes 1572872 | tf_op jit(solution)/shard_map/ppermute | solution.py:106
  6.2 15.1 %collective-permute-start = (bf16[128,2048]{1,0:T(8,128)(2,1)}, bf16[128,2048]{1,0:T(8,128)(2,1)}, u32[]{:S(2)}, u32[]{:S(2)}) collective-permute-start(bf16[128,2048]{1,0:T(8,128)(2,1)} %fusion.9), channel_id=1, source_target_pairs={{0,1},{2,0},{4,2},{6,4},{7,6},{5,7},{3,5},{1,3},{8,9},{10,8},{12,1... | collective-permute-start | bytes 1572872 | tf_op jit(solution)/shard_map/ppermute | solution.py:106
  7.8 42.0 %all-to-all-start = ((bf16[8,64,768]{2,1,0:T(8,128)(2,1)}), bf16[8,64,768]{2,1,0:T(8,128)(2,1)}, u32[]{:S(2)}, u32[]{:S(2)}) async-start(bf16[8,64,768]{2,1,0:T(8,128)(2,1)} %pad_maximum_fusion.8), calls=%async_computation | async-start | bytes 1572864 | tf_op jit(solution)/shard_map/all_to_all | solution.py:393
  21.3 22.4 %collective-permute-start.2 = (bf16[128,2048]{1,0:T(8,128)(2,1)}, bf16[128,2048]{1,0:T(8,128)(2,1)S(1)}, u32[]{:S(2)}, u32[]{:S(2)}) collective-permute-start(bf16[128,2048]{1,0:T(8,128)(2,1)} %collective-permute-done), channel_id=1, source_target_pairs={{0,1},{2,0},{4,2},{6,4},{7,6},{5,7},{3,5},{1,3},{8,9},{10,8},{12,1... | collective-permute-start | bytes 1572872 | tf_op jit(solution)/shard_map/ppermute | solution.py:106
  22.5 21.1 %collective-permute-start.3 = (bf16[128,2048]{1,0:T(8,128)(2,1)}, bf16[128,2048]{1,0:T(8,128)(2,1)S(1)}, u32[]{:S(2)}, u32[]{:S(2)}) collective-permute-start(bf16[128,2048]{1,0:T(8,128)(2,1)} %collective-permute-done.1), channel_id=1, source_target_pairs={{0,2},{2,4},{4,6},{6,7},{7,5},{5,3},{3,1},{1,0},{8,10},{10,12},{12... | collective-permute-start | bytes 1572872 | tf_op jit(solution)/shard_map/ppermute | solution.py:106
  43.6 16.6 %collective-permute-start.4 = (bf16[128,2048]{1,0:T(8,128)(2,1)S(1)}, bf16[128,2048]{1,0:T(8,128)(2,1)S(1)}, u32[]{:S(2)}, u32[]{:S(2)}) collective-permute-start(bf16[128,2048]{1,0:T(8,128)(2,1)S(1)} %collective-permute-done.2), channel_id=1, source_target_pairs={{0,1},{2,0},{4,2},{6,4},{7,6},{5,7},{3,5},{1,3},{8,9},{10,8},{12,1... | collective-permute-start | bytes 1572872 | tf_op jit(solution)/shard_map/ppermute | solution.py:106
  43.9 16.6 %collective-permute-start.5 = (bf16[128,2048]{1,0:T(8,128)(2,1)S(1)}, bf16[128,2048]{1,0:T(8,128)(2,1)S(1)}, u32[]{:S(2)}, u32[]{:S(2)}) collective-permute-start(bf16[128,2048]{1,0:T(8,128)(2,1)S(1)} %collective-permute-done.3), channel_id=1, source_target_pairs={{0,2},{2,4},{4,6},{6,7},{7,5},{5,3},{3,1},{1,0},{8,10},{10,12},{12... | collective-permute-start | bytes 1572872 | tf_op jit(solution)/shard_map/ppermute | solution.py:106
  49.8 29.1 %collective-permute-start.8 = (bf16[512,768]{1,0:T(8,128)(2,1)}, bf16[512,768]{1,0:T(8,128)(2,1)}, u32[]{:S(2)}, u32[]{:S(2)}) collective-permute-start(bf16[512,768]{1,0:T(8,128)(2,1)} %bitcast.25), channel_id=1, source_target_pairs={{0,16},{8,24},{16,0},{24,8},{1,17},{9,25},{17,1},{25,9},{2,18},{10... | collective-permute-start | bytes 2359304 | tf_op jit(solution)/shard_map/ppermute | solution.py:48
  63.7 43.8 %collective-permute-start.10 = (bf16[64,2048]{1,0:T(8,128)(2,1)}, bf16[64,2048]{1,0:T(8,128)(2,1)}, u32[]{:S(2)}, u32[]{:S(2)}) collective-permute-start(bf16[64,2048]{1,0:T(8,128)(2,1)} %param.18), channel_id=1, source_target_pairs={{0,0},{4,1},{8,2},{12,3},{16,4},{20,5},{24,6},{28,7},{1,8},{5,9},{... | collective-permute-start | bytes 786440 | tf_op jit(solution)/shard_map/ppermute | solution.py:422
  69.2 80.8 %all-to-all-start.1 = ((bf16[8,64,3072]{2,1,0:T(8,128)(2,1)}), bf16[8,64,3072]{2,1,0:T(8,128)(2,1)S(1)}, u32[]{:S(2)}, u32[]{:S(2)}) async-start(bf16[8,64,3072]{2,1,0:T(8,128)(2,1)} %pad_maximum_fusion.2), calls=%async_computation.1 | async-start | bytes 6291456 | tf_op jit(solution)/shard_map/all_to_all | solution.py:393
  159.2 12.4 %collective-permute-start.15 = (bf16[128,2048]{1,0:T(8,128)(2,1)S(1)}, bf16[128,2048]{1,0:T(8,128)(2,1)S(1)}, u32[]{:S(2)}, u32[]{:S(2)}) collective-permute-start(bf16[128,2048]{1,0:T(8,128)(2,1)S(1)} %pad_maximum_fusion.11), channel_id=1, source_target_pairs={{0,2},{2,4},{4,6},{6,7},{7,5},{5,3},{3,1},{1,0},{8,10},{10,12},{12... | collective-permute-start | bytes 1572872 | tf_op jit(solution)/shard_map/ppermute | solution.py:106
  159.5 12.3 %collective-permute-start.16 = (bf16[128,2048]{1,0:T(8,128)(2,1)S(1)}, bf16[128,2048]{1,0:T(8,128)(2,1)S(1)}, u32[]{:S(2)}, u32[]{:S(2)}) collective-permute-start(bf16[128,2048]{1,0:T(8,128)(2,1)S(1)} %pad_maximum_fusion.12), channel_id=1, source_target_pairs={{0,1},{2,0},{4,2},{6,4},{7,6},{5,7},{3,5},{1,3},{8,9},{10,8},{12,1... | collective-permute-start | bytes 1572872 | tf_op jit(solution)/shard_map/ppermute | solution.py:106
  177.3 44.9 %collective-permute-start.23 = (bf16[512,2048]{1,0:T(8,128)(2,1)}, bf16[512,2048]{1,0:T(8,128)(2,1)}, u32[]{:S(2)}, u32[]{:S(2)}) collective-permute-start(bf16[512,2048]{1,0:T(8,128)(2,1)} %slice.1036), channel_id=1, source_target_pairs={{0,16},{8,24},{16,0},{24,8},{1,17},{9,25},{17,1},{25,9},{2,18},{10... | collective-permute-start | bytes 6291464 | tf_op jit(solution)/shard_map/ppermute | solution.py:48
  202.0 24.4 %collective-permute-start.21 = (bf16[128,2048]{1,0:T(8,128)(2,1)S(1)}, bf16[128,2048]{1,0:T(8,128)(2,1)S(1)}, u32[]{:S(2)}, u32[]{:S(2)}) collective-permute-start(bf16[128,2048]{1,0:T(8,128)(2,1)S(1)} %multiply_convert_fusion.3), channel_id=1, source_target_pairs={{0,1},{2,0},{4,2},{6,4},{7,6},{5,7},{3,5},{1,3},{8,9},{10,8},{12,1... | collective-permute-start | bytes 1572872 | tf_op jit(solution)/shard_map/ppermute | solution.py:106
  203.3 23.1 %collective-permute-start.22 = (bf16[128,2048]{1,0:T(8,128)(2,1)S(1)}, bf16[128,2048]{1,0:T(8,128)(2,1)S(1)}, u32[]{:S(2)}, u32[]{:S(2)}) collective-permute-start(bf16[128,2048]{1,0:T(8,128)(2,1)S(1)} %multiply_convert_fusion.3), channel_id=1, source_target_pairs={{0,2},{2,4},{4,6},{6,7},{7,5},{5,3},{3,1},{1,0},{8,10},{10,12},{12... | collective-permute-start | bytes 1572872 | tf_op jit(solution)/shard_map/ppermute | solution.py:106
  224.7 28.6 %collective-permute-start.31 = (bf16[512,1024]{1,0:T(8,128)(2,1)S(1)}, bf16[512,1024]{1,0:T(8,128)(2,1)S(1)}, u32[]{:S(2)}, u32[]{:S(2)}) collective-permute-start(bf16[512,1024]{1,0:T(8,128)(2,1)S(1)} %slice.1055), channel_id=1, source_target_pairs={{0,16},{8,24},{16,0},{24,8},{1,17},{9,25},{17,1},{25,9},{2,18},{10... | collective-permute-start | bytes 3145736 | tf_op jit(solution)/shard_map/ppermute | solution.py:48
  228.6 57.0 %collective-permute-start.30 = (bf16[1024,2048]{1,0:T(8,128)(2,1)S(1)}, bf16[1024,2048]{1,0:T(8,128)(2,1)S(1)}, u32[]{:S(2)}, u32[]{:S(2)}) collective-permute-start(bf16[1024,2048]{1,0:T(8,128)(2,1)S(1)} %pad_maximum_fusion), channel_id=1, source_target_pairs={{0,8},{8,0},{16,24},{24,16},{1,9},{9,1},{17,25},{25,17},{2,10},{10... | collective-permute-start | bytes 12582920 | tf_op jit(solution)/shard_map/ppermute | solution.py:48
  239.0 12.2 %collective-permute-start.27 = (bf16[128,2048]{1,0:T(8,128)(2,1)S(1)}, bf16[128,2048]{1,0:T(8,128)(2,1)S(1)}, u32[]{:S(2)}, u32[]{:S(2)}) collective-permute-start(bf16[128,2048]{1,0:T(8,128)(2,1)S(1)} %collective-permute-done.25), channel_id=1, source_target_pairs={{0,2},{2,4},{4,6},{6,7},{7,5},{5,3},{3,1},{1,0},{8,10},{10,12},{12... | collective-permute-start | bytes 1572872 | tf_op jit(solution)/shard_map/ppermute | solution.py:106
  262.9 13.5 %collective-permute-start.34 = (bf16[128,2048]{1,0:T(8,128)(2,1)S(1)}, bf16[128,2048]{1,0:T(8,128)(2,1)S(1)}, u32[]{:S(2)}, u32[]{:S(2)}) collective-permute-start(bf16[128,2048]{1,0:T(8,128)(2,1)S(1)} %fusion.39), channel_id=1, source_target_pairs={{0,1},{2,0},{4,2},{6,4},{7,6},{5,7},{3,5},{1,3},{8,9},{10,8},{12,1... | collective-permute-start | bytes 1572872 | tf_op jit(solution)/shard_map/ppermute | solution.py:106
  277.3 24.4 %collective-permute-start.32 = (bf16[1024,1024]{1,0:T(8,128)(2,1)S(1)}, bf16[1024,1024]{1,0:T(8,128)(2,1)}, u32[]{:S(2)}, u32[]{:S(2)}) collective-permute-start(bf16[1024,1024]{1,0:T(8,128)(2,1)S(1)} %constant_dynamic-update-slice_fusion.84), channel_id=1, source_target_pairs={{0,8},{8,0},{16,24},{24,16},{1,9},{9,1},{17,25},{25,17},{2,10},{10... | collective-permute-start | bytes 6291464 | tf_op jit(solution)/shard_map/ppermute | solution.py:48
  277.3 18.4 %collective-permute-start.35 = (bf16[128,2048]{1,0:T(8,128)(2,1)S(1)}, bf16[128,2048]{1,0:T(8,128)(2,1)S(1)}, u32[]{:S(2)}, u32[]{:S(2)}) collective-permute-start(bf16[128,2048]{1,0:T(8,128)(2,1)S(1)} %collective-permute-done.33), channel_id=1, source_target_pairs={{0,2},{2,4},{4,6},{6,7},{7,5},{5,3},{3,1},{1,0},{8,10},{10,12},{12... | collective-permute-start | bytes 1572872 | tf_op jit(solution)/shard_map/ppermute | solution.py:106
  317.9 12.7 %collective-permute-start.41 = (bf16[128,1024]{1,0:T(8,128)(2,1)S(1)}, bf16[128,1024]{1,0:T(8,128)(2,1)S(1)}, u32[]{:S(2)}, u32[]{:S(2)}) collective-permute-start(bf16[128,1024]{1,0:T(8,128)(2,1)S(1)} %get-tuple-element.126), channel_id=1, source_target_pairs={{0,2},{2,4},{4,6},{6,7},{7,5},{5,3},{3,1},{1,0},{8,10},{10,12},{12... | collective-permute-start | bytes 786440 | tf_op jit(solution)/shard_map/ppermute | solution.py:106
  318.9 12.1 %collective-permute-start.42 = (bf16[128,1024]{1,0:T(8,128)(2,1)S(1)}, bf16[128,1024]{1,0:T(8,128)(2,1)S(1)}, u32[]{:S(2)}, u32[]{:S(2)}) collective-permute-start(bf16[128,1024]{1,0:T(8,128)(2,1)S(1)} %get-tuple-element.127), channel_id=1, source_target_pairs={{0,1},{2,0},{4,2},{6,4},{7,6},{5,7},{3,5},{1,3},{8,9},{10,8},{12,1... | collective-permute-start | bytes 786440 | tf_op jit(solution)/shard_map/ppermute | solution.py:106
  331.4 13.6 %collective-permute-start.43 = (bf16[128,2048]{1,0:T(8,128)(2,1)S(1)}, bf16[128,2048]{1,0:T(8,128)(2,1)S(1)}, u32[]{:S(2)}, u32[]{:S(2)}) collective-permute-start(bf16[128,2048]{1,0:T(8,128)(2,1)S(1)} %pad_maximum_fusion.14), channel_id=1, source_target_pairs={{0,2},{2,4},{4,6},{6,7},{7,5},{5,3},{3,1},{1,0},{8,10},{10,12},{12... | collective-permute-start | bytes 1572872 | tf_op jit(solution)/shard_map/ppermute | solution.py:106
  332.5 13.0 %collective-permute-start.44 = (bf16[128,2048]{1,0:T(8,128)(2,1)S(1)}, bf16[128,2048]{1,0:T(8,128)(2,1)S(1)}, u32[]{:S(2)}, u32[]{:S(2)}) collective-permute-start(bf16[128,2048]{1,0:T(8,128)(2,1)S(1)} %pad_maximum_fusion.15), channel_id=1, source_target_pairs={{0,1},{2,0},{4,2},{6,4},{7,6},{5,7},{3,5},{1,3},{8,9},{10,8},{12,1... | collective-permute-start | bytes 1572872 | tf_op jit(solution)/shard_map/ppermute | solution.py:106
  345.6 12.4 %collective-permute-start.45 = (bf16[128,2048]{1,0:T(8,128)(2,1)S(1)}, bf16[128,2048]{1,0:T(8,128)(2,1)S(1)}, u32[]{:S(2)}, u32[]{:S(2)}) collective-permute-start(bf16[128,2048]{1,0:T(8,128)(2,1)S(1)} %fusion.26), channel_id=1, source_target_pairs={{0,2},{2,4},{4,6},{6,7},{7,5},{5,3},{3,1},{1,0},{8,10},{10,12},{12... | collective-permute-start | bytes 1572872 | tf_op jit(solution)/shard_map/ppermute | solution.py:106
  346.7 12.1 %collective-permute-start.46 = (bf16[128,2048]{1,0:T(8,128)(2,1)S(1)}, bf16[128,2048]{1,0:T(8,128)(2,1)S(1)}, u32[]{:S(2)}, u32[]{:S(2)}) collective-permute-start(bf16[128,2048]{1,0:T(8,128)(2,1)S(1)} %fusion.27), channel_id=1, source_target_pairs={{0,1},{2,0},{4,2},{6,4},{7,6},{5,7},{3,5},{1,3},{8,9},{10,8},{12,1... | collective-permute-start | bytes 1572872 | tf_op jit(solution)/shard_map/ppermute | solution.py:106
  375.1 25.6 %collective-permute-start.55 = (bf16[1024,1024]{1,0:T(8,128)(2,1)}, bf16[1024,1024]{1,0:T(8,128)(2,1)}, u32[]{:S(2)}, u32[]{:S(2)}) collective-permute-start(bf16[1024,1024]{1,0:T(8,128)(2,1)} %convolution_convert_fusion.1), channel_id=1, source_target_pairs={{0,8},{8,0},{16,24},{24,16},{1,9},{9,1},{17,25},{25,17},{2,10},{10... | collective-permute-start | bytes 6291464 | tf_op jit(solution)/shard_map/ppermute | solution.py:48
  384.1 13.5 %collective-permute-start.51 = (bf16[128,2048]{1,0:T(8,128)(2,1)S(1)}, bf16[128,2048]{1,0:T(8,128)(2,1)S(1)}, u32[]{:S(2)}, u32[]{:S(2)}) collective-permute-start(bf16[128,2048]{1,0:T(8,128)(2,1)S(1)} %pad_maximum_fusion.17), channel_id=1, source_target_pairs={{0,2},{2,4},{4,6},{6,7},{7,5},{5,3},{3,1},{1,0},{8,10},{10,12},{12... | collective-permute-start | bytes 1572872 | tf_op jit(solution)/shard_map/ppermute | solution.py:106
  385.2 13.2 %collective-permute-start.52 = (bf16[128,2048]{1,0:T(8,128)(2,1)S(1)}, bf16[128,2048]{1,0:T(8,128)(2,1)S(1)}, u32[]{:S(2)}, u32[]{:S(2)}) collective-permute-start(bf16[128,2048]{1,0:T(8,128)(2,1)S(1)} %pad_maximum_fusion.18), channel_id=1, source_target_pairs={{0,1},{2,0},{4,2},{6,4},{7,6},{5,7},{3,5},{1,3},{8,9},{10,8},{12,1... | collective-permute-start | bytes 1572872 | tf_op jit(solution)/shard_map/ppermute | solution.py:106
  392.5 33.4 %collective-permute-start.58 = (bf16[1024,2048]{1,0:T(8,128)(2,1)}, bf16[1024,2048]{1,0:T(8,128)(2,1)S(1)}, u32[]{:S(2)}, u32[]{:S(2)}) collective-permute-start(bf16[1024,2048]{1,0:T(8,128)(2,1)} %convolution_convert_fusion), channel_id=1, source_target_pairs={{0,8},{8,0},{16,24},{24,16},{1,9},{9,1},{17,25},{25,17},{2,10},{10... | collective-permute-start | bytes 12582920 | tf_op jit(solution)/shard_map/ppermute | solution.py:48
  398.6 12.4 %collective-permute-start.53 = (bf16[128,2048]{1,0:T(8,128)(2,1)S(1)}, bf16[128,2048]{1,0:T(8,128)(2,1)S(1)}, u32[]{:S(2)}, u32[]{:S(2)}) collective-permute-start(bf16[128,2048]{1,0:T(8,128)(2,1)S(1)} %fusion.31), channel_id=1, source_target_pairs={{0,2},{2,4},{4,6},{6,7},{7,5},{5,3},{3,1},{1,0},{8,10},{10,12},{12... | collective-permute-start | bytes 1572872 | tf_op jit(solution)/shard_map/ppermute | solution.py:106
  414.5 33.3 %collective-permute-start.67 = (bf16[512,1024]{1,0:T(8,128)(2,1)S(1)}, bf16[512,1024]{1,0:T(8,128)(2,1)S(1)}, u32[]{:S(2)}, u32[]{:S(2)}) collective-permute-start(bf16[512,1024]{1,0:T(8,128)(2,1)S(1)} %slice.1546), channel_id=1, source_target_pairs={{0,16},{8,24},{16,0},{24,8},{1,17},{9,25},{17,1},{25,9},{2,18},{10... | collective-permute-start | bytes 3145736 | tf_op jit(solution)/shard_map/ppermute | solution.py:48
  460.0 13.0 %collective-permute-start.64 = (bf16[128,2048]{1,0:T(8,128)(2,1)S(1)}, bf16[128,2048]{1,0:T(8,128)(2,1)S(1)}, u32[]{:S(2)}, u32[]{:S(2)}) collective-permute-start(bf16[128,2048]{1,0:T(8,128)(2,1)S(1)} %collective-permute-done.62), channel_id=1, source_target_pairs={{0,2},{2,4},{4,6},{6,7},{7,5},{5,3},{3,1},{1,0},{8,10},{10,12},{12... | collective-permute-start | bytes 1572872 | tf_op jit(solution)/shard_map/ppermute | solution.py:106
  462.7 38.8 %collective-permute-start.68 = (bf16[512,2048]{1,0:T(8,128)(2,1)}, bf16[512,2048]{1,0:T(8,128)(2,1)}, u32[]{:S(2)}, u32[]{:S(2)}) collective-permute-start(bf16[512,2048]{1,0:T(8,128)(2,1)} %slice.1545), channel_id=1, source_target_pairs={{0,16},{8,24},{16,0},{24,8},{1,17},{9,25},{17,1},{25,9},{2,18},{10... | collective-permute-start | bytes 6291464 | tf_op jit(solution)/shard_map/ppermute | solution.py:48
  476.3 29.0 %all-to-all-start.2 = ((bf16[8,64,1024]{2,1,0:T(8,128)(2,1)}), bf16[8,64,1024]{2,1,0:T(8,128)(2,1)S(1)}, u32[]{:S(2)}, u32[]{:S(2)}) async-start(bf16[8,64,1024]{2,1,0:T(8,128)(2,1)} %bitcast.57), calls=%async_computation.2 | async-start | bytes 2097152 | tf_op jit(solution)/shard_map/all_to_all | solution.py:393
  480.1 12.4 %collective-permute-start.66 = (bf16[64,2048]{1,0:T(8,128)(2,1)S(1)}, bf16[64,2048]{1,0:T(8,128)(2,1)S(1)}, u32[]{:S(2)}, u32[]{:S(2)}) collective-permute-start(bf16[64,2048]{1,0:T(8,128)(2,1)S(1)} %slice.1107), channel_id=1, source_target_pairs={{0,1},{2,0},{4,2},{6,4},{7,6},{5,7},{3,5},{1,3},{8,9},{10,8},{12,1... | collective-permute-start | bytes 786440 | tf_op jit(solution)/shard_map/ppermute | solution.py:106
  500.7 15.8 %collective-permute-start.79 = (bf16[128,2048]{1,0:T(8,128)(2,1)}, bf16[128,2048]{1,0:T(8,128)(2,1)}, u32[]{:S(2)}, u32[]{:S(2)}) collective-permute-start(bf16[128,2048]{1,0:T(8,128)(2,1)} %pad_maximum_fusion.22), channel_id=1, source_target_pairs={{0,8},{8,0},{16,24},{24,16},{1,9},{9,1},{17,25},{25,17},{2,10},{10... | collective-permute-start | bytes 1572872 | tf_op jit(solution)/shard_map/ppermute | solution.py:48
  505.4 59.0 %all-to-all-start.3 = ((bf16[8,64,2048]{2,1,0:T(8,128)(2,1)}), bf16[8,64,2048]{2,1,0:T(8,128)(2,1)}, u32[]{:S(2)}, u32[]{:S(2)}) async-start(bf16[8,64,2048]{2,1,0:T(8,128)(2,1)} %bitcast.422), calls=%async_computation.3 | async-start | bytes 4194304 | tf_op jit(solution)/shard_map/all_to_all | solution.py:393
  567.9 16.6 %collective-permute-start.71 = (bf16[1024,768]{1,0:T(8,128)(2,1)S(1)}, bf16[1024,768]{1,0:T(8,128)(2,1)S(1)}, u32[]{:S(2)}, u32[]{:S(2)}) collective-permute-start(bf16[1024,768]{1,0:T(8,128)(2,1)S(1)} %convolution_convert_fusion.2), channel_id=1, source_target_pairs={{0,8},{8,0},{16,24},{24,16},{1,9},{9,1},{17,25},{25,17},{2,10},{10... | collective-permute-start | bytes 4718600 | tf_op jit(solution)/shard_map/ppermute | solution.py:48
  587.1 13.5 %collective-permute-start.72 = (bf16[128,2048]{1,0:T(8,128)(2,1)S(1)}, bf16[128,2048]{1,0:T(8,128)(2,1)S(1)}, u32[]{:S(2)}, u32[]{:S(2)}) collective-permute-start(bf16[128,2048]{1,0:T(8,128)(2,1)S(1)} %pad_maximum_fusion.19), channel_id=1, source_target_pairs={{0,2},{2,4},{4,6},{6,7},{7,5},{5,3},{3,1},{1,0},{8,10},{10,12},{12... | collective-permute-start | bytes 1572872 | tf_op jit(solution)/shard_map/ppermute | solution.py:106
  589.5 13.5 %collective-permute-start.73 = (bf16[128,2048]{1,0:T(8,128)(2,1)S(1)}, bf16[128,2048]{1,0:T(8,128)(2,1)S(1)}, u32[]{:S(2)}, u32[]{:S(2)}) collective-permute-start(bf16[128,2048]{1,0:T(8,128)(2,1)S(1)} %pad_maximum_fusion.20), channel_id=1, source_target_pairs={{0,1},{2,0},{4,2},{6,4},{7,6},{5,7},{3,5},{1,3},{8,9},{10,8},{12,1... | collective-permute-start | bytes 1572872 | tf_op jit(solution)/shard_map/ppermute | solution.py:106
  592.3 18.6 %collective-permute-start.76 = (bf16[512,768]{1,0:T(8,128)(2,1)S(1)}, bf16[512,768]{1,0:T(8,128)(2,1)S(1)}, u32[]{:S(2)}, u32[]{:S(2)}) collective-permute-start(bf16[512,768]{1,0:T(8,128)(2,1)S(1)} %slice.1547), channel_id=1, source_target_pairs={{0,16},{8,24},{16,0},{24,8},{1,17},{9,25},{17,1},{25,9},{2,18},{10... | collective-permute-start | bytes 2359304 | tf_op jit(solution)/shard_map/ppermute | solution.py:48
  603.9 17.4 %collective-permute-start.74 = (bf16[128,2048]{1,0:T(8,128)(2,1)}, bf16[128,2048]{1,0:T(8,128)(2,1)}, u32[]{:S(2)}, u32[]{:S(2)}) collective-permute-start(bf16[128,2048]{1,0:T(8,128)(2,1)} %fusion.36), channel_id=1, source_target_pairs={{0,2},{2,4},{4,6},{6,7},{7,5},{5,3},{3,1},{1,0},{8,10},{10,12},{12... | collective-permute-start | bytes 1572872 | tf_op jit(solution)/shard_map/ppermute | solution.py:106
  605.2 16.1 %collective-permute-start.75 = (bf16[128,2048]{1,0:T(8,128)(2,1)}, bf16[128,2048]{1,0:T(8,128)(2,1)}, u32[]{:S(2)}, u32[]{:S(2)}) collective-permute-start(bf16[128,2048]{1,0:T(8,128)(2,1)} %fusion.37), channel_id=1, source_target_pairs={{0,1},{2,0},{4,2},{6,4},{7,6},{5,7},{3,5},{1,3},{8,9},{10,8},{12,1... | collective-permute-start | bytes 1572872 | tf_op jit(solution)/shard_map/ppermute | solution.py:106
  612.0 30.9 %all-to-all-start.4 = ((bf16[8,64,768]{2,1,0:T(8,128)(2,1)}), bf16[8,64,768]{2,1,0:T(8,128)(2,1)}, u32[]{:S(2)}, u32[]{:S(2)}) async-start(bf16[8,64,768]{2,1,0:T(8,128)(2,1)} %bitcast.425), calls=%async_computation.4 | async-start | bytes 1572864 | tf_op jit(solution)/shard_map/all_to_all | solution.py:393
  642.9 17.0 %collective-permute-start.77 = (bf16[128,2048]{1,0:T(8,128)(2,1)S(1)}, bf16[128,2048]{1,0:T(8,128)(2,1)S(1)}, u32[]{:S(2)}, u32[]{:S(2)}) collective-permute-start(bf16[128,2048]{1,0:T(8,128)(2,1)S(1)} %fusion.35), channel_id=1, source_target_pairs={{0,2},{2,4},{4,6},{6,7},{7,5},{5,3},{3,1},{1,0},{8,10},{10,12},{12... | collective-permute-start | bytes 1572872 | tf_op jit(solution)/shard_map/ppermute | solution.py:106
  647.7 14.4 %collective-permute-start.78 = (bf16[128,2048]{1,0:T(8,128)(2,1)S(1)}, bf16[128,2048]{1,0:T(8,128)(2,1)S(1)}, u32[]{:S(2)}, u32[]{:S(2)}) collective-permute-start(bf16[128,2048]{1,0:T(8,128)(2,1)S(1)} %fusion.38), channel_id=1, source_target_pairs={{0,1},{2,0},{4,2},{6,4},{7,6},{5,7},{3,5},{1,3},{8,9},{10,8},{12,1... | collective-permute-start | bytes 1572872 | tf_op jit(solution)/shard_map/ppermute | solution.py:106
  (119 other events, 1557.3 us)

commit v5 on v4

--- a/solution.py
+++ b/solution.py
@@ -425,8 +425,11 @@
     ffn_columns = to_columns(
         [scaled(gate_weight, gain_two), scaled(up_weight, gain_two), down_weight], ring.done
     )
-    ffn_half = shares.gather_far(ffn_columns[:, : 2 * hidden_local])
-    down_half = shares.gather_far(ffn_columns[:, 2 * hidden_local :], (ffn_half,))
+    ffn_parts = []
+    for part in jnp.split(ffn_columns, 6, axis=1):
+        ffn_parts.append(shares.gather_far(part, ffn_parts[-1:]))
+    ffn_half = jnp.concatenate(ffn_parts[:4], axis=1)
+    down_half = jnp.concatenate(ffn_parts[4:], axis=1)
     attention = Attention(size, groups, slots, local, head_size, lengths, owners)
     mixed, query_rot, key_rot, value_low, lse = attention.forward(projected)
     mixed = mixed.reshape(size * rows, local)
@@ -439,12 +442,12 @@
     )
     attn_out = contract(mixed, mix_rows, 1, 0)
     residual = block_in + ring.scatter_sum(
-        attn_out[:, : width // 2], attn_out[:, width // 2 :], ((ffn_columns,),)
+        attn_out[:, : width // 2], attn_out[:, width // 2 :], ((ffn_columns,), ffn_parts[:1], ffn_parts[1:2], ffn_parts[2:3])
     )
 
     ffn_weights = (ffn_half, shares.swap(ffn_half, 1))
     normed_two, factor_two = normalize(residual)
-    two_all = halves(ring.gather(normed_two.astype(BF16), ((), (ffn_half,))))
+    two_all = halves(ring.gather(normed_two.astype(BF16), (ffn_parts[3:4], (), ffn_parts[4:5], ffn_parts[5:])))
     down_weights = (down_half, shares.swap(down_half, 1))
     low_part = contract(two_all[0], ffn_weights[0], 1, 0)
     gate_up = low_part + contract(two_all[1], ffn_weights[1], 1, 0)
@@ -453,7 +456,7 @@
     silu_gate = gate * sigma
     hidden = (silu_gate * up).astype(BF16)
     grad_all = halves(
-        ring.gather(grad_out.astype(BF16), fill=((), (low_part, down_half), (gate_up,), (hidden,)))
+        ring.gather(grad_out.astype(BF16), fill=((), (low_part,), (gate_up,), (hidden,)))
     )
     branch = ring.scatter_sum(*(contract(hidden, w, 1, 1) for w in down_weights))
     activations = valid * (residual + branch)
@@ -497,7 +500,8 @@
     )
     (projected_grad,) = tie([projected_grad], (both_rows,))
     attn_given, attn_half = summed(one_all, projected_grad)
-    attn_rows = to_rows(shares.scatter_rest(attn_half))
+    attn_sum = shares.scatter_rest(attn_half)
+    attn_rows = to_rows(attn_sum)
     mix_terms = shares.from_order(contract(mixed, dres_all, 0, 0))
     mix_blocks = shares.relative(jnp.split(mix_terms, count, axis=0))
     mix_blocks = [mix_blocks[k] for k in shares.order]
@@ -507,7 +511,7 @@
     )
     scaled_one = ring.scatter_sum(
         *(contract(projected_grad, w, 1, 1) for w in attn_weights),
-        fill=((attn_given,), (attn_half,), (), (attn_rows,)),
+        fill=((attn_given,), (attn_half,), (), (attn_sum,)),
     )
     input_grad = dres + factor_one * (
         scaled_one - normed_one * jnp.mean(normed_one * scaled_one, axis=-1, keepdims=True)

time: 670 us -> 661 us (0.987)
  waiting for transfers between devices: 299 us -> 281 us
  local copies, waits for them, and re-layouts: 54.1 us -> 61.1 us
    all_to_all x5, waiting for transfers between devices: 62.5 us -> 34.3 us  [exchange(): return lax.all_to_all(tie([blocks], done)[0], 'ctx', 0, 0, tiled=True)]
    ppermute x64, waiting for transfers between devices: 200 us -> 213 us  [shift(): return lax.ppermute(value, 'ctx', pairs)]
    ppermute x16 -> x20, starting transfers between devices: 9.31 us -> 21 us  [swap(): return lax.ppermute(value, 'dp', [(i, i ^ bit) for i in range(self.count)])]
    unnamed x255 -> x279, local copies, waits for them, and re-layouts: 38.9 us -> 45.8 us
    ppermute x16 -> x20, waiting for transfers between devices: 36.7 us -> 34 us  [swap(): return lax.ppermute(value, 'dp', [(i, i ^ bit) for i in range(self.count)])]
  transfers between devices with their start and end apart: 87 -> 91, of which waited for: 58 -> 53; matrix products, arithmetic and copies ran while one was open for 29% -> 29% of each run, Pallas kernels for 4% -> 4%
where the time goes in v5:
time: 661 us; the launch traced here: 655 us
  waiting for transfers between devices  281 us (43%)
  starting transfers between devices  130 us (20%)
  matrix products  96.9 us (15%)
  local copies, waits for them, and re-layouts  61.1 us (9%)
  other arithmetic  58.6 us (9%)
  Pallas kernels  23.5 us (4%)
    ppermute x64, waiting for transfers between devices, shift(): return lax.ppermute(value, 'ctx', pairs)  213 us
    dot_general x21, matrix products, contract(): lax.dot_general(left, right, (((left_dim,), (right_dim,)), ((), ())), pre...  96.9 us
    ppermute x64, starting transfers between devices, shift(): return lax.ppermute(value, 'ctx', pairs)  72.6 us
    unnamed x279, local copies, waits for them, and re-layouts  45.8 us
    all_to_all x5, waiting for transfers between devices, exchange(): return lax.all_to_all(tie([blocks], done)[0], 'ctx', 0, 0, tiled=True)  34.3 us
    ppermute x20, waiting for transfers between devices, swap(): return lax.ppermute(value, 'dp', [(i, i ^ bit) for i in range(self.count)])  34 us
    all_to_all x5, starting transfers between devices, exchange(): return lax.all_to_all(tie([blocks], done)[0], 'ctx', 0, 0, tiled=True)  31.1 us
    ppermute x20, starting transfers between devices, swap(): return lax.ppermute(value, 'dp', [(i, i ^ bit) for i in range(self.count)])  21 us
  transfers between devices with their start and end apart: 91, of which 53 were waited for; matrix products, arithmetic and copies ran while one was open for 29% of the time, Pallas kernels for 4%

profile of v5, /device:TPU:0, one launch (start us, length us, event | category | flops | bytes accessed | tf_op | source)
XLA Modules:
  0.0 654.9 jit_solution(9825867926927445258)
XLA Ops:
  7.8 6.4 all-to-all-start
  26.6 15.6 %collective-permute-done.2 = bf16[128,2048]{1,0:T(8,128)(2,1)S(1)} collective-permute-done((bf16[128,2048]{1,0:T(8,128)(2,1)}, bf16[128,2048]{1,0:T(8,128)(2,1)S(1)}, u32[]{:S(2)}, u32[]{:S(2)}) %collective-permute-start.2) | collective-permute-done | bytes 524320 | tf_op jit(solution)/shard_map/ppermute | solution.py:106
  53.3 8.2 %collective-permute-done.5 = bf16[128,2048]{1,0:T(8,128)(2,1)S(1)} collective-permute-done((bf16[128,2048]{1,0:T(8,128)(2,1)S(1)}, bf16[128,2048]{1,0:T(8,128)(2,1)S(1)}, u32[]{:S(2)}, u32[]{:S(2)}) %collective-permute-start.5) | collective-permute-done | bytes 524320 | tf_op jit(solution)/shard_map/ppermute | solution.py:106
  69.2 9.8 %all-to-all-start.1 = ((bf16[8,64,3072]{2,1,0:T(8,128)(2,1)}), bf16[8,64,3072]{2,1,0:T(8,128)(2,1)S(1)}, u32[]{:S(2)}, u32[]{:S(2)}) async-start(bf16[8,64,3072]{2,1,0:T(8,128)(2,1)} %pad_maximum_fusion.2), calls=%async_computation.1 | async-start | bytes 6291456 | tf_op jit(solution)/shard_map/all_to_all | solution.py:393
  86.1 4.7 fusion.86
  90.8 4.8 convolution_add_fusion.2
  97.1 10.6 %attention_forward.1 = (bf16[8,2,64,256]{3,2,1,0:T(8,128)(2,1)}, bf16[8,2,64,256]{3,2,1,0:T(8,128)(2,1)}, bf16[8,2,64,256]{3,2,1,0:T(8,128)(2,1)}, bf16[8,2,64,256]{3,2,1,0:T(8,128)(2,1)}, f32[2,512,4]{2,1,0:T(8,128)}) custom-call(s32[2]{0:T(128)} %lengths_ref.3, f32[8,2,64,768]{3,2,1,0:T(8,128)} %bitcast.417, f32[8,2,64,768]{3,2,1,0:T(8,128)} %bitcast.418, ...), custom_call_target="tpu_custom_call" | custom-call | flops 536870912 | bytes 4194304 | tf_op jit(solution)/shard_map/attention_forward/pallas_call | solution.py:329
  107.7 12.4 %collective-permute-start.11 = (bf16[64,2048]{1,0:T(8,128)(2,1)}, bf16[64,2048]{1,0:T(8,128)(2,1)S(1)}, u32[]{:S(2)}, u32[]{:S(2)}) collective-permute-start(bf16[64,2048]{1,0:T(8,128)(2,1)} %collective-permute-done.10), channel_id=1, source_target_pairs={{0,16},{8,24},{16,0},{24,8},{1,17},{9,25},{17,1},{25,9},{2,18},{10... | collective-permute-start | bytes 786440 | tf_op jit(solution)/shard_map/ppermute | solution.py:48
  120.1 6.7 %collective-permute-done.11 = bf16[64,2048]{1,0:T(8,128)(2,1)S(1)} collective-permute-done((bf16[64,2048]{1,0:T(8,128)(2,1)}, bf16[64,2048]{1,0:T(8,128)(2,1)S(1)}, u32[]{:S(2)}, u32[]{:S(2)}) %collective-permute-start.11) | collective-permute-done | bytes 262176 | tf_op jit(solution)/shard_map/ppermute | solution.py:48
  131.8 4.5 fusion.79
  137.4 13.4 %all-to-all-done.1 = bf16[8,64,3072]{2,1,0:T(8,128)(2,1)S(1)} async-done(((bf16[8,64,3072]{2,1,0:T(8,128)(2,1)}), bf16[8,64,3072]{2,1,0:T(8,128)(2,1)S(1)}, u32[]{:S(2)}, u32[]{:S(2)}) %all-to-all-start.1) | async-done | bytes 3145760 | tf_op jit(solution)/shard_map/all_to_all | solution.py:393
  158.8 6.6 %collective-permute-done.15 = bf16[512,512]{1,0:T(8,128)(2,1)S(1)} collective-permute-done((bf16[512,512]{1,0:T(8,128)(2,1)S(1)}, bf16[512,512]{1,0:T(8,128)(2,1)S(1)}, u32[]{:S(2)}, u32[]{:S(2)}) %collective-permute-start.15) | collective-permute-done | bytes 524320 | tf_op jit(solution)/shard_map/ppermute | solution.py:48
  167.8 8.0 %collective-permute-done.17 = bf16[128,2048]{1,0:T(8,128)(2,1)S(1)} collective-permute-done((bf16[128,2048]{1,0:T(8,128)(2,1)S(1)}, bf16[128,2048]{1,0:T(8,128)(2,1)S(1)}, u32[]{:S(2)}, u32[]{:S(2)}) %collective-permute-start.17) | collective-permute-done | bytes 524320 | tf_op jit(solution)/shard_map/ppermute | solution.py:106
  182.6 6.1 collective-permute-done.20
  196.3 5.7 collective-permute-done.23
  209.5 11.7 %collective-permute-done.25 = bf16[128,2048]{1,0:T(8,128)(2,1)S(1)} collective-permute-done((bf16[128,2048]{1,0:T(8,128)(2,1)S(1)}, bf16[128,2048]{1,0:T(8,128)(2,1)S(1)}, u32[]{:S(2)}, u32[]{:S(2)}) %collective-permute-start.25) | collective-permute-done | bytes 524320 | tf_op jit(solution)/shard_map/ppermute | solution.py:106
  229.0 6.3 collective-permute-done.27
  237.6 11.1 %collective-permute-done.31 = bf16[128,2048]{1,0:T(8,128)(2,1)S(1)} collective-permute-done((bf16[128,2048]{1,0:T(8,128)(2,1)S(1)}, bf16[128,2048]{1,0:T(8,128)(2,1)S(1)}, u32[]{:S(2)}, u32[]{:S(2)}) %collective-permute-start.31) | collective-permute-done | bytes 524320 | tf_op jit(solution)/shard_map/ppermute | solution.py:106
  251.0 7.1 %collective-permute-done.33 = bf16[64,2048]{1,0:T(8,128)(2,1)S(1)} collective-permute-done((bf16[64,2048]{1,0:T(8,128)(2,1)S(1)}, bf16[64,2048]{1,0:T(8,128)(2,1)S(1)}, u32[]{:S(2)}, u32[]{:S(2)}) %collective-permute-start.33) | collective-permute-done | bytes 262176 | tf_op jit(solution)/shard_map/ppermute | solution.py:106
  260.8 6.8 %fusion.87 = f32[1024,2048]{1,0:T(8,128)} fusion(bf16[1024,1024]{1,0:T(8,128)(2,1)S(1)} %get-tuple-element.341, bf16[1024,2048]{1,0:T(8,128)(2,1)S(1)} %pad_maximum_fusion), kind=kOutput, calls=%fused_computation.522 | convolution fusion | flops 4294967296 | bytes 14680064 | tf_op jit(solution)/shard_map/dot_general | solution.py:25
  267.5 5.2 collective-permute-done.38
  275.3 6.6 %collective-permute-done.40 = bf16[128,2048]{1,0:T(8,128)(2,1)S(1)} collective-permute-done((bf16[128,2048]{1,0:T(8,128)(2,1)S(1)}, bf16[128,2048]{1,0:T(8,128)(2,1)S(1)}, u32[]{:S(2)}, u32[]{:S(2)}) %collective-permute-start.40) | collective-permute-done | bytes 524320 | tf_op jit(solution)/shard_map/ppermute | solution.py:106
  283.9 8.2 %convolution_add_fusion = f32[1024,2048]{1,0:T(8,128)S(1)} fusion(f32[1024,2048]{1,0:T(8,128)} %fusion.87, bf16[1024,1024]{1,0:T(8,128)(2,1)S(1)} %copy-done.66, bf16[1024,2048]{1,0:T(8,128)(2,1)} %copy-done.77), kind=kOutput, calls=%fused_computation.11 | convolution fusion | flops 4297064448 | bytes 23068672 | tf_op jit(solution)/shard_map/dot_general | solution.py:25
  308.1 6.2 collective-permute-done.43
  317.3 7.5 %fusion.88 = f32[1024,1024]{1,0:T(8,128)} fusion(bf16[1024,1024]{1,0:T(8,128)(2,1)S(1)} %get-tuple-element.317, bf16[1024,1024]{1,0:T(8,128)(2,1)} %collective-permute-done.36), kind=kOutput, calls=%fused_computation.523 | convolution fusion | flops 2147483648 | bytes 8388608 | tf_op jit(solution)/shard_map/dot_general | solution.py:25
  328.9 7.6 %multiply_convert_fusion.1 = (bf16[1024,1024]{1,0:T(8,128)(2,1)}, bf16[1024,1024]{1,0:T(8,128)(2,1)}) fusion(f32[1024,2048]{1,0:T(8,128)S(1)} %convolution_add_fusion, f32[1024,1024]{1,0:T(8,128)} %fusion.88, bf16[1024,1024]{1,0:T(8,128)(2,1)} %copy-done.61, bf16[1024,512]{1,0:T(8,128)(2,1)S(1)} %constant_dynamic-update-slice_fusion.74, ...), kind=kOutput, calls=%fused_computation.7 | convolution fusion | flops 2166358016 | bytes 20971520 | tf_op jit(solution)/shard_map/dot_general | solution.py:25
  336.5 5.0 collective-permute-done.47
  344.2 4.5 fusion.80
  348.7 7.0 %collective-permute-done.49 = bf16[128,2048]{1,0:T(8,128)(2,1)S(1)} collective-permute-done((bf16[128,2048]{1,0:T(8,128)(2,1)S(1)}, bf16[128,2048]{1,0:T(8,128)(2,1)S(1)}, u32[]{:S(2)}, u32[]{:S(2)}) %collective-permute-start.49) | collective-permute-done | bytes 524320 | tf_op jit(solution)/shard_map/ppermute | solution.py:106
  358.1 6.4 fusion.81
  373.0 5.5 collective-permute-done.54
  381.1 7.8 %convolution_convert_fusion = bf16[1024,2048]{1,0:T(8,128)(2,1)} fusion(bf16[1024,1024]{1,0:T(8,128)(2,1)S(1)} %copy-done.67, bf16[1024,1024]{1,0:T(8,128)(2,1)} %get-tuple-element.185, bf16[1024,1024]{1,0:T(8,128)(2,1)S(1)} %copy-done.83), kind=kOutput, calls=%fused_computation.12 | convolution fusion | flops 4305453056 | bytes 10485760 | tf_op jit(solution)/shard_map/dot_general | solution.py:25
  398.5 7.6 %collective-permute-done.57 = bf16[128,2048]{1,0:T(8,128)(2,1)S(1)} collective-permute-done((bf16[128,2048]{1,0:T(8,128)(2,1)S(1)}, bf16[128,2048]{1,0:T(8,128)(2,1)S(1)}, u32[]{:S(2)}, u32[]{:S(2)}) %collective-permute-start.57) | collective-permute-done | bytes 524320 | tf_op jit(solution)/shard_map/ppermute | solution.py:106
  410.9 7.8 %collective-permute-done.61 = bf16[128,2048]{1,0:T(8,128)(2,1)S(1)} collective-permute-done((bf16[128,2048]{1,0:T(8,128)(2,1)S(1)}, bf16[128,2048]{1,0:T(8,128)(2,1)S(1)}, u32[]{:S(2)}, u32[]{:S(2)}) %collective-permute-start.61) | collective-permute-done | bytes 524320 | tf_op jit(solution)/shard_map/ppermute | solution.py:106
  422.0 6.8 %convert_add_fusion = f32[1024,2048]{1,0:T(8,128)S(1)} fusion(bf16[1024,2048]{1,0:T(8,128)(2,1)} %collective-permute-done.62, bf16[1024,1024]{1,0:T(8,128)(2,1)S(1)} %copy-done.69, bf16[1024,1024]{1,0:T(8,128)(2,1)S(1)} %copy-done.87, bf16[1024,1024]{1,0:T(8,128)(2,1)S(1)} %copy-done.84), kind=kOutput, calls=%fused_computation | convolution fusion | flops 4307550208 | bytes 18874368 | tf_op jit(solution)/shard_map/dot_general | solution.py:25
  430.9 10.0 %collective-permute-done.63 = bf16[128,2048]{1,0:T(8,128)(2,1)S(1)} collective-permute-done((bf16[128,2048]{1,0:T(8,128)(2,1)S(1)}, bf16[128,2048]{1,0:T(8,128)(2,1)S(1)}, u32[]{:S(2)}, u32[]{:S(2)}) %collective-permute-start.63) | collective-permute-done | bytes 524320 | tf_op jit(solution)/shard_map/ppermute | solution.py:106
  444.3 8.4 %collective-permute-done.65 = bf16[128,2048]{1,0:T(8,128)(2,1)S(1)} collective-permute-done((bf16[128,2048]{1,0:T(8,128)(2,1)S(1)}, bf16[128,2048]{1,0:T(8,128)(2,1)S(1)}, u32[]{:S(2)}, u32[]{:S(2)}) %collective-permute-start.65) | collective-permute-done | bytes 524320 | tf_op jit(solution)/shard_map/ppermute | solution.py:106
  459.3 8.1 %collective-permute-done.68 = bf16[128,2048]{1,0:T(8,128)(2,1)S(1)} collective-permute-done((bf16[128,2048]{1,0:T(8,128)(2,1)S(1)}, bf16[128,2048]{1,0:T(8,128)(2,1)S(1)}, u32[]{:S(2)}, u32[]{:S(2)}) %collective-permute-start.68) | collective-permute-done | bytes 524320 | tf_op jit(solution)/shard_map/ppermute | solution.py:106
  470.7 5.2 all-to-all-start.2
  487.7 9.1 %collective-permute-done.72 = bf16[512,2048]{1,0:T(8,128)(2,1)} collective-permute-done((bf16[512,2048]{1,0:T(8,128)(2,1)}, bf16[512,2048]{1,0:T(8,128)(2,1)}, u32[]{:S(2)}, u32[]{:S(2)}) %collective-permute-start.72) | collective-permute-done | bytes 2097184 | tf_op jit(solution)/shard_map/ppermute | solution.py:48
  500.5 5.2 all-to-all-start.3
  523.2 13.0 %attention_backward.1 = (bf16[8,2,64,256]{3,2,1,0:T(8,128)(2,1)}, bf16[8,2,64,256]{3,2,1,0:T(8,128)(2,1)}, bf16[8,2,64,256]{3,2,1,0:T(8,128)(2,1)}) custom-call(s32[2]{0:T(128)} %lengths_ref.3, bf16[8,2,64,256]{3,2,1,0:T(8,128)(2,1)} %get-tuple-element.150.q_ref, bf16[8,2,64,256]{3,2,1,0:T(8,128)(2,1)} %get-tuple-element.151.k_ref, ...), custom_call_target="tpu_custom_call" | custom-call | flops 1342177280 | bytes 4194304 | tf_op jit(solution)/shard_map/attention_backward/pallas_call | solution.py:351
  537.7 12.9 %all-to-all-done.3 = bf16[8,64,2048]{2,1,0:T(8,128)(2,1)} async-done(((bf16[8,64,2048]{2,1,0:T(8,128)(2,1)}), bf16[8,64,2048]{2,1,0:T(8,128)(2,1)}, u32[]{:S(2)}, u32[]{:S(2)}) %all-to-all-start.3) | async-done | bytes 2097184 | tf_op jit(solution)/shard_map/all_to_all | solution.py:393
  564.6 4.7 collective-permute-done.73
  579.5 7.6 %collective-permute-done.76 = bf16[128,2048]{1,0:T(8,128)(2,1)S(1)} collective-permute-done((bf16[128,2048]{1,0:T(8,128)(2,1)S(1)}, bf16[128,2048]{1,0:T(8,128)(2,1)S(1)}, u32[]{:S(2)}, u32[]{:S(2)}) %collective-permute-start.76) | collective-permute-done | bytes 524320 | tf_op jit(solution)/shard_map/ppermute | solution.py:106
  592.8 4.5 collective-permute-done.80
  617.6 15.8 %collective-permute-done.82 = bf16[128,2048]{1,0:T(8,128)(2,1)S(1)} collective-permute-done((bf16[128,2048]{1,0:T(8,128)(2,1)}, bf16[128,2048]{1,0:T(8,128)(2,1)S(1)}, u32[]{:S(2)}, u32[]{:S(2)}) %collective-permute-start.82) | collective-permute-done | bytes 524320 | tf_op jit(solution)/shard_map/ppermute | solution.py:106
  637.3 8.0 %all-to-all-done.4 = bf16[8,64,768]{2,1,0:T(8,128)(2,1)} async-done(((bf16[8,64,768]{2,1,0:T(8,128)(2,1)}), bf16[8,64,768]{2,1,0:T(8,128)(2,1)}, u32[]{:S(2)}, u32[]{:S(2)}) %all-to-all-start.4) | async-done | bytes 786464 | tf_op jit(solution)/shard_map/all_to_all | solution.py:393
  (573 shorter events, 272.9 us)
Async XLA Ops:
  3.1 18.4 %collective-permute-start = (bf16[128,2048]{1,0:T(8,128)(2,1)}, bf16[128,2048]{1,0:T(8,128)(2,1)}, u32[]{:S(2)}, u32[]{:S(2)}) collective-permute-start(bf16[128,2048]{1,0:T(8,128)(2,1)} %fusion.9), channel_id=1, source_target_pairs={{0,1},{2,0},{4,2},{6,4},{7,6},{5,7},{3,5},{1,3},{8,9},{10,8},{12,1... | collective-permute-start | bytes 1572872 | tf_op jit(solution)/shard_map/ppermute | solution.py:106
  6.1 15.4 %collective-permute-start.1 = (bf16[128,2048]{1,0:T(8,128)(2,1)}, bf16[128,2048]{1,0:T(8,128)(2,1)}, u32[]{:S(2)}, u32[]{:S(2)}) collective-permute-start(bf16[128,2048]{1,0:T(8,128)(2,1)} %fusion.9), channel_id=1, source_target_pairs={{0,2},{2,4},{4,6},{6,7},{7,5},{5,3},{3,1},{1,0},{8,10},{10,12},{12... | collective-permute-start | bytes 1572872 | tf_op jit(solution)/shard_map/ppermute | solution.py:106
  7.8 40.8 %all-to-all-start = ((bf16[8,64,768]{2,1,0:T(8,128)(2,1)}), bf16[8,64,768]{2,1,0:T(8,128)(2,1)}, u32[]{:S(2)}, u32[]{:S(2)}) async-start(bf16[8,64,768]{2,1,0:T(8,128)(2,1)} %pad_maximum_fusion.10), calls=%async_computation | async-start | bytes 1572864 | tf_op jit(solution)/shard_map/all_to_all | solution.py:393
  21.5 20.7 %collective-permute-start.2 = (bf16[128,2048]{1,0:T(8,128)(2,1)}, bf16[128,2048]{1,0:T(8,128)(2,1)S(1)}, u32[]{:S(2)}, u32[]{:S(2)}) collective-permute-start(bf16[128,2048]{1,0:T(8,128)(2,1)} %collective-permute-done), channel_id=1, source_target_pairs={{0,1},{2,0},{4,2},{6,4},{7,6},{5,7},{3,5},{1,3},{8,9},{10,8},{12,1... | collective-permute-start | bytes 1572872 | tf_op jit(solution)/shard_map/ppermute | solution.py:106
  23.7 18.4 %collective-permute-start.3 = (bf16[128,2048]{1,0:T(8,128)(2,1)}, bf16[128,2048]{1,0:T(8,128)(2,1)S(1)}, u32[]{:S(2)}, u32[]{:S(2)}) collective-permute-start(bf16[128,2048]{1,0:T(8,128)(2,1)} %collective-permute-done.1), channel_id=1, source_target_pairs={{0,2},{2,4},{4,6},{6,7},{7,5},{5,3},{3,1},{1,0},{8,10},{10,12},{12... | collective-permute-start | bytes 1572872 | tf_op jit(solution)/shard_map/ppermute | solution.py:106
  42.2 19.3 %collective-permute-start.4 = (bf16[128,2048]{1,0:T(8,128)(2,1)S(1)}, bf16[128,2048]{1,0:T(8,128)(2,1)S(1)}, u32[]{:S(2)}, u32[]{:S(2)}) collective-permute-start(bf16[128,2048]{1,0:T(8,128)(2,1)S(1)} %collective-permute-done.2), channel_id=1, source_target_pairs={{0,1},{2,0},{4,2},{6,4},{7,6},{5,7},{3,5},{1,3},{8,9},{10,8},{12,1... | collective-permute-start | bytes 1572872 | tf_op jit(solution)/shard_map/ppermute | solution.py:106
  45.2 16.3 %collective-permute-start.5 = (bf16[128,2048]{1,0:T(8,128)(2,1)S(1)}, bf16[128,2048]{1,0:T(8,128)(2,1)S(1)}, u32[]{:S(2)}, u32[]{:S(2)}) collective-permute-start(bf16[128,2048]{1,0:T(8,128)(2,1)S(1)} %collective-permute-done.3), channel_id=1, source_target_pairs={{0,2},{2,4},{4,6},{6,7},{7,5},{5,3},{3,1},{1,0},{8,10},{10,12},{12... | collective-permute-start | bytes 1572872 | tf_op jit(solution)/shard_map/ppermute | solution.py:106
  48.5 30.6 %collective-permute-start.8 = (bf16[512,768]{1,0:T(8,128)(2,1)}, bf16[512,768]{1,0:T(8,128)(2,1)}, u32[]{:S(2)}, u32[]{:S(2)}) collective-permute-start(bf16[512,768]{1,0:T(8,128)(2,1)} %bitcast.25), channel_id=1, source_target_pairs={{0,16},{8,24},{16,0},{24,8},{1,17},{9,25},{17,1},{25,9},{2,18},{10... | collective-permute-start | bytes 2359304 | tf_op jit(solution)/shard_map/ppermute | solution.py:48
  64.7 43.0 %collective-permute-start.10 = (bf16[64,2048]{1,0:T(8,128)(2,1)}, bf16[64,2048]{1,0:T(8,128)(2,1)}, u32[]{:S(2)}, u32[]{:S(2)}) collective-permute-start(bf16[64,2048]{1,0:T(8,128)(2,1)} %param.18), channel_id=1, source_target_pairs={{0,0},{4,1},{8,2},{12,3},{16,4},{20,5},{24,6},{28,7},{1,8},{5,9},{... | collective-permute-start | bytes 786440 | tf_op jit(solution)/shard_map/ppermute | solution.py:422
  69.2 81.6 %all-to-all-start.1 = ((bf16[8,64,3072]{2,1,0:T(8,128)(2,1)}), bf16[8,64,3072]{2,1,0:T(8,128)(2,1)S(1)}, u32[]{:S(2)}, u32[]{:S(2)}) async-start(bf16[8,64,3072]{2,1,0:T(8,128)(2,1)} %pad_maximum_fusion.2), calls=%async_computation.1 | async-start | bytes 6291456 | tf_op jit(solution)/shard_map/all_to_all | solution.py:393
  107.7 19.1 %collective-permute-start.11 = (bf16[64,2048]{1,0:T(8,128)(2,1)}, bf16[64,2048]{1,0:T(8,128)(2,1)S(1)}, u32[]{:S(2)}, u32[]{:S(2)}) collective-permute-start(bf16[64,2048]{1,0:T(8,128)(2,1)} %collective-permute-done.10), channel_id=1, source_target_pairs={{0,16},{8,24},{16,0},{24,8},{1,17},{9,25},{17,1},{25,9},{2,18},{10... | collective-permute-start | bytes 786440 | tf_op jit(solution)/shard_map/ppermute | solution.py:48
  206.6 14.6 %collective-permute-start.25 = (bf16[128,2048]{1,0:T(8,128)(2,1)S(1)}, bf16[128,2048]{1,0:T(8,128)(2,1)S(1)}, u32[]{:S(2)}, u32[]{:S(2)}) collective-permute-start(bf16[128,2048]{1,0:T(8,128)(2,1)S(1)} %multiply_convert_fusion.3), channel_id=1, source_target_pairs={{0,1},{2,0},{4,2},{6,4},{7,6},{5,7},{3,5},{1,3},{8,9},{10,8},{12,1... | collective-permute-start | bytes 1572872 | tf_op jit(solution)/shard_map/ppermute | solution.py:106
  207.0 14.6 %collective-permute-start.26 = (bf16[128,2048]{1,0:T(8,128)(2,1)S(1)}, bf16[128,2048]{1,0:T(8,128)(2,1)S(1)}, u32[]{:S(2)}, u32[]{:S(2)}) collective-permute-start(bf16[128,2048]{1,0:T(8,128)(2,1)S(1)} %multiply_convert_fusion.3), channel_id=1, source_target_pairs={{0,2},{2,4},{4,6},{6,7},{7,5},{5,3},{3,1},{1,0},{8,10},{10,12},{12... | collective-permute-start | bytes 1572872 | tf_op jit(solution)/shard_map/ppermute | solution.py:106
  208.9 19.4 %collective-permute-start.29 = (bf16[512,512]{1,0:T(8,128)(2,1)S(1)}, bf16[512,512]{1,0:T(8,128)(2,1)S(1)}, u32[]{:S(2)}, u32[]{:S(2)}) collective-permute-start(bf16[512,512]{1,0:T(8,128)(2,1)S(1)} %copy-done.17), channel_id=1, source_target_pairs={{0,16},{8,24},{16,0},{24,8},{1,17},{9,25},{17,1},{25,9},{2,18},{10... | collective-permute-start | bytes 1572872 | tf_op jit(solution)/shard_map/ppermute | solution.py:48
  221.6 13.7 %collective-permute-start.27 = (bf16[128,2048]{1,0:T(8,128)(2,1)S(1)}, bf16[128,2048]{1,0:T(8,128)(2,1)S(1)}, u32[]{:S(2)}, u32[]{:S(2)}) collective-permute-start(bf16[128,2048]{1,0:T(8,128)(2,1)S(1)} %collective-permute-done.25), channel_id=1, source_target_pairs={{0,1},{2,0},{4,2},{6,4},{7,6},{5,7},{3,5},{1,3},{8,9},{10,8},{12,1... | collective-permute-start | bytes 1572872 | tf_op jit(solution)/shard_map/ppermute | solution.py:106
  221.7 13.7 %collective-permute-start.28 = (bf16[128,2048]{1,0:T(8,128)(2,1)S(1)}, bf16[128,2048]{1,0:T(8,128)(2,1)S(1)}, u32[]{:S(2)}, u32[]{:S(2)}) collective-permute-start(bf16[128,2048]{1,0:T(8,128)(2,1)S(1)} %collective-permute-done.26), channel_id=1, source_target_pairs={{0,2},{2,4},{4,6},{6,7},{7,5},{5,3},{3,1},{1,0},{8,10},{10,12},{12... | collective-permute-start | bytes 1572872 | tf_op jit(solution)/shard_map/ppermute | solution.py:106
  235.4 13.5 %collective-permute-start.30 = (bf16[128,2048]{1,0:T(8,128)(2,1)S(1)}, bf16[128,2048]{1,0:T(8,128)(2,1)S(1)}, u32[]{:S(2)}, u32[]{:S(2)}) collective-permute-start(bf16[128,2048]{1,0:T(8,128)(2,1)S(1)} %collective-permute-done.27), channel_id=1, source_target_pairs={{0,1},{2,0},{4,2},{6,4},{7,6},{5,7},{3,5},{1,3},{8,9},{10,8},{12,1... | collective-permute-start | bytes 1572872 | tf_op jit(solution)/shard_map/ppermute | solution.py:106
  237.4 44.5 %collective-permute-start.35 = (bf16[1024,2048]{1,0:T(8,128)(2,1)S(1)}, bf16[1024,2048]{1,0:T(8,128)(2,1)S(1)}, u32[]{:S(2)}, u32[]{:S(2)}) collective-permute-start(bf16[1024,2048]{1,0:T(8,128)(2,1)S(1)} %pad_maximum_fusion), channel_id=1, source_target_pairs={{0,8},{8,0},{16,24},{24,16},{1,9},{9,1},{17,25},{25,17},{2,10},{10... | collective-permute-start | bytes 12582920 | tf_op jit(solution)/shard_map/ppermute | solution.py:48
  258.5 14.2 %collective-permute-start.38 = (bf16[128,2048]{1,0:T(8,128)(2,1)S(1)}, bf16[128,2048]{1,0:T(8,128)(2,1)S(1)}, u32[]{:S(2)}, u32[]{:S(2)}) collective-permute-start(bf16[128,2048]{1,0:T(8,128)(2,1)S(1)} %fusion.39), channel_id=1, source_target_pairs={{0,1},{2,0},{4,2},{6,4},{7,6},{5,7},{3,5},{1,3},{8,9},{10,8},{12,1... | collective-permute-start | bytes 1572872 | tf_op jit(solution)/shard_map/ppermute | solution.py:106
  259.9 12.8 %collective-permute-start.37 = (bf16[128,2048]{1,0:T(8,128)(2,1)S(1)}, bf16[128,2048]{1,0:T(8,128)(2,1)S(1)}, u32[]{:S(2)}, u32[]{:S(2)}) collective-permute-start(bf16[128,2048]{1,0:T(8,128)(2,1)S(1)} %fusion.39), channel_id=1, source_target_pairs={{0,2},{2,4},{4,6},{6,7},{7,5},{5,3},{3,1},{1,0},{8,10},{10,12},{12... | collective-permute-start | bytes 1572872 | tf_op jit(solution)/shard_map/ppermute | solution.py:106
  274.7 23.5 %collective-permute-start.36 = (bf16[1024,1024]{1,0:T(8,128)(2,1)S(1)}, bf16[1024,1024]{1,0:T(8,128)(2,1)}, u32[]{:S(2)}, u32[]{:S(2)}) collective-permute-start(bf16[1024,1024]{1,0:T(8,128)(2,1)S(1)} %pad_maximum_fusion.3), channel_id=1, source_target_pairs={{0,8},{8,0},{16,24},{24,16},{1,9},{9,1},{17,25},{25,17},{2,10},{10... | collective-permute-start | bytes 6291464 | tf_op jit(solution)/shard_map/ppermute | solution.py:48
  274.8 17.3 %collective-permute-start.39 = (bf16[128,2048]{1,0:T(8,128)(2,1)S(1)}, bf16[128,2048]{1,0:T(8,128)(2,1)S(1)}, u32[]{:S(2)}, u32[]{:S(2)}) collective-permute-start(bf16[128,2048]{1,0:T(8,128)(2,1)S(1)} %collective-permute-done.37), channel_id=1, source_target_pairs={{0,2},{2,4},{4,6},{6,7},{7,5},{5,3},{3,1},{1,0},{8,10},{10,12},{12... | collective-permute-start | bytes 1572872 | tf_op jit(solution)/shard_map/ppermute | solution.py:106
  292.1 13.8 %collective-permute-start.42 = (bf16[128,2048]{1,0:T(8,128)(2,1)S(1)}, bf16[128,2048]{1,0:T(8,128)(2,1)S(1)}, u32[]{:S(2)}, u32[]{:S(2)}) collective-permute-start(bf16[128,2048]{1,0:T(8,128)(2,1)S(1)} %collective-permute-done.40), channel_id=1, source_target_pairs={{0,1},{2,0},{4,2},{6,4},{7,6},{5,7},{3,5},{1,3},{8,9},{10,8},{12,1... | collective-permute-start | bytes 1572872 | tf_op jit(solution)/shard_map/ppermute | solution.py:106
  293.8 12.2 %collective-permute-start.41 = (bf16[128,2048]{1,0:T(8,128)(2,1)S(1)}, bf16[128,2048]{1,0:T(8,128)(2,1)S(1)}, u32[]{:S(2)}, u32[]{:S(2)}) collective-permute-start(bf16[128,2048]{1,0:T(8,128)(2,1)S(1)} %collective-permute-done.39), channel_id=1, source_target_pairs={{0,2},{2,4},{4,6},{6,7},{7,5},{5,3},{3,1},{1,0},{8,10},{10,12},{12... | collective-permute-start | bytes 1572872 | tf_op jit(solution)/shard_map/ppermute | solution.py:106
  326.8 14.7 %collective-permute-start.47 = (bf16[128,2048]{1,0:T(8,128)(2,1)S(1)}, bf16[128,2048]{1,0:T(8,128)(2,1)S(1)}, u32[]{:S(2)}, u32[]{:S(2)}) collective-permute-start(bf16[128,2048]{1,0:T(8,128)(2,1)S(1)} %pad_maximum_fusion.16), channel_id=1, source_target_pairs={{0,2},{2,4},{4,6},{6,7},{7,5},{5,3},{3,1},{1,0},{8,10},{10,12},{12... | collective-permute-start | bytes 1572872 | tf_op jit(solution)/shard_map/ppermute | solution.py:106
  327.1 14.5 %collective-permute-start.48 = (bf16[128,2048]{1,0:T(8,128)(2,1)S(1)}, bf16[128,2048]{1,0:T(8,128)(2,1)S(1)}, u32[]{:S(2)}, u32[]{:S(2)}) collective-permute-start(bf16[128,2048]{1,0:T(8,128)(2,1)S(1)} %pad_maximum_fusion.17), channel_id=1, source_target_pairs={{0,1},{2,0},{4,2},{6,4},{7,6},{5,7},{3,5},{1,3},{8,9},{10,8},{12,1... | collective-permute-start | bytes 1572872 | tf_op jit(solution)/shard_map/ppermute | solution.py:106
  341.7 14.0 %collective-permute-start.49 = (bf16[128,2048]{1,0:T(8,128)(2,1)S(1)}, bf16[128,2048]{1,0:T(8,128)(2,1)S(1)}, u32[]{:S(2)}, u32[]{:S(2)}) collective-permute-start(bf16[128,2048]{1,0:T(8,128)(2,1)S(1)} %fusion.26), channel_id=1, source_target_pairs={{0,2},{2,4},{4,6},{6,7},{7,5},{5,3},{3,1},{1,0},{8,10},{10,12},{12... | collective-permute-start | bytes 1572872 | tf_op jit(solution)/shard_map/ppermute | solution.py:106
  342.0 13.9 %collective-permute-start.50 = (bf16[128,2048]{1,0:T(8,128)(2,1)S(1)}, bf16[128,2048]{1,0:T(8,128)(2,1)S(1)}, u32[]{:S(2)}, u32[]{:S(2)}) collective-permute-start(bf16[128,2048]{1,0:T(8,128)(2,1)S(1)} %fusion.27), channel_id=1, source_target_pairs={{0,1},{2,0},{4,2},{6,4},{7,6},{5,7},{3,5},{1,3},{8,9},{10,8},{12,1... | collective-permute-start | bytes 1572872 | tf_op jit(solution)/shard_map/ppermute | solution.py:106
  369.7 26.3 %collective-permute-start.59 = (bf16[1024,1024]{1,0:T(8,128)(2,1)S(1)}, bf16[1024,1024]{1,0:T(8,128)(2,1)S(1)}, u32[]{:S(2)}, u32[]{:S(2)}) collective-permute-start(bf16[1024,1024]{1,0:T(8,128)(2,1)S(1)} %convolution_convert_fusion.1), channel_id=1, source_target_pairs={{0,8},{8,0},{16,24},{24,16},{1,9},{9,1},{17,25},{25,17},{2,10},{10... | collective-permute-start | bytes 6291464 | tf_op jit(solution)/shard_map/ppermute | solution.py:48
  379.0 13.5 %collective-permute-start.55 = (bf16[128,2048]{1,0:T(8,128)(2,1)S(1)}, bf16[128,2048]{1,0:T(8,128)(2,1)S(1)}, u32[]{:S(2)}, u32[]{:S(2)}) collective-permute-start(bf16[128,2048]{1,0:T(8,128)(2,1)S(1)} %pad_maximum_fusion.19), channel_id=1, source_target_pairs={{0,2},{2,4},{4,6},{6,7},{7,5},{5,3},{3,1},{1,0},{8,10},{10,12},{12... | collective-permute-start | bytes 1572872 | tf_op jit(solution)/shard_map/ppermute | solution.py:106
  380.5 13.1 %collective-permute-start.56 = (bf16[128,2048]{1,0:T(8,128)(2,1)S(1)}, bf16[128,2048]{1,0:T(8,128)(2,1)S(1)}, u32[]{:S(2)}, u32[]{:S(2)}) collective-permute-start(bf16[128,2048]{1,0:T(8,128)(2,1)S(1)} %pad_maximum_fusion.20), channel_id=1, source_target_pairs={{0,1},{2,0},{4,2},{6,4},{7,6},{5,7},{3,5},{1,3},{8,9},{10,8},{12,1... | collective-permute-start | bytes 1572872 | tf_op jit(solution)/shard_map/ppermute | solution.py:106
  388.8 31.2 %collective-permute-start.62 = (bf16[1024,2048]{1,0:T(8,128)(2,1)}, bf16[1024,2048]{1,0:T(8,128)(2,1)}, u32[]{:S(2)}, u32[]{:S(2)}) collective-permute-start(bf16[1024,2048]{1,0:T(8,128)(2,1)} %convolution_convert_fusion), channel_id=1, source_target_pairs={{0,8},{8,0},{16,24},{24,16},{1,9},{9,1},{17,25},{25,17},{2,10},{10... | collective-permute-start | bytes 12582920 | tf_op jit(solution)/shard_map/ppermute | solution.py:48
  393.7 12.3 %collective-permute-start.57 = (bf16[128,2048]{1,0:T(8,128)(2,1)S(1)}, bf16[128,2048]{1,0:T(8,128)(2,1)S(1)}, u32[]{:S(2)}, u32[]{:S(2)}) collective-permute-start(bf16[128,2048]{1,0:T(8,128)(2,1)S(1)} %fusion.31), channel_id=1, source_target_pairs={{0,2},{2,4},{4,6},{6,7},{7,5},{5,3},{3,1},{1,0},{8,10},{10,12},{12... | collective-permute-start | bytes 1572872 | tf_op jit(solution)/shard_map/ppermute | solution.py:106
  395.2 12.2 %collective-permute-start.58 = (bf16[128,2048]{1,0:T(8,128)(2,1)S(1)}, bf16[128,2048]{1,0:T(8,128)(2,1)S(1)}, u32[]{:S(2)}, u32[]{:S(2)}) collective-permute-start(bf16[128,2048]{1,0:T(8,128)(2,1)S(1)} %fusion.32), channel_id=1, source_target_pairs={{0,1},{2,0},{4,2},{6,4},{7,6},{5,7},{3,5},{1,3},{8,9},{10,8},{12,1... | collective-permute-start | bytes 1572872 | tf_op jit(solution)/shard_map/ppermute | solution.py:106
  409.7 33.2 %collective-permute-start.71 = (bf16[512,1024]{1,0:T(8,128)(2,1)S(1)}, bf16[512,1024]{1,0:T(8,128)(2,1)S(1)}, u32[]{:S(2)}, u32[]{:S(2)}) collective-permute-start(bf16[512,1024]{1,0:T(8,128)(2,1)S(1)} %slice.1536), channel_id=1, source_target_pairs={{0,16},{8,24},{16,0},{24,8},{1,17},{9,25},{17,1},{25,9},{2,18},{10... | collective-permute-start | bytes 3145736 | tf_op jit(solution)/shard_map/ppermute | solution.py:48
  453.8 14.3 %collective-permute-start.67 = (bf16[128,2048]{1,0:T(8,128)(2,1)S(1)}, bf16[128,2048]{1,0:T(8,128)(2,1)S(1)}, u32[]{:S(2)}, u32[]{:S(2)}) collective-permute-start(bf16[128,2048]{1,0:T(8,128)(2,1)S(1)} %collective-permute-done.65), channel_id=1, source_target_pairs={{0,1},{2,0},{4,2},{6,4},{7,6},{5,7},{3,5},{1,3},{8,9},{10,8},{12,1... | collective-permute-start | bytes 1572872 | tf_op jit(solution)/shard_map/ppermute | solution.py:106
  454.9 12.5 %collective-permute-start.68 = (bf16[128,2048]{1,0:T(8,128)(2,1)S(1)}, bf16[128,2048]{1,0:T(8,128)(2,1)S(1)}, u32[]{:S(2)}, u32[]{:S(2)}) collective-permute-start(bf16[128,2048]{1,0:T(8,128)(2,1)S(1)} %collective-permute-done.66), channel_id=1, source_target_pairs={{0,2},{2,4},{4,6},{6,7},{7,5},{5,3},{3,1},{1,0},{8,10},{10,12},{12... | collective-permute-start | bytes 1572872 | tf_op jit(solution)/shard_map/ppermute | solution.py:106
  458.4 38.4 %collective-permute-start.72 = (bf16[512,2048]{1,0:T(8,128)(2,1)}, bf16[512,2048]{1,0:T(8,128)(2,1)}, u32[]{:S(2)}, u32[]{:S(2)}) collective-permute-start(bf16[512,2048]{1,0:T(8,128)(2,1)} %slice.1535), channel_id=1, source_target_pairs={{0,16},{8,24},{16,0},{24,8},{1,17},{9,25},{17,1},{25,9},{2,18},{10... | collective-permute-start | bytes 6291464 | tf_op jit(solution)/shard_map/ppermute | solution.py:48
  470.7 29.8 %all-to-all-start.2 = ((bf16[8,64,1024]{2,1,0:T(8,128)(2,1)}), bf16[8,64,1024]{2,1,0:T(8,128)(2,1)}, u32[]{:S(2)}, u32[]{:S(2)}) async-start(bf16[8,64,1024]{2,1,0:T(8,128)(2,1)} %bitcast.57), calls=%async_computation.2 | async-start | bytes 2097152 | tf_op jit(solution)/shard_map/all_to_all | solution.py:393
  487.7 18.2 %collective-permute-start.83 = (bf16[128,2048]{1,0:T(8,128)(2,1)}, bf16[128,2048]{1,0:T(8,128)(2,1)}, u32[]{:S(2)}, u32[]{:S(2)}) collective-permute-start(bf16[128,2048]{1,0:T(8,128)(2,1)} %pad_maximum_fusion.24), channel_id=1, source_target_pairs={{0,8},{8,0},{16,24},{24,16},{1,9},{9,1},{17,25},{25,17},{2,10},{10... | collective-permute-start | bytes 1572872 | tf_op jit(solution)/shard_map/ppermute | solution.py:48
  500.5 50.1 %all-to-all-start.3 = ((bf16[8,64,2048]{2,1,0:T(8,128)(2,1)}), bf16[8,64,2048]{2,1,0:T(8,128)(2,1)}, u32[]{:S(2)}, u32[]{:S(2)}) async-start(bf16[8,64,2048]{2,1,0:T(8,128)(2,1)} %bitcast.421), calls=%async_computation.3 | async-start | bytes 4194304 | tf_op jit(solution)/shard_map/all_to_all | solution.py:393
  554.1 16.1 %collective-permute-start.75 = (bf16[1024,768]{1,0:T(8,128)(2,1)S(1)}, bf16[1024,768]{1,0:T(8,128)(2,1)S(1)}, u32[]{:S(2)}, u32[]{:S(2)}) collective-permute-start(bf16[1024,768]{1,0:T(8,128)(2,1)S(1)} %convolution_convert_fusion.2), channel_id=1, source_target_pairs={{0,8},{8,0},{16,24},{24,16},{1,9},{9,1},{17,25},{25,17},{2,10},{10... | collective-permute-start | bytes 4718600 | tf_op jit(solution)/shard_map/ppermute | solution.py:48
  573.9 13.2 %collective-permute-start.76 = (bf16[128,2048]{1,0:T(8,128)(2,1)S(1)}, bf16[128,2048]{1,0:T(8,128)(2,1)S(1)}, u32[]{:S(2)}, u32[]{:S(2)}) collective-permute-start(bf16[128,2048]{1,0:T(8,128)(2,1)S(1)} %pad_maximum_fusion.21), channel_id=1, source_target_pairs={{0,2},{2,4},{4,6},{6,7},{7,5},{5,3},{3,1},{1,0},{8,10},{10,12},{12... | collective-permute-start | bytes 1572872 | tf_op jit(solution)/shard_map/ppermute | solution.py:106
  576.6 13.0 %collective-permute-start.77 = (bf16[128,2048]{1,0:T(8,128)(2,1)S(1)}, bf16[128,2048]{1,0:T(8,128)(2,1)S(1)}, u32[]{:S(2)}, u32[]{:S(2)}) collective-permute-start(bf16[128,2048]{1,0:T(8,128)(2,1)S(1)} %pad_maximum_fusion.22), channel_id=1, source_target_pairs={{0,1},{2,0},{4,2},{6,4},{7,6},{5,7},{3,5},{1,3},{8,9},{10,8},{12,1... | collective-permute-start | bytes 1572872 | tf_op jit(solution)/shard_map/ppermute | solution.py:106
  579.0 18.3 %collective-permute-start.80 = (bf16[512,768]{1,0:T(8,128)(2,1)S(1)}, bf16[512,768]{1,0:T(8,128)(2,1)S(1)}, u32[]{:S(2)}, u32[]{:S(2)}) collective-permute-start(bf16[512,768]{1,0:T(8,128)(2,1)S(1)} %slice.1537), channel_id=1, source_target_pairs={{0,16},{8,24},{16,0},{24,8},{1,17},{9,25},{17,1},{25,9},{2,18},{10... | collective-permute-start | bytes 2359304 | tf_op jit(solution)/shard_map/ppermute | solution.py:48
  604.3 29.1 %collective-permute-start.82 = (bf16[128,2048]{1,0:T(8,128)(2,1)}, bf16[128,2048]{1,0:T(8,128)(2,1)S(1)}, u32[]{:S(2)}, u32[]{:S(2)}) collective-permute-start(bf16[128,2048]{1,0:T(8,128)(2,1)} %fusion.38), channel_id=1, source_target_pairs={{0,1},{2,0},{4,2},{6,4},{7,6},{5,7},{3,5},{1,3},{8,9},{10,8},{12,1... | collective-permute-start | bytes 1572872 | tf_op jit(solution)/shard_map/ppermute | solution.py:106
  605.5 28.0 %collective-permute-start.81 = (bf16[128,2048]{1,0:T(8,128)(2,1)}, bf16[128,2048]{1,0:T(8,128)(2,1)}, u32[]{:S(2)}, u32[]{:S(2)}) collective-permute-start(bf16[128,2048]{1,0:T(8,128)(2,1)} %fusion.35), channel_id=1, source_target_pairs={{0,2},{2,4},{4,6},{6,7},{7,5},{5,3},{3,1},{1,0},{8,10},{10,12},{12... | collective-permute-start | bytes 1572872 | tf_op jit(solution)/shard_map/ppermute | solution.py:106
  612.4 33.0 %all-to-all-start.4 = ((bf16[8,64,768]{2,1,0:T(8,128)(2,1)}), bf16[8,64,768]{2,1,0:T(8,128)(2,1)}, u32[]{:S(2)}, u32[]{:S(2)}) async-start(bf16[8,64,768]{2,1,0:T(8,128)(2,1)} %bitcast.64), calls=%async_computation.4 | async-start | bytes 1572864 | tf_op jit(solution)/shard_map/all_to_all | solution.py:393
  (133 other events, 1636.8 us)

commit v6 on v5

--- a/solution.py
+++ b/solution.py
@@ -442,12 +442,12 @@
     )
     attn_out = contract(mixed, mix_rows, 1, 0)
     residual = block_in + ring.scatter_sum(
-        attn_out[:, : width // 2], attn_out[:, width // 2 :], ((ffn_columns,), ffn_parts[:1], ffn_parts[1:2], ffn_parts[2:3])
+        attn_out[:, : width // 2], attn_out[:, width // 2 :], ((), (ffn_columns,), ffn_parts[:1], ffn_parts[1:2])
     )
 
     ffn_weights = (ffn_half, shares.swap(ffn_half, 1))
     normed_two, factor_two = normalize(residual)
-    two_all = halves(ring.gather(normed_two.astype(BF16), (ffn_parts[3:4], (), ffn_parts[4:5], ffn_parts[5:])))
+    two_all = halves(ring.gather(normed_two.astype(BF16), [(part,) for part in ffn_parts[2:]]))
     down_weights = (down_half, shares.swap(down_half, 1))
     low_part = contract(two_all[0], ffn_weights[0], 1, 0)
     gate_up = low_part + contract(two_all[1], ffn_weights[1], 1, 0)

time: 661 us -> 656 us (level)
  local copies, waits for them, and re-layouts: 61.1 us -> 82.3 us
  waiting for transfers between devices: 281 us -> 265 us
  starting transfers between devices: 130 us -> 121 us
    ppermute x64, waiting for transfers between devices: 213 us -> 186 us  [shift(): return lax.ppermute(value, 'ctx', pairs)]
    unnamed x279 -> x289, local copies, waits for them, and re-layouts: 45.8 us -> 62.3 us
    ppermute x20, waiting for transfers between devices: 34 us -> 41 us  [swap(): return lax.ppermute(value, 'dp', [(i, i ^ bit) for i in range(self.count)])]
  transfers between devices with their start and end apart: 91 -> 91, of which waited for: 53 -> 55; matrix products, arithmetic and copies ran while one was open for 29% -> 31% of each run, Pallas kernels for 4% -> 4%
where the time goes in v6:
time: 656 us; the launch traced here: 650 us
  waiting for transfers between devices  265 us (40%)
  starting transfers between devices  121 us (18%)
  matrix products  94.7 us (14%)
  local copies, waits for them, and re-layouts  82.3 us (13%)
  other arithmetic  60.1 us (9%)
  Pallas kernels  23.4 us (4%)
    ppermute x64, waiting for transfers between devices, shift(): return lax.ppermute(value, 'ctx', pairs)  186 us
    dot_general x21, matrix products, contract(): lax.dot_general(left, right, (((left_dim,), (right_dim,)), ((), ())), pre...  94.7 us
    ppermute x64, starting transfers between devices, shift(): return lax.ppermute(value, 'ctx', pairs)  71.9 us
    unnamed x289, local copies, waits for them, and re-layouts  62.3 us
    ppermute x20, waiting for transfers between devices, swap(): return lax.ppermute(value, 'dp', [(i, i ^ bit) for i in range(self.count)])  41 us
    all_to_all x5, waiting for transfers between devices, exchange(): return lax.all_to_all(tie([blocks], done)[0], 'ctx', 0, 0, tiled=True)  38.4 us
    all_to_all x5, starting transfers between devices, exchange(): return lax.all_to_all(tie([blocks], done)[0], 'ctx', 0, 0, tiled=True)  29.4 us
    ppermute x20, starting transfers between devices, swap(): return lax.ppermute(value, 'dp', [(i, i ^ bit) for i in range(self.count)])  14.6 us
  transfers between devices with their start and end apart: 91, of which 55 were waited for; matrix products, arithmetic and copies ran while one was open for 31% of the time, Pallas kernels for 4%

profile of v6, /device:TPU:0, one launch (start us, length us, event | category | flops | bytes accessed | tf_op | source)
XLA Modules:
  0.0 649.8 jit_solution(13610054145964657119)
XLA Ops:
  7.8 6.4 all-to-all-start
  39.4 8.3 %collective-permute-done.2 = bf16[128,2048]{1,0:T(8,128)(2,1)} collective-permute-done((bf16[128,2048]{1,0:T(8,128)(2,1)}, bf16[128,2048]{1,0:T(8,128)(2,1)}, u32[]{:S(2)}, u32[]{:S(2)}) %collective-permute-start.2) | collective-permute-done | bytes 524320 | tf_op jit(solution)/shard_map/ppermute | solution.py:106
  55.5 6.0 collective-permute-done.5
  71.7 8.7 %all-to-all-start.1 = ((bf16[8,64,3072]{2,1,0:T(8,128)(2,1)}), bf16[8,64,3072]{2,1,0:T(8,128)(2,1)S(1)}, u32[]{:S(2)}, u32[]{:S(2)}) async-start(bf16[8,64,3072]{2,1,0:T(8,128)(2,1)} %pad_maximum_fusion.2), calls=%async_computation.1 | async-start | bytes 6291456 | tf_op jit(solution)/shard_map/all_to_all | solution.py:393
  86.8 4.0 fusion.86
  90.8 4.6 convolution_add_fusion.2
  96.9 10.4 %attention_forward.1 = (bf16[8,2,64,256]{3,2,1,0:T(8,128)(2,1)}, bf16[8,2,64,256]{3,2,1,0:T(8,128)(2,1)}, bf16[8,2,64,256]{3,2,1,0:T(8,128)(2,1)}, bf16[8,2,64,256]{3,2,1,0:T(8,128)(2,1)}, f32[2,512,4]{2,1,0:T(8,128)}) custom-call(s32[2]{0:T(128)} %lengths_ref.3, f32[8,2,64,768]{3,2,1,0:T(8,128)} %bitcast.417, f32[8,2,64,768]{3,2,1,0:T(8,128)} %bitcast.418, ...), custom_call_target="tpu_custom_call" | custom-call | flops 536870912 | bytes 4194304 | tf_op jit(solution)/shard_map/attention_forward/pallas_call | solution.py:329
  110.4 4.6 collective-permute-done.11
  124.3 7.0 %collective-permute-done.14 = bf16[128,1024]{1,0:T(8,128)(2,1)S(1)} collective-permute-done((bf16[128,1024]{1,0:T(8,128)(2,1)S(1)}, bf16[128,1024]{1,0:T(8,128)(2,1)S(1)}, u32[]{:S(2)}, u32[]{:S(2)}) %collective-permute-start.14) | collective-permute-done | bytes 262176 | tf_op jit(solution)/shard_map/ppermute | solution.py:106
  136.5 15.2 %all-to-all-done.1 = bf16[8,64,3072]{2,1,0:T(8,128)(2,1)S(1)} async-done(((bf16[8,64,3072]{2,1,0:T(8,128)(2,1)}), bf16[8,64,3072]{2,1,0:T(8,128)(2,1)S(1)}, u32[]{:S(2)}, u32[]{:S(2)}) %all-to-all-start.1) | async-done | bytes 3145760 | tf_op jit(solution)/shard_map/all_to_all | solution.py:393
  154.3 4.3 collective-permute-start.15
  163.1 5.8 collective-permute-done.16
  176.4 8.3 %collective-permute-done.19 = bf16[128,2048]{1,0:T(8,128)(2,1)S(1)} collective-permute-done((bf16[128,2048]{1,0:T(8,128)(2,1)S(1)}, bf16[128,2048]{1,0:T(8,128)(2,1)S(1)}, u32[]{:S(2)}, u32[]{:S(2)}) %collective-permute-start.19) | collective-permute-done | bytes 524320 | tf_op jit(solution)/shard_map/ppermute | solution.py:106
  192.9 7.8 %collective-permute-done.22 = bf16[128,2048]{1,0:T(8,128)(2,1)S(1)} collective-permute-done((bf16[128,2048]{1,0:T(8,128)(2,1)}, bf16[128,2048]{1,0:T(8,128)(2,1)S(1)}, u32[]{:S(2)}, u32[]{:S(2)}) %collective-permute-start.22) | collective-permute-done | bytes 524320 | tf_op jit(solution)/shard_map/ppermute | solution.py:106
  210.3 5.0 collective-permute-done.26
  220.9 8.2 %collective-permute-done.29 = bf16[512,512]{1,0:T(8,128)(2,1)S(1)} collective-permute-done((bf16[512,512]{1,0:T(8,128)(2,1)S(1)}, bf16[512,512]{1,0:T(8,128)(2,1)S(1)}, u32[]{:S(2)}, u32[]{:S(2)}) %collective-permute-start.29) | collective-permute-done | bytes 524320 | tf_op jit(solution)/shard_map/ppermute | solution.py:48
  233.8 4.6 pad_maximum_fusion
  243.2 5.6 collective-permute-done.33
  252.0 6.7 %fusion.87 = f32[1024,2048]{1,0:T(8,128)} fusion(bf16[1024,1024]{1,0:T(8,128)(2,1)S(1)} %get-tuple-element.341, bf16[1024,2048]{1,0:T(8,128)(2,1)S(1)} %pad_maximum_fusion), kind=kOutput, calls=%fused_computation.522 | convolution fusion | flops 4294967296 | bytes 14680064 | tf_op jit(solution)/shard_map/dot_general | solution.py:25
  265.0 8.5 %collective-permute-done.40 = bf16[128,2048]{1,0:T(8,128)(2,1)S(1)} collective-permute-done((bf16[128,2048]{1,0:T(8,128)(2,1)S(1)}, bf16[128,2048]{1,0:T(8,128)(2,1)S(1)}, u32[]{:S(2)}, u32[]{:S(2)}) %collective-permute-start.40) | collective-permute-done | bytes 524320 | tf_op jit(solution)/shard_map/ppermute | solution.py:106
  275.6 8.9 %convolution_add_fusion = f32[1024,2048]{1,0:T(8,128)S(1)} fusion(f32[1024,2048]{1,0:T(8,128)} %fusion.87, bf16[1024,1024]{1,0:T(8,128)(2,1)S(1)} %get-tuple-element.340, bf16[1024,2048]{1,0:T(8,128)(2,1)} %copy-done.86), kind=kOutput, calls=%fused_computation.11 | convolution fusion | flops 4297064448 | bytes 23068672 | tf_op jit(solution)/shard_map/dot_general | solution.py:25
  290.6 4.0 fusion.83
  300.8 6.1 collective-permute-done.43
  311.9 6.7 %fusion.88 = f32[1024,1024]{1,0:T(8,128)} fusion(bf16[1024,1024]{1,0:T(8,128)(2,1)S(1)} %get-tuple-element.317, bf16[1024,1024]{1,0:T(8,128)(2,1)} %collective-permute-done.36), kind=kOutput, calls=%fused_computation.523 | convolution fusion | flops 2147483648 | bytes 8388608 | tf_op jit(solution)/shard_map/dot_general | solution.py:25
  322.8 7.5 %multiply_convert_fusion.1 = (bf16[1024,1024]{1,0:T(8,128)(2,1)S(1)}, bf16[1024,1024]{1,0:T(8,128)(2,1)}) fusion(f32[1024,2048]{1,0:T(8,128)S(1)} %convolution_add_fusion, f32[1024,1024]{1,0:T(8,128)} %fusion.88, bf16[1024,1024]{1,0:T(8,128)(2,1)} %get-tuple-element.316, bf16[1024,512]{1,0:T(8,128)(2,1)S(1)} %constant_dynamic-update-slice_fusion.74, ...), kind=kOutput, calls=%fused_computation.7 | convolution fusion | flops 2166358016 | bytes 20971520 | tf_op jit(solution)/shard_map/dot_general | solution.py:25
  330.3 5.0 collective-permute-done.47
  338.8 4.5 fusion.80
  343.3 7.2 %collective-permute-done.49 = bf16[128,2048]{1,0:T(8,128)(2,1)S(1)} collective-permute-done((bf16[128,2048]{1,0:T(8,128)(2,1)S(1)}, bf16[128,2048]{1,0:T(8,128)(2,1)S(1)}, u32[]{:S(2)}, u32[]{:S(2)}) %collective-permute-start.49) | collective-permute-done | bytes 524320 | tf_op jit(solution)/shard_map/ppermute | solution.py:106
  353.1 7.0 %fusion.81 = (bf16[1024,1024]{1,0:T(8,128)(2,1)S(1)}, f32[1024,1024]{1,0:T(8,128)S(1)}) fusion(bf16[1024,2048]{1,0:T(8,128)(2,1)} %copy-done.86, bf16[1024,1024]{1,0:T(8,128)(2,1)} %get-tuple-element.185, bf16[1024,1024]{1,0:T(8,128)(2,1)S(1)} %copy-done.90), kind=kOutput, calls=%fused_computation.516 | convolution fusion | flops 4304404480 | bytes 14680064 | tf_op jit(solution)/shard_map/dot_general | solution.py:25
  367.9 5.3 collective-permute-done.54
  375.7 7.7 %convolution_convert_fusion = bf16[1024,2048]{1,0:T(8,128)(2,1)} fusion(bf16[1024,1024]{1,0:T(8,128)(2,1)S(1)} %copy-done.70, bf16[1024,1024]{1,0:T(8,128)(2,1)} %get-tuple-element.185, bf16[1024,1024]{1,0:T(8,128)(2,1)S(1)} %copy-done.91), kind=kOutput, calls=%fused_computation.12 | convolution fusion | flops 4305453056 | bytes 10485760 | tf_op jit(solution)/shard_map/dot_general | solution.py:25
  392.1 7.8 %collective-permute-done.57 = bf16[128,2048]{1,0:T(8,128)(2,1)S(1)} collective-permute-done((bf16[128,2048]{1,0:T(8,128)(2,1)S(1)}, bf16[128,2048]{1,0:T(8,128)(2,1)S(1)}, u32[]{:S(2)}, u32[]{:S(2)}) %collective-permute-start.57) | collective-permute-done | bytes 524320 | tf_op jit(solution)/shard_map/ppermute | solution.py:106
  403.5 8.9 %collective-permute-done.61 = bf16[128,2048]{1,0:T(8,128)(2,1)S(1)} collective-permute-done((bf16[128,2048]{1,0:T(8,128)(2,1)S(1)}, bf16[128,2048]{1,0:T(8,128)(2,1)S(1)}, u32[]{:S(2)}, u32[]{:S(2)}) %collective-permute-start.61) | collective-permute-done | bytes 524320 | tf_op jit(solution)/shard_map/ppermute | solution.py:106
  415.8 7.3 %convert_add_fusion = f32[1024,2048]{1,0:T(8,128)S(1)} fusion(bf16[1024,2048]{1,0:T(8,128)(2,1)} %collective-permute-done.62, bf16[1024,1024]{1,0:T(8,128)(2,1)S(1)} %copy-done.72, bf16[1024,1024]{1,0:T(8,128)(2,1)} %get-tuple-element.185, bf16[1024,1024]{1,0:T(8,128)(2,1)S(1)} %copy-done.91), kind=kOutput, calls=%fused_computation | convolution fusion | flops 4307550208 | bytes 18874368 | tf_op jit(solution)/shard_map/dot_general | solution.py:25
  425.2 10.1 %collective-permute-done.63 = bf16[128,2048]{1,0:T(8,128)(2,1)S(1)} collective-permute-done((bf16[128,2048]{1,0:T(8,128)(2,1)S(1)}, bf16[128,2048]{1,0:T(8,128)(2,1)S(1)}, u32[]{:S(2)}, u32[]{:S(2)}) %collective-permute-start.63) | collective-permute-done | bytes 524320 | tf_op jit(solution)/shard_map/ppermute | solution.py:106
  438.9 8.2 %collective-permute-done.65 = bf16[128,2048]{1,0:T(8,128)(2,1)S(1)} collective-permute-done((bf16[128,2048]{1,0:T(8,128)(2,1)S(1)}, bf16[128,2048]{1,0:T(8,128)(2,1)S(1)}, u32[]{:S(2)}, u32[]{:S(2)}) %collective-permute-start.65) | collective-permute-done | bytes 524320 | tf_op jit(solution)/shard_map/ppermute | solution.py:106
  452.5 9.0 %collective-permute-done.68 = bf16[128,2048]{1,0:T(8,128)(2,1)S(1)} collective-permute-done((bf16[128,2048]{1,0:T(8,128)(2,1)S(1)}, bf16[128,2048]{1,0:T(8,128)(2,1)S(1)}, u32[]{:S(2)}, u32[]{:S(2)}) %collective-permute-start.68) | collective-permute-done | bytes 524320 | tf_op jit(solution)/shard_map/ppermute | solution.py:106
  464.7 5.6 all-to-all-start.2
  482.1 9.4 %collective-permute-done.72 = bf16[512,2048]{1,0:T(8,128)(2,1)} collective-permute-done((bf16[512,2048]{1,0:T(8,128)(2,1)}, bf16[512,2048]{1,0:T(8,128)(2,1)}, u32[]{:S(2)}, u32[]{:S(2)}) %collective-permute-start.72) | collective-permute-done | bytes 2097184 | tf_op jit(solution)/shard_map/ppermute | solution.py:48
  495.3 4.5 all-to-all-start.3
  517.4 13.0 %attention_backward.1 = (bf16[8,2,64,256]{3,2,1,0:T(8,128)(2,1)}, bf16[8,2,64,256]{3,2,1,0:T(8,128)(2,1)}, bf16[8,2,64,256]{3,2,1,0:T(8,128)(2,1)}) custom-call(s32[2]{0:T(128)} %lengths_ref.3, bf16[8,2,64,256]{3,2,1,0:T(8,128)(2,1)} %get-tuple-element.150.q_ref, bf16[8,2,64,256]{3,2,1,0:T(8,128)(2,1)} %get-tuple-element.151.k_ref, ...), custom_call_target="tpu_custom_call" | custom-call | flops 1342177280 | bytes 4194304 | tf_op jit(solution)/shard_map/attention_backward/pallas_call | solution.py:351
  531.8 12.9 %all-to-all-done.3 = bf16[8,64,2048]{2,1,0:T(8,128)(2,1)} async-done(((bf16[8,64,2048]{2,1,0:T(8,128)(2,1)}), bf16[8,64,2048]{2,1,0:T(8,128)(2,1)}, u32[]{:S(2)}, u32[]{:S(2)}) %all-to-all-start.3) | async-done | bytes 2097184 | tf_op jit(solution)/shard_map/all_to_all | solution.py:393
  559.9 4.7 collective-permute-done.73
  574.2 7.9 %collective-permute-done.76 = bf16[128,2048]{1,0:T(8,128)(2,1)S(1)} collective-permute-done((bf16[128,2048]{1,0:T(8,128)(2,1)S(1)}, bf16[128,2048]{1,0:T(8,128)(2,1)S(1)}, u32[]{:S(2)}, u32[]{:S(2)}) %collective-permute-start.76) | collective-permute-done | bytes 524320 | tf_op jit(solution)/shard_map/ppermute | solution.py:106
  587.9 4.5 collective-permute-done.80
  607.4 4.2 all-to-all-start.4
  612.4 15.7 %collective-permute-done.82 = bf16[128,2048]{1,0:T(8,128)(2,1)S(1)} collective-permute-done((bf16[128,2048]{1,0:T(8,128)(2,1)}, bf16[128,2048]{1,0:T(8,128)(2,1)S(1)}, u32[]{:S(2)}, u32[]{:S(2)}) %collective-permute-start.82) | collective-permute-done | bytes 524320 | tf_op jit(solution)/shard_map/ppermute | solution.py:106
  632.1 8.2 %all-to-all-done.4 = bf16[8,64,768]{2,1,0:T(8,128)(2,1)} async-done(((bf16[8,64,768]{2,1,0:T(8,128)(2,1)}), bf16[8,64,768]{2,1,0:T(8,128)(2,1)}, u32[]{:S(2)}, u32[]{:S(2)}) %all-to-all-start.4) | async-done | bytes 786464 | tf_op jit(solution)/shard_map/all_to_all | solution.py:393
  (583 shorter events, 295.2 us)
Async XLA Ops:
  3.1 28.3 %collective-permute-start = (bf16[128,2048]{1,0:T(8,128)(2,1)}, bf16[128,2048]{1,0:T(8,128)(2,1)}, u32[]{:S(2)}, u32[]{:S(2)}) collective-permute-start(bf16[128,2048]{1,0:T(8,128)(2,1)} %fusion.9), channel_id=1, source_target_pairs={{0,1},{2,0},{4,2},{6,4},{7,6},{5,7},{3,5},{1,3},{8,9},{10,8},{12,1... | collective-permute-start | bytes 1572872 | tf_op jit(solution)/shard_map/ppermute | solution.py:106
  6.1 25.3 %collective-permute-start.1 = (bf16[128,2048]{1,0:T(8,128)(2,1)}, bf16[128,2048]{1,0:T(8,128)(2,1)}, u32[]{:S(2)}, u32[]{:S(2)}) collective-permute-start(bf16[128,2048]{1,0:T(8,128)(2,1)} %fusion.9), channel_id=1, source_target_pairs={{0,2},{2,4},{4,6},{6,7},{7,5},{5,3},{3,1},{1,0},{8,10},{10,12},{12... | collective-permute-start | bytes 1572872 | tf_op jit(solution)/shard_map/ppermute | solution.py:106
  7.8 29.9 %all-to-all-start = ((bf16[8,64,768]{2,1,0:T(8,128)(2,1)}), bf16[8,64,768]{2,1,0:T(8,128)(2,1)}, u32[]{:S(2)}, u32[]{:S(2)}) async-start(bf16[8,64,768]{2,1,0:T(8,128)(2,1)} %pad_maximum_fusion.10), calls=%async_computation | async-start | bytes 1572864 | tf_op jit(solution)/shard_map/all_to_all | solution.py:393
  31.4 16.3 %collective-permute-start.2 = (bf16[128,2048]{1,0:T(8,128)(2,1)}, bf16[128,2048]{1,0:T(8,128)(2,1)}, u32[]{:S(2)}, u32[]{:S(2)}) collective-permute-start(bf16[128,2048]{1,0:T(8,128)(2,1)} %collective-permute-done), channel_id=1, source_target_pairs={{0,1},{2,0},{4,2},{6,4},{7,6},{5,7},{3,5},{1,3},{8,9},{10,8},{12,1... | collective-permute-start | bytes 1572872 | tf_op jit(solution)/shard_map/ppermute | solution.py:106
  33.5 14.2 %collective-permute-start.3 = (bf16[128,2048]{1,0:T(8,128)(2,1)}, bf16[128,2048]{1,0:T(8,128)(2,1)S(1)}, u32[]{:S(2)}, u32[]{:S(2)}) collective-permute-start(bf16[128,2048]{1,0:T(8,128)(2,1)} %collective-permute-done.1), channel_id=1, source_target_pairs={{0,2},{2,4},{4,6},{6,7},{7,5},{5,3},{3,1},{1,0},{8,10},{10,12},{12... | collective-permute-start | bytes 1572872 | tf_op jit(solution)/shard_map/ppermute | solution.py:106
  37.6 29.8 %collective-permute-start.8 = (bf16[512,768]{1,0:T(8,128)(2,1)}, bf16[512,768]{1,0:T(8,128)(2,1)S(1)}, u32[]{:S(2)}, u32[]{:S(2)}) collective-permute-start(bf16[512,768]{1,0:T(8,128)(2,1)} %bitcast.25), channel_id=1, source_target_pairs={{0,16},{8,24},{16,0},{24,8},{1,17},{9,25},{17,1},{25,9},{2,18},{10... | collective-permute-start | bytes 2359304 | tf_op jit(solution)/shard_map/ppermute | solution.py:48
  47.7 14.1 %collective-permute-start.4 = (bf16[128,2048]{1,0:T(8,128)(2,1)}, bf16[128,2048]{1,0:T(8,128)(2,1)S(1)}, u32[]{:S(2)}, u32[]{:S(2)}) collective-permute-start(bf16[128,2048]{1,0:T(8,128)(2,1)} %collective-permute-done.2), channel_id=1, source_target_pairs={{0,1},{2,0},{4,2},{6,4},{7,6},{5,7},{3,5},{1,3},{8,9},{10,8},{12,1... | collective-permute-start | bytes 1572872 | tf_op jit(solution)/shard_map/ppermute | solution.py:106
  49.2 12.3 %collective-permute-start.5 = (bf16[128,2048]{1,0:T(8,128)(2,1)S(1)}, bf16[128,2048]{1,0:T(8,128)(2,1)S(1)}, u32[]{:S(2)}, u32[]{:S(2)}) collective-permute-start(bf16[128,2048]{1,0:T(8,128)(2,1)S(1)} %collective-permute-done.3), channel_id=1, source_target_pairs={{0,2},{2,4},{4,6},{6,7},{7,5},{5,3},{3,1},{1,0},{8,10},{10,12},{12... | collective-permute-start | bytes 1572872 | tf_op jit(solution)/shard_map/ppermute | solution.py:106
  63.8 43.5 %collective-permute-start.10 = (bf16[64,2048]{1,0:T(8,128)(2,1)}, bf16[64,2048]{1,0:T(8,128)(2,1)}, u32[]{:S(2)}, u32[]{:S(2)}) collective-permute-start(bf16[64,2048]{1,0:T(8,128)(2,1)} %param.18), channel_id=1, source_target_pairs={{0,0},{4,1},{8,2},{12,3},{16,4},{20,5},{24,6},{28,7},{1,8},{5,9},{... | collective-permute-start | bytes 786440 | tf_op jit(solution)/shard_map/ppermute | solution.py:422
  70.1 16.7 %collective-permute-start.9 = (bf16[1024,768]{1,0:T(8,128)(2,1)}, bf16[1024,768]{1,0:T(8,128)(2,1)}, u32[]{:S(2)}, u32[]{:S(2)}) collective-permute-start(bf16[1024,768]{1,0:T(8,128)(2,1)} %pad_maximum_fusion.5), channel_id=1, source_target_pairs={{0,8},{8,0},{16,24},{24,16},{1,9},{9,1},{17,25},{25,17},{2,10},{10... | collective-permute-start | bytes 4718600 | tf_op jit(solution)/shard_map/ppermute | solution.py:48
  71.7 80.0 %all-to-all-start.1 = ((bf16[8,64,3072]{2,1,0:T(8,128)(2,1)}), bf16[8,64,3072]{2,1,0:T(8,128)(2,1)S(1)}, u32[]{:S(2)}, u32[]{:S(2)}) async-start(bf16[8,64,3072]{2,1,0:T(8,128)(2,1)} %pad_maximum_fusion.2), calls=%async_computation.1 | async-start | bytes 6291456 | tf_op jit(solution)/shard_map/all_to_all | solution.py:393
  153.2 15.7 %collective-permute-start.16 = (bf16[128,2048]{1,0:T(8,128)(2,1)S(1)}, bf16[128,2048]{1,0:T(8,128)(2,1)S(1)}, u32[]{:S(2)}, u32[]{:S(2)}) collective-permute-start(bf16[128,2048]{1,0:T(8,128)(2,1)S(1)} %pad_maximum_fusion.14), channel_id=1, source_target_pairs={{0,1},{2,0},{4,2},{6,4},{7,6},{5,7},{3,5},{1,3},{8,9},{10,8},{12,1... | collective-permute-start | bytes 1572872 | tf_op jit(solution)/shard_map/ppermute | solution.py:106
  154.3 16.4 %collective-permute-start.15 = (bf16[128,2048]{1,0:T(8,128)(2,1)S(1)}, bf16[128,2048]{1,0:T(8,128)(2,1)S(1)}, u32[]{:S(2)}, u32[]{:S(2)}) collective-permute-start(bf16[128,2048]{1,0:T(8,128)(2,1)S(1)} %copy-done.61), channel_id=1, source_target_pairs={{0,2},{2,4},{4,6},{6,7},{7,5},{5,3},{3,1},{1,0},{8,10},{10,12},{12... | collective-permute-start | bytes 1572872 | tf_op jit(solution)/shard_map/ppermute | solution.py:106
  172.5 12.1 %collective-permute-start.19 = (bf16[128,2048]{1,0:T(8,128)(2,1)S(1)}, bf16[128,2048]{1,0:T(8,128)(2,1)S(1)}, u32[]{:S(2)}, u32[]{:S(2)}) collective-permute-start(bf16[128,2048]{1,0:T(8,128)(2,1)S(1)} %get-tuple-element.110), channel_id=1, source_target_pairs={{0,1},{2,0},{4,2},{6,4},{7,6},{5,7},{3,5},{1,3},{8,9},{10,8},{12,1... | collective-permute-start | bytes 1572872 | tf_op jit(solution)/shard_map/ppermute | solution.py:106
  174.6 13.9 %collective-permute-start.20 = (bf16[512,512]{1,0:T(8,128)(2,1)S(1)}, bf16[512,512]{1,0:T(8,128)(2,1)S(1)}, u32[]{:S(2)}, u32[]{:S(2)}) collective-permute-start(bf16[512,512]{1,0:T(8,128)(2,1)S(1)} %get-tuple-element.111), channel_id=1, source_target_pairs={{0,16},{8,24},{16,0},{24,8},{1,17},{9,25},{17,1},{25,9},{2,18},{10... | collective-permute-start | bytes 1572872 | tf_op jit(solution)/shard_map/ppermute | solution.py:48
  190.7 13.5 %collective-permute-start.23 = (bf16[512,512]{1,0:T(8,128)(2,1)S(1)}, bf16[512,512]{1,0:T(8,128)(2,1)S(1)}, u32[]{:S(2)}, u32[]{:S(2)}) collective-permute-start(bf16[512,512]{1,0:T(8,128)(2,1)S(1)} %copy-done.21), channel_id=1, source_target_pairs={{0,16},{8,24},{16,0},{24,8},{1,17},{9,25},{17,1},{25,9},{2,18},{10... | collective-permute-start | bytes 1572872 | tf_op jit(solution)/shard_map/ppermute | solution.py:48
  238.4 35.2 %collective-permute-start.35 = (bf16[1024,2048]{1,0:T(8,128)(2,1)S(1)}, bf16[1024,2048]{1,0:T(8,128)(2,1)S(1)}, u32[]{:S(2)}, u32[]{:S(2)}) collective-permute-start(bf16[1024,2048]{1,0:T(8,128)(2,1)S(1)} %pad_maximum_fusion), channel_id=1, source_target_pairs={{0,8},{8,0},{16,24},{24,16},{1,9},{9,1},{17,25},{25,17},{2,10},{10... | collective-permute-start | bytes 12582920 | tf_op jit(solution)/shard_map/ppermute | solution.py:48
  248.7 12.5 %collective-permute-start.38 = (bf16[128,2048]{1,0:T(8,128)(2,1)S(1)}, bf16[128,2048]{1,0:T(8,128)(2,1)S(1)}, u32[]{:S(2)}, u32[]{:S(2)}) collective-permute-start(bf16[128,2048]{1,0:T(8,128)(2,1)S(1)} %fusion.39), channel_id=1, source_target_pairs={{0,1},{2,0},{4,2},{6,4},{7,6},{5,7},{3,5},{1,3},{8,9},{10,8},{12,1... | collective-permute-start | bytes 1572872 | tf_op jit(solution)/shard_map/ppermute | solution.py:106
  264.2 26.4 %collective-permute-start.36 = (bf16[1024,1024]{1,0:T(8,128)(2,1)S(1)}, bf16[1024,1024]{1,0:T(8,128)(2,1)}, u32[]{:S(2)}, u32[]{:S(2)}) collective-permute-start(bf16[1024,1024]{1,0:T(8,128)(2,1)S(1)} %pad_maximum_fusion.3), channel_id=1, source_target_pairs={{0,8},{8,0},{16,24},{24,16},{1,9},{9,1},{17,25},{25,17},{2,10},{10... | collective-permute-start | bytes 6291464 | tf_op jit(solution)/shard_map/ppermute | solution.py:48
  264.3 20.2 %collective-permute-start.39 = (bf16[128,2048]{1,0:T(8,128)(2,1)S(1)}, bf16[128,2048]{1,0:T(8,128)(2,1)S(1)}, u32[]{:S(2)}, u32[]{:S(2)}) collective-permute-start(bf16[128,2048]{1,0:T(8,128)(2,1)S(1)} %collective-permute-done.37), channel_id=1, source_target_pairs={{0,2},{2,4},{4,6},{6,7},{7,5},{5,3},{3,1},{1,0},{8,10},{10,12},{12... | collective-permute-start | bytes 1572872 | tf_op jit(solution)/shard_map/ppermute | solution.py:106
  284.5 13.4 %collective-permute-start.42 = (bf16[128,2048]{1,0:T(8,128)(2,1)S(1)}, bf16[128,2048]{1,0:T(8,128)(2,1)S(1)}, u32[]{:S(2)}, u32[]{:S(2)}) collective-permute-start(bf16[128,2048]{1,0:T(8,128)(2,1)S(1)} %collective-permute-done.40), channel_id=1, source_target_pairs={{0,1},{2,0},{4,2},{6,4},{7,6},{5,7},{3,5},{1,3},{8,9},{10,8},{12,1... | collective-permute-start | bytes 1572872 | tf_op jit(solution)/shard_map/ppermute | solution.py:106
  285.7 12.2 %collective-permute-start.41 = (bf16[128,2048]{1,0:T(8,128)(2,1)S(1)}, bf16[128,2048]{1,0:T(8,128)(2,1)S(1)}, u32[]{:S(2)}, u32[]{:S(2)}) collective-permute-start(bf16[128,2048]{1,0:T(8,128)(2,1)S(1)} %collective-permute-done.39), channel_id=1, source_target_pairs={{0,2},{2,4},{4,6},{6,7},{7,5},{5,3},{3,1},{1,0},{8,10},{10,12},{12... | collective-permute-start | bytes 1572872 | tf_op jit(solution)/shard_map/ppermute | solution.py:106
  306.9 13.3 %collective-permute-start.46 = (bf16[128,1024]{1,0:T(8,128)(2,1)S(1)}, bf16[128,1024]{1,0:T(8,128)(2,1)S(1)}, u32[]{:S(2)}, u32[]{:S(2)}) collective-permute-start(bf16[128,1024]{1,0:T(8,128)(2,1)S(1)} %get-tuple-element.135), channel_id=1, source_target_pairs={{0,1},{2,0},{4,2},{6,4},{7,6},{5,7},{3,5},{1,3},{8,9},{10,8},{12,1... | collective-permute-start | bytes 786440 | tf_op jit(solution)/shard_map/ppermute | solution.py:106
  320.7 14.5 %collective-permute-start.47 = (bf16[128,2048]{1,0:T(8,128)(2,1)S(1)}, bf16[128,2048]{1,0:T(8,128)(2,1)S(1)}, u32[]{:S(2)}, u32[]{:S(2)}) collective-permute-start(bf16[128,2048]{1,0:T(8,128)(2,1)S(1)} %pad_maximum_fusion.16), channel_id=1, source_target_pairs={{0,2},{2,4},{4,6},{6,7},{7,5},{5,3},{3,1},{1,0},{8,10},{10,12},{12... | collective-permute-start | bytes 1572872 | tf_op jit(solution)/shard_map/ppermute | solution.py:106
  321.9 14.3 %collective-permute-start.48 = (bf16[128,2048]{1,0:T(8,128)(2,1)S(1)}, bf16[128,2048]{1,0:T(8,128)(2,1)S(1)}, u32[]{:S(2)}, u32[]{:S(2)}) collective-permute-start(bf16[128,2048]{1,0:T(8,128)(2,1)S(1)} %pad_maximum_fusion.17), channel_id=1, source_target_pairs={{0,1},{2,0},{4,2},{6,4},{7,6},{5,7},{3,5},{1,3},{8,9},{10,8},{12,1... | collective-permute-start | bytes 1572872 | tf_op jit(solution)/shard_map/ppermute | solution.py:106
  336.3 14.2 %collective-permute-start.49 = (bf16[128,2048]{1,0:T(8,128)(2,1)S(1)}, bf16[128,2048]{1,0:T(8,128)(2,1)S(1)}, u32[]{:S(2)}, u32[]{:S(2)}) collective-permute-start(bf16[128,2048]{1,0:T(8,128)(2,1)S(1)} %fusion.26), channel_id=1, source_target_pairs={{0,2},{2,4},{4,6},{6,7},{7,5},{5,3},{3,1},{1,0},{8,10},{10,12},{12... | collective-permute-start | bytes 1572872 | tf_op jit(solution)/shard_map/ppermute | solution.py:106
  336.6 14.2 %collective-permute-start.50 = (bf16[128,2048]{1,0:T(8,128)(2,1)S(1)}, bf16[128,2048]{1,0:T(8,128)(2,1)S(1)}, u32[]{:S(2)}, u32[]{:S(2)}) collective-permute-start(bf16[128,2048]{1,0:T(8,128)(2,1)S(1)} %fusion.27), channel_id=1, source_target_pairs={{0,1},{2,0},{4,2},{6,4},{7,6},{5,7},{3,5},{1,3},{8,9},{10,8},{12,1... | collective-permute-start | bytes 1572872 | tf_op jit(solution)/shard_map/ppermute | solution.py:106
  364.4 25.2 %collective-permute-start.59 = (bf16[1024,1024]{1,0:T(8,128)(2,1)S(1)}, bf16[1024,1024]{1,0:T(8,128)(2,1)S(1)}, u32[]{:S(2)}, u32[]{:S(2)}) collective-permute-start(bf16[1024,1024]{1,0:T(8,128)(2,1)S(1)} %convolution_convert_fusion.1), channel_id=1, source_target_pairs={{0,8},{8,0},{16,24},{24,16},{1,9},{9,1},{17,25},{25,17},{2,10},{10... | collective-permute-start | bytes 6291464 | tf_op jit(solution)/shard_map/ppermute | solution.py:48
  373.6 13.5 %collective-permute-start.55 = (bf16[128,2048]{1,0:T(8,128)(2,1)S(1)}, bf16[128,2048]{1,0:T(8,128)(2,1)S(1)}, u32[]{:S(2)}, u32[]{:S(2)}) collective-permute-start(bf16[128,2048]{1,0:T(8,128)(2,1)S(1)} %pad_maximum_fusion.19), channel_id=1, source_target_pairs={{0,2},{2,4},{4,6},{6,7},{7,5},{5,3},{3,1},{1,0},{8,10},{10,12},{12... | collective-permute-start | bytes 1572872 | tf_op jit(solution)/shard_map/ppermute | solution.py:106
  374.0 13.2 %collective-permute-start.56 = (bf16[128,2048]{1,0:T(8,128)(2,1)S(1)}, bf16[128,2048]{1,0:T(8,128)(2,1)S(1)}, u32[]{:S(2)}, u32[]{:S(2)}) collective-permute-start(bf16[128,2048]{1,0:T(8,128)(2,1)S(1)} %pad_maximum_fusion.20), channel_id=1, source_target_pairs={{0,1},{2,0},{4,2},{6,4},{7,6},{5,7},{3,5},{1,3},{8,9},{10,8},{12,1... | collective-permute-start | bytes 1572872 | tf_op jit(solution)/shard_map/ppermute | solution.py:106
  383.4 31.2 %collective-permute-start.62 = (bf16[1024,2048]{1,0:T(8,128)(2,1)}, bf16[1024,2048]{1,0:T(8,128)(2,1)}, u32[]{:S(2)}, u32[]{:S(2)}) collective-permute-start(bf16[1024,2048]{1,0:T(8,128)(2,1)} %convolution_convert_fusion), channel_id=1, source_target_pairs={{0,8},{8,0},{16,24},{24,16},{1,9},{9,1},{17,25},{25,17},{2,10},{10... | collective-permute-start | bytes 12582920 | tf_op jit(solution)/shard_map/ppermute | solution.py:48
  387.4 12.6 %collective-permute-start.57 = (bf16[128,2048]{1,0:T(8,128)(2,1)S(1)}, bf16[128,2048]{1,0:T(8,128)(2,1)S(1)}, u32[]{:S(2)}, u32[]{:S(2)}) collective-permute-start(bf16[128,2048]{1,0:T(8,128)(2,1)S(1)} %fusion.31), channel_id=1, source_target_pairs={{0,2},{2,4},{4,6},{6,7},{7,5},{5,3},{3,1},{1,0},{8,10},{10,12},{12... | collective-permute-start | bytes 1572872 | tf_op jit(solution)/shard_map/ppermute | solution.py:106
  388.9 12.2 %collective-permute-start.58 = (bf16[128,2048]{1,0:T(8,128)(2,1)S(1)}, bf16[128,2048]{1,0:T(8,128)(2,1)S(1)}, u32[]{:S(2)}, u32[]{:S(2)}) collective-permute-start(bf16[128,2048]{1,0:T(8,128)(2,1)S(1)} %fusion.32), channel_id=1, source_target_pairs={{0,1},{2,0},{4,2},{6,4},{7,6},{5,7},{3,5},{1,3},{8,9},{10,8},{12,1... | collective-permute-start | bytes 1572872 | tf_op jit(solution)/shard_map/ppermute | solution.py:106
  403.4 34.1 %collective-permute-start.71 = (bf16[512,1024]{1,0:T(8,128)(2,1)S(1)}, bf16[512,1024]{1,0:T(8,128)(2,1)S(1)}, u32[]{:S(2)}, u32[]{:S(2)}) collective-permute-start(bf16[512,1024]{1,0:T(8,128)(2,1)S(1)} %slice.1536), channel_id=1, source_target_pairs={{0,16},{8,24},{16,0},{24,8},{1,17},{9,25},{17,1},{25,9},{2,18},{10... | collective-permute-start | bytes 3145736 | tf_op jit(solution)/shard_map/ppermute | solution.py:48
  423.1 12.1 %collective-permute-start.63 = (bf16[128,2048]{1,0:T(8,128)(2,1)S(1)}, bf16[128,2048]{1,0:T(8,128)(2,1)S(1)}, u32[]{:S(2)}, u32[]{:S(2)}) collective-permute-start(bf16[128,2048]{1,0:T(8,128)(2,1)S(1)} %get-tuple-element.154), channel_id=1, source_target_pairs={{0,1},{2,0},{4,2},{6,4},{7,6},{5,7},{3,5},{1,3},{8,9},{10,8},{12,1... | collective-permute-start | bytes 1572872 | tf_op jit(solution)/shard_map/ppermute | solution.py:106
  447.9 14.3 %collective-permute-start.67 = (bf16[128,2048]{1,0:T(8,128)(2,1)S(1)}, bf16[128,2048]{1,0:T(8,128)(2,1)S(1)}, u32[]{:S(2)}, u32[]{:S(2)}) collective-permute-start(bf16[128,2048]{1,0:T(8,128)(2,1)S(1)} %collective-permute-done.65), channel_id=1, source_target_pairs={{0,1},{2,0},{4,2},{6,4},{7,6},{5,7},{3,5},{1,3},{8,9},{10,8},{12,1... | collective-permute-start | bytes 1572872 | tf_op jit(solution)/shard_map/ppermute | solution.py:106
  452.4 39.1 %collective-permute-start.72 = (bf16[512,2048]{1,0:T(8,128)(2,1)}, bf16[512,2048]{1,0:T(8,128)(2,1)}, u32[]{:S(2)}, u32[]{:S(2)}) collective-permute-start(bf16[512,2048]{1,0:T(8,128)(2,1)} %slice.1535), channel_id=1, source_target_pairs={{0,16},{8,24},{16,0},{24,8},{1,17},{9,25},{17,1},{25,9},{2,18},{10... | collective-permute-start | bytes 6291464 | tf_op jit(solution)/shard_map/ppermute | solution.py:48
  464.7 30.6 %all-to-all-start.2 = ((bf16[8,64,1024]{2,1,0:T(8,128)(2,1)}), bf16[8,64,1024]{2,1,0:T(8,128)(2,1)}, u32[]{:S(2)}, u32[]{:S(2)}) async-start(bf16[8,64,1024]{2,1,0:T(8,128)(2,1)} %bitcast.57), calls=%async_computation.2 | async-start | bytes 2097152 | tf_op jit(solution)/shard_map/all_to_all | solution.py:393
  482.1 17.9 %collective-permute-start.83 = (bf16[128,2048]{1,0:T(8,128)(2,1)}, bf16[128,2048]{1,0:T(8,128)(2,1)}, u32[]{:S(2)}, u32[]{:S(2)}) collective-permute-start(bf16[128,2048]{1,0:T(8,128)(2,1)} %pad_maximum_fusion.24), channel_id=1, source_target_pairs={{0,8},{8,0},{16,24},{24,16},{1,9},{9,1},{17,25},{25,17},{2,10},{10... | collective-permute-start | bytes 1572872 | tf_op jit(solution)/shard_map/ppermute | solution.py:48
  495.3 49.4 %all-to-all-start.3 = ((bf16[8,64,2048]{2,1,0:T(8,128)(2,1)}), bf16[8,64,2048]{2,1,0:T(8,128)(2,1)}, u32[]{:S(2)}, u32[]{:S(2)}) async-start(bf16[8,64,2048]{2,1,0:T(8,128)(2,1)} %bitcast.421), calls=%async_computation.3 | async-start | bytes 4194304 | tf_op jit(solution)/shard_map/all_to_all | solution.py:393
  548.2 17.3 %collective-permute-start.75 = (bf16[1024,768]{1,0:T(8,128)(2,1)S(1)}, bf16[1024,768]{1,0:T(8,128)(2,1)S(1)}, u32[]{:S(2)}, u32[]{:S(2)}) collective-permute-start(bf16[1024,768]{1,0:T(8,128)(2,1)S(1)} %convolution_convert_fusion.2), channel_id=1, source_target_pairs={{0,8},{8,0},{16,24},{24,16},{1,9},{9,1},{17,25},{25,17},{2,10},{10... | collective-permute-start | bytes 4718600 | tf_op jit(solution)/shard_map/ppermute | solution.py:48
  569.0 13.2 %collective-permute-start.76 = (bf16[128,2048]{1,0:T(8,128)(2,1)S(1)}, bf16[128,2048]{1,0:T(8,128)(2,1)S(1)}, u32[]{:S(2)}, u32[]{:S(2)}) collective-permute-start(bf16[128,2048]{1,0:T(8,128)(2,1)S(1)} %pad_maximum_fusion.21), channel_id=1, source_target_pairs={{0,2},{2,4},{4,6},{6,7},{7,5},{5,3},{3,1},{1,0},{8,10},{10,12},{12... | collective-permute-start | bytes 1572872 | tf_op jit(solution)/shard_map/ppermute | solution.py:106
  571.8 12.9 %collective-permute-start.77 = (bf16[128,2048]{1,0:T(8,128)(2,1)S(1)}, bf16[128,2048]{1,0:T(8,128)(2,1)S(1)}, u32[]{:S(2)}, u32[]{:S(2)}) collective-permute-start(bf16[128,2048]{1,0:T(8,128)(2,1)S(1)} %pad_maximum_fusion.22), channel_id=1, source_target_pairs={{0,1},{2,0},{4,2},{6,4},{7,6},{5,7},{3,5},{1,3},{8,9},{10,8},{12,1... | collective-permute-start | bytes 1572872 | tf_op jit(solution)/shard_map/ppermute | solution.py:106
  574.2 18.3 %collective-permute-start.80 = (bf16[512,768]{1,0:T(8,128)(2,1)S(1)}, bf16[512,768]{1,0:T(8,128)(2,1)S(1)}, u32[]{:S(2)}, u32[]{:S(2)}) collective-permute-start(bf16[512,768]{1,0:T(8,128)(2,1)S(1)} %slice.1537), channel_id=1, source_target_pairs={{0,16},{8,24},{16,0},{24,8},{1,17},{9,25},{17,1},{25,9},{2,18},{10... | collective-permute-start | bytes 2359304 | tf_op jit(solution)/shard_map/ppermute | solution.py:48
  586.4 12.0 %collective-permute-start.79 = (bf16[128,2048]{1,0:T(8,128)(2,1)S(1)}, bf16[128,2048]{1,0:T(8,128)(2,1)S(1)}, u32[]{:S(2)}, u32[]{:S(2)}) collective-permute-start(bf16[128,2048]{1,0:T(8,128)(2,1)S(1)} %fusion.37), channel_id=1, source_target_pairs={{0,1},{2,0},{4,2},{6,4},{7,6},{5,7},{3,5},{1,3},{8,9},{10,8},{12,1... | collective-permute-start | bytes 1572872 | tf_op jit(solution)/shard_map/ppermute | solution.py:106
  599.3 28.8 %collective-permute-start.82 = (bf16[128,2048]{1,0:T(8,128)(2,1)}, bf16[128,2048]{1,0:T(8,128)(2,1)S(1)}, u32[]{:S(2)}, u32[]{:S(2)}) collective-permute-start(bf16[128,2048]{1,0:T(8,128)(2,1)} %fusion.38), channel_id=1, source_target_pairs={{0,1},{2,0},{4,2},{6,4},{7,6},{5,7},{3,5},{1,3},{8,9},{10,8},{12,1... | collective-permute-start | bytes 1572872 | tf_op jit(solution)/shard_map/ppermute | solution.py:106
  600.5 27.7 %collective-permute-start.81 = (bf16[128,2048]{1,0:T(8,128)(2,1)}, bf16[128,2048]{1,0:T(8,128)(2,1)}, u32[]{:S(2)}, u32[]{:S(2)}) collective-permute-start(bf16[128,2048]{1,0:T(8,128)(2,1)} %fusion.35), channel_id=1, source_target_pairs={{0,2},{2,4},{4,6},{6,7},{7,5},{5,3},{3,1},{1,0},{8,10},{10,12},{12... | collective-permute-start | bytes 1572872 | tf_op jit(solution)/shard_map/ppermute | solution.py:106
  607.4 32.9 %all-to-all-start.4 = ((bf16[8,64,768]{2,1,0:T(8,128)(2,1)}), bf16[8,64,768]{2,1,0:T(8,128)(2,1)}, u32[]{:S(2)}, u32[]{:S(2)}) async-start(bf16[8,64,768]{2,1,0:T(8,128)(2,1)} %bitcast.424), calls=%async_computation.4 | async-start | bytes 1572864 | tf_op jit(solution)/shard_map/all_to_all | solution.py:393
  (138 other events, 1744.7 us)
